TPU v7x, 128 devices: a whole 4x4x4 slice. The times are simulated.
128 devices in a mesh: dp: 128 (over z, y, x, core).
Axes of the slice: x: 4, y: 4, z: 4, core: 2. Of those that a mesh axis runs over, the one named last changes fastest.
Arguments:
- features: bfloat16 [8192, 256], P('dp')
- w_in: bfloat16 [256, 1024], replicated
- w_out: bfloat16 [1024, 128], replicated
- item_table: bfloat16 [1048576, 128], P('dp')
- cand_ids: int32 [131072], replicated
- log_q: float32 [131072], replicated
- targets: int32 [8192], P('dp')
Outputs:
- output 1: float32 [], replicated
- output 2: float32 [1048576, 128], P('dp')
- output 3: float32 [256, 1024], replicated
- output 4: float32 [1024, 128], replicated
All inputs are finite; a program needn't handle non-finite values.
Results may differ from a plain program's by a relative error of at most 0.001.
Values are sent between devices in bfloat16 or wider.
A program may use at most 1 GiB of HBM per device.

v0:
```python
import jax
import jax.numpy as jnp
from jax import lax
from jax.sharding import PartitionSpec as P


def solution(mesh):
    num_dev = mesh.shape["dp"]

    def local_step(features, w_in, w_out, table_blk, cand_ids, log_q, targets):
        dev_index = lax.axis_index("dp")
        block_rows = table_blk.shape[0]
        cand_dev = cand_ids.shape[0] // num_dev
        tok_total = features.shape[0] * num_dev
        pre_act = jnp.dot(features, w_in, preferred_element_type=jnp.float32)
        act_val, gelu_back = jax.vjp(jax.nn.gelu, pre_act)
        act_b = act_val.astype(jnp.bfloat16)
        query = jnp.dot(act_b, w_out, preferred_element_type=jnp.float32).astype(jnp.bfloat16)
        query_all = lax.all_gather(query, "dp", axis=0, tiled=True)
        tgt_all = lax.all_gather(targets, "dp", axis=0, tiled=True)
        row_base = dev_index * block_rows
        tgt_local = tgt_all - row_base
        tgt_own = (tgt_local >= 0) & (tgt_local < block_rows)
        tgt_index = jnp.clip(tgt_local, 0, block_rows - 1)
        tgt_rows = table_blk[tgt_index]
        own_cands = lax.dynamic_slice_in_dim(cand_ids, dev_index * cand_dev, cand_dev)
        own_logq = lax.dynamic_slice_in_dim(log_q, dev_index * cand_dev, cand_dev)
        cand_index = own_cands - row_base
        cand_rows = table_blk[cand_index]
        tgt_dot = jnp.einsum("td,td->t", query_all, tgt_rows, preferred_element_type=jnp.float32)
        tgt_logit = lax.psum(jnp.where(tgt_own, tgt_dot, 0.0), "dp")
        cand_logit = jnp.einsum("td,cd->tc", query_all, cand_rows, preferred_element_type=jnp.float32) - own_logq[None, :]
        cand_logit = jnp.where(own_cands[None, :] == tgt_all[:, None], -1e9, cand_logit)
        top_val = jnp.maximum(lax.pmax(jnp.max(cand_logit, axis=1), "dp"), tgt_logit)
        exp_sum = lax.psum(jnp.sum(jnp.exp(cand_logit - top_val[:, None]), axis=1), "dp")
        log_norm = top_val + jnp.log(exp_sum + jnp.exp(tgt_logit - top_val))
        loss = jnp.sum(log_norm - tgt_logit) / tok_total
        grad_tgt = (jnp.exp(tgt_logit - log_norm) - 1.0) / tok_total
        cand_grad = (jnp.exp(cand_logit - log_norm[:, None]) / tok_total).astype(jnp.bfloat16)
        own_grad = jnp.where(tgt_own, grad_tgt, 0.0)
        dq_part = own_grad[:, None] * tgt_rows + jnp.einsum("tc,cd->td", cand_grad, cand_rows, preferred_element_type=jnp.float32)
        dq_local = lax.psum_scatter(dq_part, "dp", scatter_dimension=0, tiled=True).astype(jnp.bfloat16)
        grad_cand = jnp.einsum("tc,td->cd", cand_grad, query_all, preferred_element_type=jnp.float32)
        grad_blk = jnp.zeros(table_blk.shape, jnp.float32).at[cand_index].add(grad_cand).at[tgt_index].add(own_grad[:, None] * query_all)
        d_act = jnp.einsum("td,fd->tf", dq_local, w_out, preferred_element_type=jnp.float32)
        d_pre = gelu_back(d_act)[0].astype(jnp.bfloat16)
        grad_w_out = lax.psum(jnp.einsum("tf,td->fd", act_b, dq_local, preferred_element_type=jnp.float32), "dp")
        grad_w_in = lax.psum(jnp.einsum("ti,tf->if", features, d_pre, preferred_element_type=jnp.float32), "dp")
        return loss, grad_blk, grad_w_in, grad_w_out

    return jax.shard_map(local_step, mesh=mesh, in_specs=(P("dp", None), P(), P(), P("dp", None), P(), P(), P("dp")), out_specs=(P(), P("dp", None), P(), P()), check_vma=False)
```

profile of v0, /device:TPU:1, one launch (start us, length us, event | category | flops | bytes accessed | tf_op | source)
XLA Modules:
  0.0 1172.8 jit_solution(10457845507534464162)
XLA Ops:
  7.2 0.0 copy-start
  7.2 0.0 all-gather.2.cloned.1.call-start
  7.2 1.4 fusion.34
  8.6 1.8 convolution_convert_fusion
  10.4 0.0 all-gather.2.cloned.1.call-update
  10.4 0.0 reduce-scatter.2.cloned.1.call-start
  10.5 0.7 dynamic_slice.7
  11.2 0.7 broadcast_clamp_fusion.1
  11.9 0.0 copy-done
  11.9 3.2 gather_fusion
  15.1 0.9 dynamic-update-slice
  16.0 69.1 %all-reduce = s32[8192]{0:T(1024)S(1)} all-reduce(s32[8192]{0:T(1024)S(1)} %dynamic-update-slice), channel_id=1, replica_groups=mesh['dp'=128] {'dp'}, use_global_device_ids=true, to_apply=%add | all-reduce | flops 8192 | bytes 65536
  85.1 29.7 %gather_fusion.1 = bf16[8192,128]{1,0:T(8,128)(2,1)} fusion(bf16[8192,128]{1,0:T(8,128)(2,1)S(1)} %copy-done, s32[8192]{0:T(1024)S(1)} %get-tuple-element.18), kind=kCustom, calls=%fused_computation.1 | custom fusion | bytes 4227072 | tf_op jit(solution)/shard_map/gather | solution.py:25
  114.8 0.0 all-gather.2.cloned.1.call-done
  114.8 0.0 copy-start.4
  114.8 3.5 fusion.1
  118.3 62.6 %psum.28 = f32[8192]{0:T(1024)S(1)} all-reduce(f32[8192]{0:T(1024)S(1)} %get-tuple-element.16), channel_id=1, replica_groups=mesh['dp'=128] {'dp'}, use_global_device_ids=true, to_apply=%region_2.3 | all-reduce | flops 8192 | bytes 65536 | tf_op jit(solution)/shard_map/psum | solution.py:31
  180.9 0.0 copy-done.4
  180.9 12.5 %fusion = (f32[8192]{0:T(1024)S(1)}, f32[8192,1024]{0,1:T(8,128)}) fusion(f32[1024]{0:T(1024)S(1)} %dynamic_slice.7, s32[8192]{0:T(1024)S(1)} %all-reduce, s32[1024]{0:T(1024)S(1)} %get-tuple-element.22, bf16[8192,128]{1,0:T(8,128)(2,1)S(1)} %copy-done.4, bf16[1024,128]{1,0:T(8,128)(2,1)S(1)} %gather_fusion), kind=kOutput, calls=%fused_computation.7 | convolution fusion | flops 2181029888 | bytes 35987456 | tf_op jit(solution)/shard_map/td,cd->tc/dot_general | solution.py:32
  193.4 64.0 %pmax.7 = f32[8192]{0:T(1024)S(1)} all-reduce(f32[8192]{0:T(1024)S(1)} %get-tuple-element.23), channel_id=1, replica_groups=mesh['dp'=128] {'dp'}, use_global_device_ids=true, to_apply=%region_1.2 | all-reduce | flops 8192 | bytes 65536 | tf_op jit(solution)/shard_map/pmax | solution.py:34
  257.5 15.0 %exponential_reduce_fusion = f32[8192]{0:T(1024)S(1)} fusion(f32[8192,1024]{0,1:T(8,128)} %get-tuple-element.24, f32[8192]{0:T(1024)S(1)} %max.9, f32[1024]{0:T(1024)S(1)} %dynamic_slice.7, s32[8192]{0:T(1024)S(1)} %all-reduce, s32[1024]{0:T(1024)S(1)} %get-tuple-element.22), kind=kLoop, calls=%fused_computation.5 | loop fusion | flops 41934848 | bytes 33660928 | tf_op jit(solution)/shard_map/reduce_sum | solution.py:35
  272.4 62.8 %psum.29 = f32[8192]{0:T(1024)S(1)} all-reduce(f32[8192]{0:T(1024)S(1)} %exponential_reduce_fusion), channel_id=1, replica_groups=mesh['dp'=128] {'dp'}, use_global_device_ids=true, to_apply=%region_4.5 | all-reduce | flops 8192 | bytes 65536 | tf_op jit(solution)/shard_map/psum | solution.py:35
  335.2 0.0 copy-start.3
  335.2 15.4 %multiply_convert_fusion = bf16[8192,1024]{0,1:T(8,128)(2,1)S(1)} fusion(f32[8192,1024]{0,1:T(8,128)} %get-tuple-element.24, f32[8192]{0:T(1024)S(1)} %get-tuple-element.15, f32[1024]{0:T(1024)S(1)} %dynamic_slice.7, s32[8192]{0:T(1024)S(1)} %all-reduce, s32[1024]{0:T(1024)S(1)} %get-tuple-element.22), kind=kLoop, calls=%fused_computation.4 | loop fusion | flops 50331648 | bytes 50405376 | tf_op jit(solution)/shard_map/convert_element_type | solution.py:39
  350.7 0.0 copy-start.2
  350.7 5.7 copy-done.2
  356.4 0.0 copy-done.3
  356.4 7.3 convolution_add_fusion
  363.7 0.0 copy-start.7
  363.7 0.0 copy-start.5
  363.7 0.0 reduce-scatter.2.cloned.1.call-update
  363.7 0.0 all-reduce.4.cloned.1.call-start
  363.8 0.6 subtract_reduce_fusion
  365.1 639.4 %reduce-scatter.2.cloned.1.call-done = f32[64,128]{1,0:T(8,128)} async-done(((f32[8192,128]{1,0:T(8,128)}), f32[64,128]{1,0:T(8,128)}) %reduce-scatter.2.cloned.1.call-update) | async-done | bytes 32784 | tf_op jit(solution)/shard_map/reduce_scatter | solution.py:42
  1004.5 1.8 fusion.20
  1006.3 0.0 copy-done.6
  1006.3 0.0 copy-done.7
  1006.3 2.3 convolution_bitcast_fusion
  1008.6 0.0 all-reduce.4.cloned.1.call-update
  1008.6 0.0 copy-done.5
  1008.6 8.1 fusion.35
  1016.7 8.3 scatter_custom_fusion
  1025.0 0.0 copy-start.1
  1025.0 64.2 %scatter_custom_fusion.1 = f32[8192,128]{1,0:T(8,128)} fusion(f32[8192,128]{1,0:T(8,128)} %scatter_custom_fusion, s32[8192]{0:T(1024)S(1)} %get-tuple-element.19, bf16[8192,128]{1,0:T(8,128)(2,1)} %all-gather.2.cloned.1.call-done, f32[8192]{0:T(1024)S(1)} %get-tuple-element.14), kind=kCustom, calls=%fused_computation.13 | custom fusion | flops 3145728 | bytes 6324224 | tf_op jit(solution)/shard_map/scatter-add | solution.py:44
  1089.2 71.6 %all-reduce.4.cloned.1.call-done = (f32[256,1024]{0,1:T(8,128)}, f32[1024,128]{1,0:T(8,128)}) async-done(((f32[256,1024]{0,1:T(8,128)}, f32[1024,128]{1,0:T(8,128)}), (f32[256,1024]{0,1:T(8,128)}, f32[1024,128]{1,0:T(8,128)})) %all-reduce.4.cloned.1.call-update) | async-done | bytes 1572880 | tf_op jit(solution)/shard_map/psum | solution.py:48
  1160.8 2.5 copy.12
  1163.3 1.9 copy.22
  1165.2 0.0 copy-done.1
  (6 shorter events, 0.1 us)
Async XLA Ops:
  7.2 4.7 copy-start
  7.2 107.6 %all-gather.2.cloned.1.call-start = ((), (), s32[]{:S(2)}) async-start(), calls=%async_computation.1 | async-start | bytes 2113536 | tf_op jit(solution)/shard_map/all_gather | solution.py:19
  10.4 994.0 %reduce-scatter.2.cloned.1.call-start = ((), (), s32[]{:S(2)}) async-start(), calls=%async_computation.2 | async-start | bytes 4227072 | tf_op jit(solution)/shard_map/reduce_scatter | solution.py:42
  114.8 66.1 %copy-start.4 = (bf16[8192,128]{1,0:T(8,128)(2,1)S(1)}, bf16[8192,128]{1,0:T(8,128)(2,1)}, u32[]{:S(2)}) copy-start(bf16[8192,128]{1,0:T(8,128)(2,1)} %all-gather.2.cloned.1.call-done) | copy-start | bytes 6291460
  335.2 21.2 %copy-start.3 = (bf16[8192,128]{1,0:T(8,128)(2,1)S(1)}, bf16[8192,128]{1,0:T(8,128)(2,1)}, u32[]{:S(2)}) copy-start(bf16[8192,128]{1,0:T(8,128)(2,1)} %gather_fusion.1) | copy-start | bytes 6291460
  350.7 5.7 copy-start.2
  363.7 642.6 %copy-start.6 = (bf16[64,256]{1,0:T(8,128)(2,1)S(1)}, bf16[64,256]{1,0:T(8,128)(2,1)}, u32[]{:S(2)}) copy-start(bf16[64,256]{1,0:T(8,128)(2,1)} %param.7) | copy-start | bytes 98308
  363.7 642.6 %copy-start.7 = (bf16[1024,128]{1,0:T(8,128)(2,1)S(1)}, bf16[1024,128]{1,0:T(8,128)(2,1)}, u32[]{:S(2)}) copy-start(bf16[1024,128]{1,0:T(8,128)(2,1)} %param.9) | copy-start | bytes 786436
  363.7 644.9 %copy-start.5 = (bf16[8192,128]{1,0:T(8,128)(2,1)S(1)}, bf16[8192,128]{1,0:T(8,128)(2,1)}, u32[]{:S(2)}) copy-start(bf16[8192,128]{1,0:T(8,128)(2,1)} %all-gather.2.cloned.1.call-done) | copy-start | bytes 6291460
  363.7 797.1 %all-reduce.4.cloned.1.call-start = ((), (), s32[]{:S(2)}) async-start(), calls=%async_computation.3 | async-start | bytes 3145728 | tf_op jit(solution)/shard_map/psum | solution.py:48
  1025.0 140.2 %copy-start.1 = (bf16[8192,128]{1,0:T(8,128)(2,1)S(1)}, bf16[8192,128]{1,0:T(8,128)(2,1)}, u32[]{:S(2)}) copy-start(bf16[8192,128]{1,0:T(8,128)(2,1)} %param.10) | copy-start | bytes 6291460
Sparse Core Ops, SparseCore 0:
  11.7 68.9 all-gather.1
  363.8 640.5 reduce-scatter.1
  1009.9 150.8 all-reduce.3
where the time goes:
time: 1170 us
  waiting for transfers between devices  711 us (61%)
  blocking collectives  259 us (22%)
  other arithmetic  108 us (9%)
  local copies, waits for them, and re-layouts  44.6 us (4%)
  matrix products  35.2 us (3%)
  between operations  15.7 us (1%)
    reduce_scatter x1, waiting for transfers between devices, local_step(): lax.psum_scatter(dq_part, 'dp', scatter_dimension=0, tiled=True)  639 us
    scatter-add x2, other arithmetic, local_step(): jnp.zeros(table_blk.shape, jnp.float32).at[cand_index].add(grad_cand)  72.4 us
    psum x1, waiting for transfers between devices, local_step(): lax.psum(jnp.einsum('ti,tf->if', features, d_pre, preferred_element_type=...  71.6 us
    unnamed x1, blocking collectives  69.1 us
    pmax x1, blocking collectives, local_step(): lax.pmax(jnp.max(cand_logit, axis=1), 'dp')  64 us
    psum x1, blocking collectives, local_step(): lax.psum(jnp.sum(jnp.exp(cand_logit - top_val[:, None]), axis=1), 'dp')  62.8 us
    psum x1, blocking collectives, local_step(): tgt_logit = lax.psum(jnp.where(tgt_own, tgt_dot, 0.0), 'dp')  62.6 us
    gather x1, local copies, waits for them, and re-layouts, local_step(): tgt_rows = table_blk[tgt_index]  29.7 us
  transfers between devices with their start and end apart: 3, of which 2 were waited for; matrix products, arithmetic and copies ran while one was open for 10% of the time, Pallas kernels for 0%

commit v1 on v0

v1 whole, which is shorter than its diff:
```python
import functools
import jax
import jax.numpy as jnp
from jax import lax
from jax.experimental import pallas as pl
from jax.experimental.pallas import tpu as pltpu
from jax.sharding import PartitionSpec as P

MESH = pl.DeviceIdType.MESH
F32, BF16 = jnp.float32, jnp.bfloat16
COORD = {"core": (1, 2), "x": (2, 4), "y": (8, 4), "z": (32, 4)}
ORDERS = (("x", "y", "z"), ("y", "z", "x"), ("z", "x", "y"))
NDEV = 128
NPEER = 10


def coord(me, axis):
    stride, radix = COORD[axis]
    return (me // stride) % radix


def peer(me, axis, k):
    stride, radix = COORD[axis]
    c = coord(me, axis)
    return me + ((c + k) % radix - c) * stride


def block_index(me, order):
    idx, weight = 0, 1
    for axis in order:
        idx = idx + coord(me, axis) * weight
        weight *= COORD[axis][1]
    return idx


def entry_barrier(me):
    barrier = pltpu.get_barrier_semaphore()
    for axis in COORD:
        for k in range(1, COORD[axis][1]):
            pl.semaphore_signal(barrier, inc=1, device_id=(peer(me, axis, k),), device_id_type=MESH)
    pl.semaphore_wait(barrier, NPEER)


def remote(src, dst, send, recv, dev):
    return pltpu.make_async_remote_copy(src_ref=src, dst_ref=dst, send_sem=send, recv_sem=recv, device_id=(dev,), device_id_type=MESH)


def gather_streams(me, streams, bulk, send_sem, recv_sem):
    pending, sent = [None] * len(streams), []
    for phase in range(4):
        for s, (ref, off, unit, order) in enumerate(streams):
            if pending[s]:
                for c in pending[s]:
                    c.wait_recv()
            if phase == 3:
                continue
            span = 4 ** phase
            idx = block_index(me, order)
            where = ref.at[pl.ds(off + (idx - idx % span) * unit, span * unit)]
            pending[s] = []
            for k in range(1, 4):
                n = s * 9 + phase * 3 + k - 1
                c = remote(where, where, send_sem.at[n], recv_sem.at[n], peer(me, order[phase], k))
                c.start()
                pending[s].append(c)
                sent.append(c)
    last = []
    for i, (ref, count) in enumerate(bulk):
        n = len(streams) * 9 + i
        where = ref.at[pl.ds(coord(me, "core") * count, count)]
        c = remote(where, where, send_sem.at[n], recv_sem.at[n], peer(me, "core", 1))
        c.start()
        last.append(c)
    for c in last:
        c.wait_recv()
    return sent + last


def add_rows(ref, start, rref, base, count, parts):
    def add(i, carry):
        acc = ref[start + i]
        for k in range(parts):
            acc = acc + rref[base + k * count + i]
        ref[start + i] = acc
        return carry

    lax.fori_loop(0, count, add, 0, unroll=4)


def scatter_streams(me, ref, half, rref, streams, send_sem, recv_sem):
    mine = coord(me, "core")
    c = remote(ref.at[pl.ds((1 - mine) * half, half)], rref.at[pl.ds(0, half)], send_sem.at[0], recv_sem.at[0], peer(me, "core", 1))
    c.start()
    sent = [c]
    c.wait_recv()
    add_rows(ref, mine * half, rref, 0, half, 1)
    pending, rbase = [None] * 3, half
    for step in range(4):
        for s, (off, unit, order) in enumerate(streams):
            idx = block_index(me, order)
            if pending[s]:
                for c in pending[s][0]:
                    c.wait_recv()
                add_rows(ref, pending[s][1], rref, pending[s][2], pending[s][3], 3)
            if step == 3:
                continue
            span = 4 ** (2 - step)
            axis = order[2 - step]
            start = mine * half + off + (idx - idx % (4 * span)) * unit
            d = coord(me, axis)
            copies = []
            for k in range(1, 4):
                n = 1 + s * 9 + step * 3 + k - 1
                src = ref.at[pl.ds(start + (d + k) % 4 * span * unit, span * unit)]
                dst = rref.at[pl.ds(rbase + (k - 1) * span * unit, span * unit)]
                c = remote(src, dst, send_sem.at[n], recv_sem.at[n], peer(me, axis, k))
                c.start()
                copies.append(c)
            sent += copies
            pending[s] = (copies, start + d * span * unit, rbase, span * unit)
            rbase += 3 * span * unit
    return sent


def gelu_parts(a):
    c = 0.7978845608028654
    inner = jnp.tanh(c * (a + 0.044715 * (a * a * a)))
    half = 0.5 * (1.0 + inner)
    return a * half, half + 0.5 * a * (1.0 - inner * inner) * (c * (1.0 + 3.0 * 0.044715 * (a * a)))


def nt_dot(a, b):
    return lax.dot_general(a, b, (((1,), (1,)), ((), ())), preferred_element_type=F32)


def tn_dot(a, b):
    return lax.dot_general(a, b, (((0,), (0,)), ((), ())), preferred_element_type=F32)


H_OFF = (0, 192, 384)
H_UNIT = (3, 3, 2)
H_FIRST = (0, 3, 6)


def query_kernel(x_ref, win_ref, wout_ref, tgt_ref, h_ref, tall_ref, pre_ref, send_sem, recv_sem):
    me = lax.axis_index("dp")
    entry_barrier(me)
    pre = jnp.dot(x_ref[...], win_ref[...], preferred_element_type=F32)
    pre_ref[...] = pre
    act = gelu_parts(pre)[0].astype(BF16)
    query = jnp.dot(act, wout_ref[...], preferred_element_type=F32)
    core = coord(me, "core")
    streams = []
    for s in range(3):
        idx = block_index(me, ORDERS[s])
        for g in range(H_UNIT[s]):
            row = 8 * (H_FIRST[s] + g)
            h_ref[core * 512 + H_OFF[s] + idx * H_UNIT[s] + g] = query[row : row + 8, :].astype(BF16)
        streams.append((h_ref, core * 512 + H_OFF[s], H_UNIT[s], ORDERS[s]))
    tall_ref[core * 64 + block_index(me, ORDERS[2])] = tgt_ref[...]
    streams.append((tall_ref, core * 64, 1, ORDERS[2]))
    for c in gather_streams(me, streams, [(h_ref, 512), (tall_ref, 64)], send_sem, recv_sem):
        c.wait_send()


def stats_kernel(st_ref, out_ref, recv, cur, send_sem, recv_sem):
    me = lax.axis_index("dp")
    entry_barrier(me)
    sent = []
    pending = [None] * 3
    for phase in range(5):
        for s in range(3):
            g0, ng = H_FIRST[s], H_UNIT[s]
            if phase:
                for c in pending[s]:
                    c.wait_recv()
                base = 8 * (0, 3, 6, 9)[phase - 1]
                npart = len(pending[s])

                def merge(g, carry, phase=phase, base=base, npart=npart):
                    old = st_ref[g] if phase == 1 else cur[8 * (phase - 2) + g]
                    parts = [recv[base + 8 * k + g] for k in range(npart)]
                    top, z = old[0], old[2]
                    for p in parts:
                        top = jnp.maximum(top, p[0])
                        z = jnp.maximum(z, p[2])
                    total = old[1] * jnp.exp(old[0] - top)
                    for p in parts:
                        total = total + p[1] * jnp.exp(p[0] - top)
                    row = 8 * (phase - 1) + g
                    cur[row, 0] = top
                    cur[row, 1] = total
                    cur[row, 2] = z
                    return carry

                lax.fori_loop(g0, g0 + ng, merge, 0)
            if phase == 4:
                continue
            axis = (ORDERS[s] + ("core",))[phase]
            src = st_ref.at[pl.ds(g0, ng)] if phase == 0 else cur.at[pl.ds(8 * (phase - 1) + g0, ng)]
            base = 8 * (0, 3, 6, 9)[phase]
            pending[s] = []
            for k in range(1, COORD[axis][1]):
                n = s * NPEER + phase * 3 + k - 1
                c = remote(src, recv.at[pl.ds(base + 8 * (k - 1) + g0, ng)], send_sem.at[n], recv_sem.at[n], peer(me, axis, k))
                c.start()
                pending[s].append(c)
                sent.append(c)
    for g in range(8):
        m, t, z = cur[24 + g, 0], cur[24 + g, 1], cur[24 + g, 2]
        top = jnp.maximum(m, z)
        out_ref[0, 8 * g : 8 * g + 8, :] = top + jnp.log(t * jnp.exp(m - top) + jnp.exp(z - top))
        out_ref[1, 8 * g : 8 * g + 8, :] = z
    for c in sent:
        c.wait_send()


def grad_kernel(dq_ref, x_ref, wout_ref, pre_ref, dwin_ref, dwout_ref, acc, recv, tiles, trecv, whole, send_sem, recv_sem):
    me = lax.axis_index("dp")
    entry_barrier(me)

    def fill(i, carry):
        acc[i] = dq_ref[i]
        return carry

    lax.fori_loop(0, 1024, fill, 0, unroll=8)
    streams = [(H_OFF[s], H_UNIT[s], ORDERS[s]) for s in range(3)]
    sent = scatter_streams(me, acc, 512, recv, streams, send_sem.at[0], recv_sem.at[0])
    core = coord(me, "core")
    rows = []
    for s in range(3):
        idx = block_index(me, ORDERS[s])
        for g in range(H_UNIT[s]):
            rows.append(acc[core * 512 + H_OFF[s] + idx * H_UNIT[s] + g])
    dh = jnp.concatenate(rows, axis=0).astype(BF16)
    act, slope = gelu_parts(pre_ref[...])
    d_pre = (slope * nt_dot(dh, wout_ref[...])).astype(BF16)
    dw_out = tn_dot(act.astype(BF16), dh)
    tiles[0:128] = dw_out.reshape(128, 8, 128)
    dw_in = tn_dot(x_ref[...], d_pre)
    for j in range(8):
        tiles[128 + 32 * j : 160 + 32 * j] = dw_in[:, 128 * j : 128 * j + 128].reshape(32, 8, 128)
    streams = [(64 * s, 1, ORDERS[s]) for s in range(3)]
    sent2 = scatter_streams(me, tiles, 192, trecv, streams, send_sem.at[1], recv_sem.at[1])
    for c in sent + sent2:
        c.wait_send()
    streams = []
    for s in range(3):
        own = core * 192 + 64 * s + block_index(me, ORDERS[s])
        whole[own] = tiles[own]
        streams.append((whole, core * 192 + 64 * s, 1, ORDERS[s]))
    sent = gather_streams(me, streams, [(whole, 192)], send_sem.at[2], recv_sem.at[2])
    dwout_ref[...] = whole[0:128].reshape(1024, 128)
    for j in range(8):
        dwin_ref[:, 128 * j : 128 * j + 128] = whole[128 + 32 * j : 160 + 32 * j].reshape(256, 128)
    for c in sent:
        c.wait_send()


def vmem(n):
    return [pl.BlockSpec(memory_space=pltpu.VMEM)] * n


def params(cid):
    return pltpu.CompilerParams(collective_id=cid, has_side_effects=True, vmem_limit_bytes=48 * 1024 * 1024)


def dma(*shape):
    return pltpu.SemaphoreType.DMA(shape)


def solution(mesh):
    num_dev = mesh.shape["dp"]

    def local_step(features, w_in, w_out, table_blk, cand_ids, log_q, targets):
        dev_index = lax.axis_index("dp")
        block_rows = table_blk.shape[0]
        cand_dev = cand_ids.shape[0] // num_dev
        tok_total = features.shape[0] * num_dev
        tgt_row = jnp.pad(targets[None, :], ((0, 0), (0, 64)))
        h_all, tall, pre = pl.pallas_call(
            query_kernel,
            out_shape=[jax.ShapeDtypeStruct((1024, 8, 128), BF16), jax.ShapeDtypeStruct((128, 1, 128), jnp.int32), jax.ShapeDtypeStruct((64, 1024), F32)],
            in_specs=vmem(4), out_specs=vmem(3),
            scratch_shapes=[dma(4 * NPEER), dma(4 * NPEER)],
            compiler_params=params(0), name="query_gather",
        )(features, w_in, w_out, tgt_row)
        query_all = h_all.reshape(8192, 128)
        t5 = tall[:, 0, :64].reshape(2, 4, 4, 4, 64)
        tgt_all = jnp.concatenate([
            t5.transpose(0, 3, 1, 2, 4)[..., 0:24].reshape(2, -1),
            t5.transpose(0, 2, 3, 1, 4)[..., 24:48].reshape(2, -1),
            t5[..., 48:64].reshape(2, -1)], axis=1).reshape(-1)
        row_base = dev_index * block_rows
        tgt_local = tgt_all - row_base
        tgt_own = (tgt_local >= 0) & (tgt_local < block_rows)
        tgt_index = jnp.clip(tgt_local, 0, block_rows - 1)
        tgt_rows = table_blk[tgt_index]
        own_cands = lax.dynamic_slice_in_dim(cand_ids, dev_index * cand_dev, cand_dev)
        own_logq = lax.dynamic_slice_in_dim(log_q, dev_index * cand_dev, cand_dev)
        cand_index = own_cands - row_base
        cand_rows = table_blk[cand_index]
        tgt_dot = jnp.einsum("td,td->t", query_all, tgt_rows, preferred_element_type=F32)
        z_own = jnp.where(tgt_own, tgt_dot, -jnp.inf)
        cand_logit = jnp.einsum("td,cd->tc", query_all, cand_rows, preferred_element_type=F32) - own_logq[None, :]
        cand_logit = jnp.where(own_cands[None, :] == tgt_all[:, None], -1e9, cand_logit)
        top = jnp.max(cand_logit, axis=1)
        part = jnp.sum(jnp.exp(cand_logit - top[:, None]), axis=1)
        stats = jnp.stack([v.reshape(8, 8, 128) for v in (top, part, z_own)], axis=1)
        norm = pl.pallas_call(
            stats_kernel,
            out_shape=jax.ShapeDtypeStruct((2, 64, 128), F32),
            in_specs=vmem(1), out_specs=vmem(1)[0],
            scratch_shapes=[pltpu.VMEM((80, 3, 8, 128), F32), pltpu.VMEM((32, 3, 8, 128), F32), dma(3 * NPEER), dma(3 * NPEER)],
            compiler_params=params(1), name="stats_reduce",
        )(stats)
        log_norm, tgt_logit = norm[0].reshape(8192), norm[1].reshape(8192)
        loss = jnp.sum(log_norm - tgt_logit) / tok_total
        grad_tgt = (jnp.exp(tgt_logit - log_norm) - 1.0) / tok_total
        cand_grad = (jnp.exp(cand_logit - log_norm[:, None]) / tok_total).astype(BF16)
        own_grad = jnp.where(tgt_own, grad_tgt, 0.0)
        dq_part = own_grad[:, None] * tgt_rows + jnp.einsum("tc,cd->td", cand_grad, cand_rows, preferred_element_type=F32)
        grad_w_in, grad_w_out = pl.pallas_call(
            grad_kernel,
            out_shape=[jax.ShapeDtypeStruct((256, 1024), F32), jax.ShapeDtypeStruct((1024, 128), F32)],
            in_specs=vmem(4), out_specs=vmem(2),
            scratch_shapes=[
                pltpu.VMEM((1024, 8, 128), F32), pltpu.VMEM((8 * 127 + 8, 8, 128), F32),
                pltpu.VMEM((384, 8, 128), F32), pltpu.VMEM((3 * 127, 8, 128), F32), pltpu.VMEM((384, 8, 128), F32),
                dma(3, 3 * NPEER), dma(3, 3 * NPEER)],
            compiler_params=params(2), name="grad_reduce",
        )(dq_part.reshape(1024, 8, 128), features, w_out, pre)
        grad_cand = jnp.einsum("tc,td->cd", cand_grad, query_all, preferred_element_type=F32)
        grad_blk = jnp.zeros(table_blk.shape, F32).at[cand_index].add(grad_cand).at[tgt_index].add(own_grad[:, None] * query_all)
        return loss, grad_blk, grad_w_in, grad_w_out

    return jax.shard_map(local_step, mesh=mesh, in_specs=(P("dp", None), P(), P(), P("dp", None), P(), P(), P("dp")), out_specs=(P(), P("dp", None), P(), P()), check_vma=False)
```

time: 1170 us -> 280 us (0.24)
  waiting for transfers between devices: 711 us -> 0 us
  blocking collectives: 259 us -> 0 us
  Pallas kernels: 0 us -> 100 us
  between operations: 15.7 us -> 2.67 us
    reduce_scatter x1 -> x0, waiting for transfers between devices: 639 us -> none  [local_step(): lax.psum_scatter(dq_part, 'dp', scatter_dimension=0, tiled=True)]
    psum x2 -> x0, blocking collectives: 125 us -> none  [the longest x1 62.8 us: local_step(): lax.psum(jnp.sum(jnp.exp(cand_logit - top_val[:, None]), axis=1), 'dp')]
    pallas_call x0 -> x3, Pallas kernels: none -> 100 us  [the longest x1 59.6 us: local_step(): pl.pallas_call(grad_kernel, out_shape=[jax.ShapeDtypeStruct((256, 1024),...]
    psum x1 -> x0, waiting for transfers between devices: 71.6 us -> none  [local_step(): lax.psum(jnp.einsum('ti,tf->if', features, d_pre, preferred_element_type=...]
    unnamed x1 -> x0, blocking collectives: 69.1 us -> none
    pmax x1 -> x0, blocking collectives: 64 us -> none  [local_step(): lax.pmax(jnp.max(cand_logit, axis=1), 'dp')]
    dot_general x7 -> x3, matrix products: 35.2 us -> 25.3 us  [the longest x1 12.5 us: local_step(): jnp.einsum('td,cd->tc', query_all, cand_rows, preferred_element_type=F32)]
  transfers between devices with their start and end apart: 3 -> 0, of which waited for: 2 -> 0; matrix products, arithmetic and copies ran while one was open for 10% -> 0% of each run, Pallas kernels for 0% -> 0%
where the time goes in v1:
time: 280 us; the launch traced here: 279 us
  other arithmetic  108 us (39%)
  Pallas kernels  100 us (36%)
  local copies, waits for them, and re-layouts  42.7 us (15%)
  matrix products  25.3 us (9%)
    scatter-add x2, other arithmetic, local_step(): jnp.zeros(table_blk.shape, F32).at[cand_index].add(grad_cand).at[tgt_index]  72.8 us
    pallas_call x1, Pallas kernels, local_step(): pl.pallas_call(grad_kernel, out_shape=[jax.ShapeDtypeStruct((256, 1024),...  59.6 us
    gather x1, local copies, waits for them, and re-layouts, local_step(): tgt_rows = table_blk[tgt_index]  29.7 us
    pallas_call x1, Pallas kernels, local_step(): pl.pallas_call(query_kernel, out_shape=[jax.ShapeDtypeStruct((1024, 8, 12...  24 us
    pallas_call x1, Pallas kernels, local_step(): pl.pallas_call(stats_kernel, out_shape=jax.ShapeDtypeStruct((2, 64, 128),...  16.5 us
    convert_element_type x1, other arithmetic, local_step(): (jnp.exp(cand_logit - log_norm[:, None]) / tok_total).astype(BF16)  15.4 us
    reduce_sum x1, other arithmetic, local_step(): part = jnp.sum(jnp.exp(cand_logit - top[:, None]), axis=1)  14.9 us
    dot_general x1, matrix products, local_step(): jnp.einsum('td,cd->tc', query_all, cand_rows, preferred_element_type=F32)  12.5 us

profile of v1, /device:TPU:1, one launch (start us, length us, event | category | flops | bytes accessed | tf_op | source)
XLA Modules:
  0.0 278.9 jit_solution(2945259531246502446)
XLA Ops:
  0.6 0.0 copy-start
  0.7 0.8 pad.4.tgt_ref
  1.5 0.7 dynamic_slice.7
  2.1 0.7 broadcast_clamp_fusion.1
  2.8 0.0 copy-done
  2.8 3.2 %gather_fusion = bf16[1024,128]{1,0:T(8,128)(2,1)S(1)} fusion(bf16[8192,128]{1,0:T(8,128)(2,1)S(1)} %copy-done, s32[1024]{0:T(1024)S(1)} %get-tuple-element.14), kind=kCustom, calls=%fused_computation | custom fusion | bytes 528384 | tf_op jit(solution)/shard_map/gather | solution.py:302
  6.1 0.0 copy-start.5
  6.1 0.9 copy-done.5
  7.0 0.0 copy-start.7
  7.0 1.0 copy-done.7
  8.1 0.0 copy-start.9
  8.1 0.8 copy-done.9
  8.8 24.0 %query_gather.1 = (bf16[1024,8,128]{2,1,0:T(8,128)(2,1)S(1)}, s32[128,1,128]{2,1,0:T(1,128)S(1)}, f32[64,1024]{1,0:T(8,128)S(1)}) custom-call(bf16[64,256]{1,0:T(8,128)(2,1)S(1)} %copy-done.9, bf16[256,1024]{1,0:T(8,128)(2,1)S(1)} %copy-done.7, bf16[1024,128]{1,0:T(8,128)(2,1)S(1)} %copy-done.5, s32[1,128]{1,0:T(1,128)S(1)} %pad.4.tgt_ref), custom_call_target="tpu_custom_call" | custom-call | tf_op jit(solution)/shard_map/query_gather/pallas_call | solution.py:281
  32.8 0.0 copy-start.2
  32.8 1.3 copy-done.2
  34.1 0.1 slice.30
  34.2 0.1 reshape.77
  34.4 0.1 reshape.75
  34.5 0.1 slice.29
  34.6 0.1 reshape.76
  34.9 29.7 %gather_fusion.1 = bf16[8192,128]{1,0:T(8,128)(2,1)} fusion(bf16[8192,128]{1,0:T(8,128)(2,1)S(1)} %copy-done, s32[8192]{0:T(1024)S(1)} %broadcast_clamp_fusion), kind=kCustom, calls=%fused_computation.1 | custom fusion | bytes 4227072 | tf_op jit(solution)/shard_map/gather | solution.py:298
  64.6 0.0 copy-start.3
  64.6 3.5 %fusion.1 = f32[8192]{0:T(1024)S(1)} fusion(bf16[8192,128]{1,0:T(8,128)(2,1)} %gather_fusion.1, bf16[1024,8,128]{2,1,0:T(8,128)(2,1)} %copy-done.2), kind=kLoop, calls=%fused_computation.12 | loop fusion | flops 4186112 | bytes 4227072 | tf_op jit(solution)/shard_map/td,td->t/dot_general | solution.py:303
  68.1 0.0 copy-done.3
  68.2 12.5 %fusion = (f32[8192]{0:T(1024)S(1)}, f32[8192,1024]{0,1:T(8,128)}) fusion(f32[1024]{0:T(1024)S(1)} %dynamic_slice.7, s32[8192]{0:T(1024)S(1)} %bitcast.58, s32[1024]{0:T(1024)S(1)} %get-tuple-element.16, bf16[1024,128]{1,0:T(8,128)(2,1)S(1)} %gather_fusion, bf16[1024,8,128]{2,1,0:T(8,128)(2,1)S(1)} %copy-done.3), kind=kOutput, calls=%fused_computation.7 | convolution fusion | flops 2181029888 | bytes 35987456 | tf_op jit(solution)/shard_map/td,cd->tc/dot_general | solution.py:305
  80.7 14.9 %exponential_reduce_fusion = f32[8192]{0:T(1024)S(1)} fusion(f32[8192,1024]{0,1:T(8,128)} %get-tuple-element.22, f32[8192]{0:T(1024)S(1)} %get-tuple-element.21, f32[1024]{0:T(1024)S(1)} %dynamic_slice.7, s32[8192]{0:T(1024)S(1)} %bitcast.59, s32[1024]{0:T(1024)S(1)} %get-tuple-element.16), kind=kLoop, calls=%fused_computation.5 | loop fusion | flops 41934848 | bytes 33660928 | tf_op jit(solution)/shard_map/reduce_sum | solution.py:308
  95.6 16.5 %stats_reduce.1 = f32[2,64,128]{2,1,0:T(8,128)S(1)} custom-call(f32[8,3,8,128]{3,2,1,0:T(8,128)S(1)} %pad_maximum_fusion.st_ref), custom_call_target="tpu_custom_call" | custom-call | tf_op jit(solution)/shard_map/stats_reduce/pallas_call | solution.py:310
  112.2 0.6 slice_bitcast_fusion
  113.4 0.0 copy-start.4
  113.4 15.4 %multiply_convert_fusion = bf16[8192,1024]{0,1:T(8,128)(2,1)S(1)} fusion(f32[8192,1024]{0,1:T(8,128)} %get-tuple-element.22, f32[8192]{0:T(1024)S(1)} %get-tuple-element.19, f32[1024]{0:T(1024)S(1)} %dynamic_slice.7, s32[8192]{0:T(1024)S(1)} %bitcast.60, s32[1024]{0:T(1024)S(1)} %get-tuple-element.16), kind=kLoop, calls=%fused_computation.4 | loop fusion | flops 50331648 | bytes 50405376 | tf_op jit(solution)/shard_map/convert_element_type | solution.py:320
  128.9 0.0 copy-done.4
  128.9 0.0 copy-start.11
  128.9 5.3 %fusion.5 = f32[1024,128]{1,0:T(8,128)} fusion(bf16[8192,1024]{0,1:T(8,128)(2,1)S(1)} %multiply_convert_fusion, bf16[1024,8,128]{2,1,0:T(8,128)(2,1)S(1)} %copy-done.4), kind=kOutput, calls=%fused_computation.16 | convolution fusion | flops 2147483648 | bytes 19398656 | tf_op jit(solution)/shard_map/tc,td->cd/dot_general | solution.py:333
  134.2 0.0 copy-done.11
  134.2 0.0 copy-start.6
  134.2 0.0 copy-start.10
  134.2 7.5 %fusion.3.dq_ref = f32[1024,8,128]{2,1,0:T(8,128)} fusion(bf16[8192,1024]{0,1:T(8,128)(2,1)S(1)} %multiply_convert_fusion, bf16[1024,128]{1,0:T(8,128)(2,1)S(1)} %gather_fusion, bf16[8192,128]{1,0:T(8,128)(2,1)S(1)} %copy-done.11, f32[8192]{0:T(1024)S(1)} %fusion.15), kind=kOutput, calls=%fused_computation.14 | convolution fusion | flops 2150629376 | bytes 23363584 | tf_op jit(solution)/shard_map/tc,cd->td/dot_general | solution.py:322
  141.7 0.0 copy-done.6
  141.7 0.0 copy-done.10
  141.7 59.6 %grad_reduce.1 = (f32[256,1024]{1,0:T(8,128)S(1)}, f32[1024,128]{1,0:T(8,128)S(1)}) custom-call(f32[1024,8,128]{2,1,0:T(8,128)} %fusion.3.dq_ref, bf16[64,256]{1,0:T(8,128)(2,1)S(1)} %copy-done.10, bf16[1024,128]{1,0:T(8,128)(2,1)S(1)} %copy-done.6, f32[64,1024]{1,0:T(8,128)S(1)} %get-tuple-element.11.pre_ref), custom_call_target="tpu_custom_call" | custom-call | tf_op jit(solution)/shard_map/grad_reduce/pallas_call | solution.py:323
  201.3 0.0 copy-start.8
  201.3 0.8 copy-done.8
  202.1 0.0 copy-start.1
  202.1 8.8 %scatter_custom_fusion = f32[8192,128]{1,0:T(8,128)} fusion(s32[1024]{0:T(1024)S(1)} %get-tuple-element.15, f32[1024,128]{1,0:T(8,128)} %fusion.5, f32[]{:T(128)} %constant.18.clone.1), kind=kCustom, calls=%fused_computation.21 | custom fusion | flops 131072 | bytes 4194816 | tf_op jit(solution)/shard_map/scatter-add | solution.py:334
  210.9 64.0 %scatter_custom_fusion.1 = f32[8192,128]{1,0:T(8,128)} fusion(f32[8192,128]{1,0:T(8,128)} %scatter_custom_fusion, s32[8192]{0:T(1024)S(1)} %bitcast.65, bf16[1024,8,128]{2,1,0:T(8,128)(2,1)} %copy-done.2, f32[8192]{0:T(1024)S(1)} %fusion.15), kind=kCustom, calls=%fused_computation.13 | custom fusion | flops 3145728 | bytes 6324224 | tf_op jit(solution)/shard_map/scatter-add | solution.py:334
  274.9 1.0 copy.29
  275.9 1.9 copy.30
  277.7 0.0 copy-done.1
  (13 shorter events, 0.2 us)
Async XLA Ops:
  0.6 2.2 copy-start
  6.1 1.0 copy-start.5
  7.0 1.0 copy-start.7
  8.1 0.8 copy-start.9
  32.8 1.3 copy-start.2
  64.6 3.6 %copy-start.3 = (bf16[1024,8,128]{2,1,0:T(8,128)(2,1)S(1)}, bf16[1024,8,128]{2,1,0:T(8,128)(2,1)}, u32[]{:S(2)}) copy-start(bf16[1024,8,128]{2,1,0:T(8,128)(2,1)} %copy-done.2) | copy-start | bytes 6291460
  113.4 15.5 %copy-start.4 = (bf16[1024,8,128]{2,1,0:T(8,128)(2,1)S(1)}, bf16[1024,8,128]{2,1,0:T(8,128)(2,1)}, u32[]{:S(2)}) copy-start(bf16[1024,8,128]{2,1,0:T(8,128)(2,1)} %copy-done.2) | copy-start | bytes 6291460
  128.9 5.3 %copy-start.11 = (bf16[8192,128]{1,0:T(8,128)(2,1)S(1)}, bf16[8192,128]{1,0:T(8,128)(2,1)}, u32[]{:S(2)}) copy-start(bf16[8192,128]{1,0:T(8,128)(2,1)} %gather_fusion.1) | copy-start | bytes 6291460
  134.2 7.5 %copy-start.6 = (bf16[1024,128]{1,0:T(8,128)(2,1)S(1)}, bf16[1024,128]{1,0:T(8,128)(2,1)}, u32[]{:S(2)}) copy-start(bf16[1024,128]{1,0:T(8,128)(2,1)} %wout_ref.3) | copy-start | bytes 786436
  134.2 7.5 %copy-start.10 = (bf16[64,256]{1,0:T(8,128)(2,1)S(1)}, bf16[64,256]{1,0:T(8,128)(2,1)}, u32[]{:S(2)}) copy-start(bf16[64,256]{1,0:T(8,128)(2,1)} %x_ref.3) | copy-start | bytes 98308
  201.3 0.8 copy-start.8
  202.1 75.6 %copy-start.1 = (bf16[8192,128]{1,0:T(8,128)(2,1)S(1)}, bf16[8192,128]{1,0:T(8,128)(2,1)}, u32[]{:S(2)}) copy-start(bf16[8192,128]{1,0:T(8,128)(2,1)} %param.10) | copy-start | bytes 6291460

commit v2 on v1

--- a/solution.py
+++ b/solution.py
@@ -12,6 +12,11 @@
 ORDERS = (("x", "y", "z"), ("y", "z", "x"), ("z", "x", "y"))
 NDEV = 128
 NPEER = 10
+LANE, TOK, ALL, KILO, WIDE = 128, 64, 8192, 1024, 256
+
+
+def one(i):
+    return pl.ds(i, 1)
 
 
 def coord(me, axis):
@@ -157,9 +162,9 @@
             row = 8 * (H_FIRST[s] + g)
             h_ref[core * 512 + H_OFF[s] + idx * H_UNIT[s] + g] = query[row : row + 8, :].astype(BF16)
         streams.append((h_ref, core * 512 + H_OFF[s], H_UNIT[s], ORDERS[s]))
-    tall_ref[core * 64 + block_index(me, ORDERS[2])] = tgt_ref[...]
-    streams.append((tall_ref, core * 64, 1, ORDERS[2]))
-    for c in gather_streams(me, streams, [(h_ref, 512), (tall_ref, 64)], send_sem, recv_sem):
+    tall_ref[core * TOK + block_index(me, ORDERS[2])] = tgt_ref[...]
+    streams.append((tall_ref, core * TOK, 1, ORDERS[2]))
+    for c in gather_streams(me, streams, [(h_ref, 512), (tall_ref, TOK)], send_sem, recv_sem):
         c.wait_send()
 
 
@@ -215,6 +220,150 @@
         c.wait_send()
 
 
+TILE = KILO
+
+
+def score_kernel(h_ref, blk_ref, cand_ref, cid_ref, logq_ref, tgt_ref, e_ref, st_ref, pos_ref, row_ref, tok_ref, hc_ref, tc_ref, zd, cidb, logqb):
+    step = pl.program_id(0)
+    block_rows = blk_ref.shape[0]
+    base = lax.axis_index("dp") * block_rows
+
+    @pl.when(step == 0)
+    def _():
+        cidb[...] = jnp.broadcast_to(cid_ref[...], cidb.shape)
+        logqb[...] = jnp.broadcast_to(logq_ref[...], logqb.shape)
+        local = tgt_ref[...] - base
+        own = (local >= 0) & (local < block_rows)
+        own_f = jnp.where(own, 1.0, 0.0)
+        own_b = own_f.astype(BF16)
+        up = lax.broadcasted_iota(jnp.int32, (LANE, LANE), 0) < lax.broadcasted_iota(jnp.int32, (LANE, LANE), 1)
+        prefix = jnp.dot(own_b, jnp.where(up, 1.0, 0.0).astype(BF16), preferred_element_type=F32)
+        total = jnp.dot(own_b, jnp.ones((LANE, LANE), BF16), preferred_element_type=F32)
+        low = lax.broadcasted_iota(jnp.int32, (TOK, TOK), 0) > lax.broadcasted_iota(jnp.int32, (TOK, TOK), 1)
+        offset = jnp.dot(jnp.where(low, 1.0, 0.0).astype(BF16), total.astype(BF16), preferred_element_type=F32)
+        pos_ref[...] = jnp.where(own, prefix + offset, -1.0)
+        zd[...] = jnp.zeros_like(zd)
+        chunks = (jnp.sum(own_f).astype(jnp.int32) + 127) // LANE
+        slot0 = lax.broadcasted_iota(jnp.int32, (LANE, LANE), 0).astype(F32)
+        lane = lax.broadcasted_iota(jnp.int32, (1, LANE), 1)
+
+        def chunk(c, carry):
+            slot = slot0 + (c * LANE).astype(F32)
+
+            def collect(r, acc):
+                hsum, code = acc
+                hit = pos_ref[one(r), :] == slot
+                local_row = tgt_ref[one(r), :] - base
+                code = code + jnp.where(hit, local_row * ALL + (lane + r * LANE), 0)
+                pick = jnp.where(hit, 1.0, 0.0).astype(BF16)
+                return hsum + jnp.dot(pick, h_ref[pl.ds(r * LANE, LANE), :], preferred_element_type=F32), code
+
+            hsum, code = lax.fori_loop(0, TOK, collect, (jnp.zeros((LANE, LANE), F32), jnp.zeros((LANE, LANE), jnp.int32)), unroll=4)
+            row = jnp.sum((code // ALL).astype(F32), axis=1, keepdims=True)
+            tok = jnp.sum((code % ALL).astype(F32), axis=1, keepdims=True)
+            rowb = jnp.broadcast_to(row, (LANE, LANE))
+            row_ref[one(c), :] = jnp.transpose(rowb)[0:1, :].astype(jnp.int32)
+            tok_ref[one(c), :] = jnp.transpose(jnp.broadcast_to(tok, (LANE, LANE)))[0:1, :].astype(jnp.int32)
+
+            def fetch(r, acc):
+                hit = rowb == (lane + r * LANE).astype(F32)
+                pick = jnp.where(hit, 1.0, 0.0).astype(BF16)
+                return acc + jnp.dot(pick, blk_ref[pl.ds(r * LANE, LANE), :], preferred_element_type=F32)
+
+            tsum = lax.fori_loop(0, block_rows // LANE, fetch, jnp.zeros((LANE, LANE), F32), unroll=4)
+            hc_ref[pl.ds(c * LANE, LANE), :] = hsum.astype(BF16)
+            tc_ref[pl.ds(c * LANE, LANE), :] = tsum.astype(BF16)
+            z = jnp.broadcast_to(jnp.sum(hsum * tsum, axis=1, keepdims=True), (LANE, LANE))
+
+            def spread(r, carry2):
+                hit = pos_ref[one(r), :] == slot
+                zd[one(r), :] += jnp.sum(jnp.where(hit, z, 0.0), axis=0, keepdims=True)
+                return carry2
+
+            lax.fori_loop(0, TOK, spread, 0, unroll=4)
+            return carry
+
+        lax.fori_loop(0, chunks, chunk, 0)
+
+    for j in range(TILE // WIDE):
+        col = pl.multiple_of(step * TILE + WIDE * j, WIDE)
+        dots = nt_dot(cand_ref[...], h_ref[pl.ds(col, WIDE), :])
+        for half in range(2):
+            q = 2 * j + half
+            cols = slice(LANE * q, LANE * q + LANE)
+            tgt = tgt_ref[pl.ds(step * (TILE // LANE) + q, 1), :]
+            s = dots[:, LANE * half : LANE * half + LANE] - logqb[...]
+            s = jnp.where(cidb[...] == tgt, -1e9, s)
+            m = jnp.max(s, axis=0, keepdims=True)
+            e = jnp.exp(s - m)
+            e_ref[:, cols] = e
+            st_ref[0, 0, q : q + 1, :] = m
+            st_ref[0, 1, q : q + 1, :] = jnp.sum(e, axis=0, keepdims=True)
+    grp = pl.ds(pl.multiple_of(step * 8, 8), 8)
+    st_ref[0, 2] = jnp.where(pos_ref[grp, :] >= 0.0, zd[grp, :], -jnp.inf)
+
+
+def assemble_kernel(cidx_ref, row_ref, tok_ref, e_ref, st_ref, norm_ref, h_ref, cand_ref, pos_ref, hc_ref, tc_ref, dq_ref, de_ref, dcand, gh, gt, candt):
+    step = pl.program_id(0)
+    tokens = h_ref.shape[0]
+
+    @pl.when(step == 0)
+    def _():
+        dcand[...] = jnp.zeros_like(dcand)
+        candt[...] = jnp.transpose(cand_ref[...].astype(F32)).astype(BF16)
+
+    for j in range(TILE // WIDE):
+        probs = []
+        for half in range(2):
+            q = 2 * j + half
+            cols = slice(LANE * q, LANE * q + LANE)
+            scale = jnp.exp(st_ref[0, 0, q : q + 1, :] - norm_ref[0, pl.ds(step * 8 + q, 1), :]) / tokens
+            probs.append((e_ref[:, cols] * scale).astype(BF16))
+        p = jnp.concatenate(probs, axis=1)
+        row = pl.multiple_of(step * TILE + WIDE * j, WIDE)
+        dq_ref[pl.ds(row, WIDE), :] = jnp.transpose(jnp.dot(candt[...], p, preferred_element_type=F32))
+        dcand[...] += jnp.dot(p, h_ref[pl.ds(row, WIDE), :], preferred_element_type=F32)
+
+    @pl.when(step == pl.num_programs(0) - 1)
+    def _():
+        def clear(i, carry):
+            de_ref[pl.ds(pl.multiple_of(i * TOK, TOK), TOK), :] = jnp.zeros((TOK, LANE), F32)
+            return carry
+
+        lax.fori_loop(0, de_ref.shape[0] // TOK, clear, 0)
+
+        def place(i, carry):
+            for u in range(8):
+                de_ref[pl.ds(cidx_ref[i * 8 + u], 1), :] = dcand[pl.ds(i * 8 + u, 1), :]
+            return carry
+
+        lax.fori_loop(0, dcand.shape[0] // 8, place, 0)
+        count = jnp.sum(jnp.where(pos_ref[...] >= 0.0, 1.0, 0.0)).astype(jnp.int32)
+        slot0 = lax.broadcasted_iota(jnp.int32, (LANE, LANE), 0).astype(F32)
+
+        def chunk(c, carry):
+            slot = slot0 + (c * LANE).astype(F32)
+
+            def collect(r, acc):
+                hit = pos_ref[one(r), :] == slot
+                g = (jnp.exp(norm_ref[1, one(r), :] - norm_ref[0, one(r), :]) - 1.0) / tokens
+                return acc + jnp.where(hit, g, 0.0)
+
+            g = jnp.sum(lax.fori_loop(0, TOK, collect, jnp.zeros((LANE, LANE), F32), unroll=4), axis=1, keepdims=True)
+            gh[...] = g * hc_ref[pl.ds(c * LANE, LANE), :].astype(F32)
+            gt[...] = g * tc_ref[pl.ds(c * LANE, LANE), :].astype(F32)
+
+            def put(i, carry2):
+                de_ref[pl.ds(row_ref[c, i], 1), :] += gh[one(i), :]
+                dq_ref[pl.ds(tok_ref[c, i], 1), :] += gt[one(i), :]
+                return carry2
+
+            lax.fori_loop(0, jnp.minimum(count - c * LANE, LANE), put, 0)
+            return carry
+
+        lax.fori_loop(0, (count + 127) // LANE, chunk, 0)
+
+
 def grad_kernel(dq_ref, x_ref, wout_ref, pre_ref, dwin_ref, dwout_ref, acc, recv, tiles, trecv, whole, send_sem, recv_sem):
     me = lax.axis_index("dp")
     entry_barrier(me)
@@ -223,7 +372,7 @@
         acc[i] = dq_ref[i]
         return carry
 
-    lax.fori_loop(0, 1024, fill, 0, unroll=8)
+    lax.fori_loop(0, KILO, fill, 0, unroll=8)
     streams = [(H_OFF[s], H_UNIT[s], ORDERS[s]) for s in range(3)]
     sent = scatter_streams(me, acc, 512, recv, streams, send_sem.at[0], recv_sem.at[0])
     core = coord(me, "core")
@@ -236,23 +385,23 @@
     act, slope = gelu_parts(pre_ref[...])
     d_pre = (slope * nt_dot(dh, wout_ref[...])).astype(BF16)
     dw_out = tn_dot(act.astype(BF16), dh)
-    tiles[0:128] = dw_out.reshape(128, 8, 128)
+    tiles[0:LANE] = dw_out.reshape(LANE, 8, LANE)
     dw_in = tn_dot(x_ref[...], d_pre)
     for j in range(8):
-        tiles[128 + 32 * j : 160 + 32 * j] = dw_in[:, 128 * j : 128 * j + 128].reshape(32, 8, 128)
-    streams = [(64 * s, 1, ORDERS[s]) for s in range(3)]
+        tiles[LANE + 32 * j : 160 + 32 * j] = dw_in[:, LANE * j : LANE * j + LANE].reshape(32, 8, LANE)
+    streams = [(TOK * s, 1, ORDERS[s]) for s in range(3)]
     sent2 = scatter_streams(me, tiles, 192, trecv, streams, send_sem.at[1], recv_sem.at[1])
     for c in sent + sent2:
         c.wait_send()
     streams = []
     for s in range(3):
-        own = core * 192 + 64 * s + block_index(me, ORDERS[s])
+        own = core * 192 + TOK * s + block_index(me, ORDERS[s])
         whole[own] = tiles[own]
-        streams.append((whole, core * 192 + 64 * s, 1, ORDERS[s]))
+        streams.append((whole, core * 192 + TOK * s, 1, ORDERS[s]))
     sent = gather_streams(me, streams, [(whole, 192)], send_sem.at[2], recv_sem.at[2])
-    dwout_ref[...] = whole[0:128].reshape(1024, 128)
+    dwout_ref[...] = whole[0:LANE].reshape(KILO, LANE)
     for j in range(8):
-        dwin_ref[:, 128 * j : 128 * j + 128] = whole[128 + 32 * j : 160 + 32 * j].reshape(256, 128)
+        dwin_ref[:, LANE * j : LANE * j + LANE] = whole[LANE + 32 * j : 160 + 32 * j].reshape(WIDE, LANE)
     for c in sent:
         c.wait_send()
 
@@ -262,7 +411,7 @@
 
 
 def params(cid):
-    return pltpu.CompilerParams(collective_id=cid, has_side_effects=True, vmem_limit_bytes=48 * 1024 * 1024)
+    return pltpu.CompilerParams(collective_id=cid, has_side_effects=True, vmem_limit_bytes=48 * KILO * KILO)
 
 
 def dma(*shape):
@@ -277,61 +426,66 @@
         block_rows = table_blk.shape[0]
         cand_dev = cand_ids.shape[0] // num_dev
         tok_total = features.shape[0] * num_dev
-        tgt_row = jnp.pad(targets[None, :], ((0, 0), (0, 64)))
+        tgt_row = jnp.pad(targets[None, :], ((0, 0), (0, TOK)))
         h_all, tall, pre = pl.pallas_call(
             query_kernel,
-            out_shape=[jax.ShapeDtypeStruct((1024, 8, 128), BF16), jax.ShapeDtypeStruct((128, 1, 128), jnp.int32), jax.ShapeDtypeStruct((64, 1024), F32)],
+            out_shape=[jax.ShapeDtypeStruct((KILO, 8, LANE), BF16), jax.ShapeDtypeStruct((LANE, 1, LANE), jnp.int32), jax.ShapeDtypeStruct((TOK, KILO), F32)],
             in_specs=vmem(4), out_specs=vmem(3),
             scratch_shapes=[dma(4 * NPEER), dma(4 * NPEER)],
             compiler_params=params(0), name="query_gather",
         )(features, w_in, w_out, tgt_row)
-        query_all = h_all.reshape(8192, 128)
-        t5 = tall[:, 0, :64].reshape(2, 4, 4, 4, 64)
+        query_all = h_all.reshape(ALL, LANE)
+        t5 = tall[:, 0, :TOK].reshape(2, 4, 4, 4, TOK)
         tgt_all = jnp.concatenate([
             t5.transpose(0, 3, 1, 2, 4)[..., 0:24].reshape(2, -1),
             t5.transpose(0, 2, 3, 1, 4)[..., 24:48].reshape(2, -1),
-            t5[..., 48:64].reshape(2, -1)], axis=1).reshape(-1)
-        row_base = dev_index * block_rows
-        tgt_local = tgt_all - row_base
-        tgt_own = (tgt_local >= 0) & (tgt_local < block_rows)
-        tgt_index = jnp.clip(tgt_local, 0, block_rows - 1)
-        tgt_rows = table_blk[tgt_index]
+            t5[..., 48:TOK].reshape(2, -1)], axis=1).reshape(TOK, LANE)
         own_cands = lax.dynamic_slice_in_dim(cand_ids, dev_index * cand_dev, cand_dev)
         own_logq = lax.dynamic_slice_in_dim(log_q, dev_index * cand_dev, cand_dev)
-        cand_index = own_cands - row_base
+        cand_index = own_cands - dev_index * block_rows
         cand_rows = table_blk[cand_index]
-        tgt_dot = jnp.einsum("td,td->t", query_all, tgt_rows, preferred_element_type=F32)
-        z_own = jnp.where(tgt_own, tgt_dot, -jnp.inf)
-        cand_logit = jnp.einsum("td,cd->tc", query_all, cand_rows, preferred_element_type=F32) - own_logq[None, :]
-        cand_logit = jnp.where(own_cands[None, :] == tgt_all[:, None], -1e9, cand_logit)
-        top = jnp.max(cand_logit, axis=1)
-        part = jnp.sum(jnp.exp(cand_logit - top[:, None]), axis=1)
-        stats = jnp.stack([v.reshape(8, 8, 128) for v in (top, part, z_own)], axis=1)
+        steps = tok_total // TILE
+        whole = lambda *shape: pl.BlockSpec(shape, lambda i: (0,) * len(shape))
+        smem = pl.BlockSpec(memory_space=pltpu.SMEM)
+        e_spec = pl.BlockSpec((cand_dev, TILE), lambda i: (0, i))
+        st_spec = pl.BlockSpec((1, 3, 8, LANE), lambda i: (i, 0, 0, 0))
+        e, stats, pos, rows, toks, hc, tc = pl.pallas_call(
+            score_kernel, grid=(steps,),
+            out_shape=[
+                jax.ShapeDtypeStruct((cand_dev, tok_total), F32), jax.ShapeDtypeStruct((steps, 3, 8, LANE), F32),
+                jax.ShapeDtypeStruct((TOK, LANE), F32), jax.ShapeDtypeStruct((TOK, LANE), jnp.int32), jax.ShapeDtypeStruct((TOK, LANE), jnp.int32),
+                jax.ShapeDtypeStruct((tok_total, LANE), BF16), jax.ShapeDtypeStruct((tok_total, LANE), BF16)],
+            in_specs=[whole(tok_total, LANE), whole(block_rows, LANE), whole(cand_dev, LANE), whole(cand_dev, 1), whole(cand_dev, 1), whole(TOK, LANE)],
+            out_specs=[e_spec, st_spec, whole(TOK, LANE), whole(TOK, LANE), whole(TOK, LANE), whole(tok_total, LANE), whole(tok_total, LANE)],
+            scratch_shapes=[pltpu.VMEM((TOK, LANE), F32), pltpu.VMEM((cand_dev, LANE), jnp.int32), pltpu.VMEM((cand_dev, LANE), F32)],
+            compiler_params=pltpu.CompilerParams(dimension_semantics=("arbitrary",), vmem_limit_bytes=48 * KILO * KILO), name="score",
+        )(query_all, table_blk, cand_rows, own_cands[:, None], own_logq[:, None], tgt_all)
         norm = pl.pallas_call(
             stats_kernel,
-            out_shape=jax.ShapeDtypeStruct((2, 64, 128), F32),
+            out_shape=jax.ShapeDtypeStruct((2, TOK, LANE), F32),
             in_specs=vmem(1), out_specs=vmem(1)[0],
-            scratch_shapes=[pltpu.VMEM((80, 3, 8, 128), F32), pltpu.VMEM((32, 3, 8, 128), F32), dma(3 * NPEER), dma(3 * NPEER)],
+            scratch_shapes=[pltpu.VMEM((80, 3, 8, LANE), F32), pltpu.VMEM((32, 3, 8, LANE), F32), dma(3 * NPEER), dma(3 * NPEER)],
             compiler_params=params(1), name="stats_reduce",
         )(stats)
-        log_norm, tgt_logit = norm[0].reshape(8192), norm[1].reshape(8192)
-        loss = jnp.sum(log_norm - tgt_logit) / tok_total
-        grad_tgt = (jnp.exp(tgt_logit - log_norm) - 1.0) / tok_total
-        cand_grad = (jnp.exp(cand_logit - log_norm[:, None]) / tok_total).astype(BF16)
-        own_grad = jnp.where(tgt_own, grad_tgt, 0.0)
-        dq_part = own_grad[:, None] * tgt_rows + jnp.einsum("tc,cd->td", cand_grad, cand_rows, preferred_element_type=F32)
+        loss = jnp.sum(norm[0] - norm[1]) / tok_total
+        dq_part, grad_blk = pl.pallas_call(
+            assemble_kernel, grid=(steps,),
+            out_shape=[jax.ShapeDtypeStruct((tok_total, LANE), F32), jax.ShapeDtypeStruct((block_rows, LANE), F32)],
+            in_specs=[smem, smem, smem, e_spec, st_spec, whole(2, TOK, LANE), whole(tok_total, LANE), whole(cand_dev, LANE), whole(TOK, LANE), whole(tok_total, LANE), whole(tok_total, LANE)],
+            out_specs=[whole(tok_total, LANE), whole(block_rows, LANE)],
+            scratch_shapes=[pltpu.VMEM((cand_dev, LANE), F32), pltpu.VMEM((LANE, LANE), F32), pltpu.VMEM((LANE, LANE), F32), pltpu.VMEM((LANE, cand_dev), BF16)],
+            compiler_params=pltpu.CompilerParams(dimension_semantics=("arbitrary",), vmem_limit_bytes=48 * KILO * KILO), name="assemble",
+        )(cand_index, rows, toks, e, stats, norm, query_all, cand_rows, pos, hc, tc)
         grad_w_in, grad_w_out = pl.pallas_call(
             grad_kernel,
-            out_shape=[jax.ShapeDtypeStruct((256, 1024), F32), jax.ShapeDtypeStruct((1024, 128), F32)],
+            out_shape=[jax.ShapeDtypeStruct((WIDE, KILO), F32), jax.ShapeDtypeStruct((KILO, LANE), F32)],
             in_specs=vmem(4), out_specs=vmem(2),
             scratch_shapes=[
-                pltpu.VMEM((1024, 8, 128), F32), pltpu.VMEM((8 * 127 + 8, 8, 128), F32),
-                pltpu.VMEM((384, 8, 128), F32), pltpu.VMEM((3 * 127, 8, 128), F32), pltpu.VMEM((384, 8, 128), F32),
+                pltpu.VMEM((KILO, 8, LANE), F32), pltpu.VMEM((8 * 127 + 8, 8, LANE), F32),
+                pltpu.VMEM((384, 8, LANE), F32), pltpu.VMEM((3 * 127, 8, LANE), F32), pltpu.VMEM((384, 8, LANE), F32),
                 dma(3, 3 * NPEER), dma(3, 3 * NPEER)],
             compiler_params=params(2), name="grad_reduce",
-        )(dq_part.reshape(1024, 8, 128), features, w_out, pre)
-        grad_cand = jnp.einsum("tc,td->cd", cand_grad, query_all, preferred_element_type=F32)
-        grad_blk = jnp.zeros(table_blk.shape, F32).at[cand_index].add(grad_cand).at[tgt_index].add(own_grad[:, None] * query_all)
+        )(dq_part.reshape(KILO, 8, LANE), features, w_out, pre)
         return loss, grad_blk, grad_w_in, grad_w_out
 
     return jax.shard_map(local_step, mesh=mesh, in_specs=(P("dp", None), P(), P(), P("dp", None), P(), P(), P("dp")), out_specs=(P(), P("dp", None), P(), P()), check_vma=False)

time: 280 us -> 170 us (0.61)
  other arithmetic: 108 us -> 1.38 us
  Pallas kernels: 100 us -> 156 us
  local copies, waits for them, and re-layouts: 42.7 us -> 10.2 us
  matrix products: 25.3 us -> 0 us
    scatter-add x2 -> x0, other arithmetic: 72.8 us -> none  [local_step(): jnp.zeros(table_blk.shape, F32).at[cand_index].add(grad_cand).at[tgt_index]]
    pallas_call x3 -> x5, Pallas kernels: 100 us -> 156 us  [the longest x1 61.7 us: local_step(): pl.pallas_call(grad_kernel, out_shape=[jax.ShapeDtypeStruct((WIDE, KILO),...]
    gather x1 -> x0, local copies, waits for them, and re-layouts: 29.7 us -> none  [local_step(): tgt_rows = table_blk[tgt_index]]
    dot_general x3 -> x0, matrix products: 25.3 us -> none  [the longest x1 12.5 us: local_step(): jnp.einsum('td,cd->tc', query_all, cand_rows, preferred_element_type=F32)]
    convert_element_type x1 -> x0, other arithmetic: 15.4 us -> none  [local_step(): (jnp.exp(cand_logit - log_norm[:, None]) / tok_total).astype(BF16)]
    reduce_sum x1, other arithmetic: 14.9 us -> 0.61 us  [local_step(): loss = jnp.sum(norm[0] - norm[1]) / tok_total]
    dot_general x1 -> x0, other arithmetic: 3.52 us -> none  [local_step(): jnp.einsum('td,td->t', query_all, tgt_rows, preferred_element_type=F32)]
    unnamed x30 -> x16, local copies, waits for them, and re-layouts: 7.76 us -> 4.41 us
where the time goes in v2:
time: 170 us; the launch traced here: 171 us
  Pallas kernels  156 us (92%)
  local copies, waits for them, and re-layouts  10.2 us (6%)
  between operations  2.64 us (2%)
    pallas_call x1, Pallas kernels, local_step(): pl.pallas_call(grad_kernel, out_shape=[jax.ShapeDtypeStruct((WIDE, KILO),...  61.7 us
    pallas_call x1, Pallas kernels, local_step(): pl.pallas_call(score_kernel, grid=(steps,), out_shape=[jax.ShapeDtypeStru...  25.2 us
    pallas_call x1, Pallas kernels, local_step(): pl.pallas_call(query_kernel, out_shape=[jax.ShapeDtypeStruct((KILO, 8, LA...  24.1 us
    pallas_call x1, Pallas kernels, local_step(): pl.pallas_call(assemble_kernel, grid=(steps,), out_shape=[jax.ShapeDtypeS...  23.2 us
    pallas_call x1, Pallas kernels, local_step(): pl.pallas_call(stats_kernel, out_shape=jax.ShapeDtypeStruct((2, TOK, LANE...  22.3 us
    gather x1, local copies, waits for them, and re-layouts, local_step(): cand_rows = table_blk[cand_index]  4.75 us
    unnamed x16, local copies, waits for them, and re-layouts  4.41 us

profile of v2, /device:TPU:1, one launch (start us, length us, event | category | flops | bytes accessed | tf_op | source)
XLA Modules:
  0.0 170.7 jit_solution(9441905746862852643)
XLA Ops:
  0.6 0.0 copy-start.6
  0.6 0.0 copy-start.5
  0.7 0.0 copy-start.4
  0.7 0.0 copy-start.3
  0.7 0.8 fusion
  1.4 0.0 dynamic-slice-start
  1.4 4.8 %gather_fusion = bf16[1024,128]{1,0:T(8,128)(2,1)S(1)} fusion(bf16[8192,128]{1,0:T(8,128)(2,1)} %blk_ref.1, s32[1024]{0:T(1024)S(1)} %get-tuple-element.32), kind=kCustom, calls=%fused_computation | custom fusion | bytes 528384 | tf_op jit(solution)/shard_map/gather | solution.py:446
  6.2 0.2 copy.15.cid_ref
  6.4 0.0 copy-done.6
  6.5 0.0 copy-done.5
  6.5 0.0 copy-done.4
  6.5 0.0 copy-done.3
  6.5 24.1 %query_gather.1 = (bf16[1024,8,128]{2,1,0:T(8,128)(2,1)S(1)}, s32[128,1,128]{2,1,0:T(1,128)S(1)}, f32[64,1024]{1,0:T(8,128)S(1)}) custom-call(bf16[64,256]{1,0:T(8,128)(2,1)S(1)} %copy-done.5, bf16[256,1024]{1,0:T(8,128)(2,1)S(1)} %copy-done.4, bf16[1024,128]{1,0:T(8,128)(2,1)S(1)} %copy-done.3, s32[1,128]{1,0:T(1,128)S(1)} %pad.4.tgt_ref), custom_call_target="tpu_custom_call" | custom-call | tf_op jit(solution)/shard_map/query_gather/pallas_call | solution.py:430
  30.6 0.0 copy-start
  30.6 1.3 copy-done
  31.9 0.1 slice.27
  32.1 0.1 reshape.29
  32.2 0.1 reshape.28
  32.3 0.1 slice.28
  32.4 0.1 reshape.30
  32.6 0.0 dynamic-slice-done
  32.6 0.2 copy.16.logq_ref
  32.8 0.0 copy-start.1
  32.9 25.2 %score.1 = (f32[1024,8192]{1,0:T(8,128)}, f32[8,3,8,128]{3,2,1,0:T(8,128)S(1)}, f32[64,128]{1,0:T(8,128)S(1)}, s32[64,128]{1,0:T(8,128)S(1)}, s32[64,128]{1,0:T(...) custom-call(bf16[8192,128]{1,0:T(8,128)(2,1)} %bitcast.12, bf16[8192,128]{1,0:T(8,128)(2,1)} %blk_ref.1, ...), custom_call_target="tpu_custom_call" | custom-call | tf_op jit(solution)/shard_map/score/pallas_call | solution.py:452
  58.0 0.0 copy-start.2
  58.0 1.3 copy-done.2
  59.3 22.3 %stats_reduce.1.norm_ref = f32[2,64,128]{2,1,0:T(8,128)S(1)} custom-call(f32[8,3,8,128]{3,2,1,0:T(8,128)S(1)} %get-tuple-element.20.st_ref), custom_call_target="tpu_custom_call" | custom-call | tf_op jit(solution)/shard_map/stats_reduce/pallas_call | solution.py:463
  81.6 0.0 copy-done.1
  81.7 23.2 %assemble.1 = (f32[8192,128]{1,0:T(8,128)}, f32[8192,128]{1,0:T(8,128)}) custom-call(s32[1024]{0:T(1024)S(1)} %get-tuple-element.33.cidx_ref, s32[64,128]{1,0:T(8,128)S(1)} %get-tuple-element.21.row_ref, s32[64,128]{1,0:T(8,128)S(1)} %get-tuple-element.22.tok_ref, f32[1024,8192]{1,0:T(8,128)} %get-tuple-element.23.e_ref, ...), custom_call_target="tpu_custom_call" | custom-call | tf_op jit(solution)/shard_map/assemble/pallas_call | solution.py:471
  104.8 61.7 %grad_reduce.1 = (f32[256,1024]{1,0:T(8,128)S(1)}, f32[1024,128]{1,0:T(8,128)S(1)}) custom-call(f32[1024,8,128]{2,1,0:T(8,128)} %bitcast.17, bf16[64,256]{1,0:T(8,128)(2,1)S(1)} %copy-done.5, bf16[1024,128]{1,0:T(8,128)(2,1)S(1)} %copy-done.3, f32[64,1024]{1,0:T(8,128)S(1)} %get-tuple-element.29.pre_ref), custom_call_target="tpu_custom_call" | custom-call | tf_op jit(solution)/shard_map/grad_reduce/pallas_call | solution.py:479
  166.5 0.6 subtract_reduce_fusion
  167.8 1.0 copy.19
  168.7 0.8 copy.20
  (5 shorter events, 0.1 us)
Async XLA Ops:
  0.6 5.8 %copy-start.6 = (s32[64]{0:T(128)S(1)}, s32[64]{0:T(128)}, u32[]{:S(2)}) copy-start(s32[64]{0:T(128)} %param.13) | copy-start | bytes 772
  0.6 5.8 %copy-start.5 = (bf16[64,256]{1,0:T(8,128)(2,1)S(1)}, bf16[64,256]{1,0:T(8,128)(2,1)}, u32[]{:S(2)}) copy-start(bf16[64,256]{1,0:T(8,128)(2,1)} %x_ref.3) | copy-start | bytes 98308
  0.7 5.8 %copy-start.4 = (bf16[256,1024]{1,0:T(8,128)(2,1)S(1)}, bf16[256,1024]{1,0:T(8,128)(2,1)}, u32[]{:S(2)}) copy-start(bf16[256,1024]{1,0:T(8,128)(2,1)} %win_ref.1) | copy-start | bytes 1572868
  0.7 5.8 %copy-start.3 = (bf16[1024,128]{1,0:T(8,128)(2,1)S(1)}, bf16[1024,128]{1,0:T(8,128)(2,1)}, u32[]{:S(2)}) copy-start(bf16[1024,128]{1,0:T(8,128)(2,1)} %wout_ref.3) | copy-start | bytes 786436
  1.4 31.2 %dynamic-slice-start = ((f32[131072]{0:T(1024)}, s32[]{:T(128)}), f32[1024]{0:T(1024)S(1)}, s32[]{:S(2)}) async-start(f32[131072]{0:T(1024)} %param.12, s32[]{:T(128)} %select_n.7), calls=%async_computation | async-start | bytes 8704 | tf_op jit(solution)/shard_map/dynamic_slice | solution.py:444
  30.6 1.3 copy-start
  32.8 48.8 %copy-start.1 = (bf16[1024,8,128]{2,1,0:T(8,128)(2,1)S(1)}, bf16[1024,8,128]{2,1,0:T(8,128)(2,1)}, u32[]{:S(2)}) copy-start(bf16[1024,8,128]{2,1,0:T(8,128)(2,1)} %copy-done) | copy-start | bytes 6291460
  58.0 1.3 copy-start.2

commit v3 on v1

v3 whole, which is shorter than its diff:
```python
import functools
import jax
import jax.numpy as jnp
from jax import lax
from jax.experimental import pallas as pl
from jax.experimental.pallas import tpu as pltpu
from jax.sharding import PartitionSpec as P

MESH = pl.DeviceIdType.MESH
F32, BF16 = jnp.float32, jnp.bfloat16
COORD = {"core": (1, 2), "x": (2, 4), "y": (8, 4), "z": (32, 4)}
ORDERS = (("x", "y", "z"), ("y", "z", "x"), ("z", "x", "y"))
NDEV = 128
NPEER = 10
LANE, TOK, ALL, KILO, WIDE = 128, 64, 8192, 1024, 256


def one(i):
    return pl.ds(i, 1)


def coord(me, axis):
    stride, radix = COORD[axis]
    return (me // stride) % radix


def peer(me, axis, k):
    stride, radix = COORD[axis]
    c = coord(me, axis)
    return me + ((c + k) % radix - c) * stride


def block_index(me, order):
    idx, weight = 0, 1
    for axis in order:
        idx = idx + coord(me, axis) * weight
        weight *= COORD[axis][1]
    return idx


def entry_barrier(me):
    barrier = pltpu.get_barrier_semaphore()
    for axis in COORD:
        for k in range(1, COORD[axis][1]):
            pl.semaphore_signal(barrier, inc=1, device_id=(peer(me, axis, k),), device_id_type=MESH)
    pl.semaphore_wait(barrier, NPEER)


def remote(src, dst, send, recv, dev):
    return pltpu.make_async_remote_copy(src_ref=src, dst_ref=dst, send_sem=send, recv_sem=recv, device_id=(dev,), device_id_type=MESH)


def gather_streams(me, streams, bulk, send_sem, recv_sem):
    pending, sent = [None] * len(streams), []
    for phase in range(4):
        for s, (ref, off, unit, order) in enumerate(streams):
            if pending[s]:
                for c in pending[s]:
                    c.wait_recv()
            if phase == 3:
                continue
            span = 4 ** phase
            idx = block_index(me, order)
            where = ref.at[pl.ds(off + (idx - idx % span) * unit, span * unit)]
            pending[s] = []
            for k in range(1, 4):
                n = s * 9 + phase * 3 + k - 1
                c = remote(where, where, send_sem.at[n], recv_sem.at[n], peer(me, order[phase], k))
                c.start()
                pending[s].append(c)
                sent.append(c)
    last = []
    for i, (ref, count) in enumerate(bulk):
        n = len(streams) * 9 + i
        where = ref.at[pl.ds(coord(me, "core") * count, count)]
        c = remote(where, where, send_sem.at[n], recv_sem.at[n], peer(me, "core", 1))
        c.start()
        last.append(c)
    for c in last:
        c.wait_recv()
    return sent + last


def add_rows(ref, start, rref, base, count, parts):
    def add(i, carry):
        acc = ref[start + i]
        for k in range(parts):
            acc = acc + rref[base + k * count + i]
        ref[start + i] = acc
        return carry

    lax.fori_loop(0, count, add, 0, unroll=4)


def scatter_streams(me, ref, first, rref, rbase, streams, send_sem, recv_sem, between):
    sent = []
    pending = [None] * 3
    for step in range(4):
        for s, (off, unit, order) in enumerate(streams):
            idx = block_index(me, order)
            if pending[s]:
                for c in pending[s][0]:
                    c.wait_recv()
                add_rows(ref, pending[s][1], rref, pending[s][2], pending[s][3], 3)
            if step == 3:
                continue
            span = 4 ** (2 - step)
            axis = order[2 - step]
            start = first + off + (idx - idx % (4 * span)) * unit
            d = coord(me, axis)
            copies = []
            for k in range(1, 4):
                n = s * 9 + step * 3 + k - 1
                src = ref.at[pl.ds(start + (d + k) % 4 * span * unit, span * unit)]
                dst = rref.at[pl.ds(rbase + (k - 1) * span * unit, span * unit)]
                c = remote(src, dst, send_sem.at[n], recv_sem.at[n], peer(me, axis, k))
                c.start()
                copies.append(c)
            sent += copies
            pending[s] = (copies, start + d * span * unit, rbase, span * unit)
            rbase += 3 * span * unit
        if step == 0:
            between()
    return sent


def gelu_parts(a):
    c = 0.7978845608028654
    inner = jnp.tanh(c * (a + 0.044715 * (a * a * a)))
    half = 0.5 * (1.0 + inner)
    return a * half, half + 0.5 * a * (1.0 - inner * inner) * (c * (1.0 + 3.0 * 0.044715 * (a * a)))


def nt_dot(a, b):
    return lax.dot_general(a, b, (((1,), (1,)), ((), ())), preferred_element_type=F32)


def tn_dot(a, b):
    return lax.dot_general(a, b, (((0,), (0,)), ((), ())), preferred_element_type=F32)


H_OFF = (0, 192, 384)
H_UNIT = (3, 3, 2)
H_FIRST = (0, 3, 6)


def query_kernel(x_ref, win_ref, wout_ref, tgt_ref, h_ref, tall_ref, pre_ref, send_sem, recv_sem):
    me = lax.axis_index("dp")
    entry_barrier(me)
    pre = jnp.dot(x_ref[...], win_ref[...], preferred_element_type=F32)
    pre_ref[...] = pre
    act = gelu_parts(pre)[0].astype(BF16)
    query = jnp.dot(act, wout_ref[...], preferred_element_type=F32)
    core = coord(me, "core")
    streams = []
    for s in range(3):
        idx = block_index(me, ORDERS[s])
        for g in range(H_UNIT[s]):
            row = 8 * (H_FIRST[s] + g)
            h_ref[core * 512 + H_OFF[s] + idx * H_UNIT[s] + g] = query[row : row + 8, :].astype(BF16)
        streams.append((h_ref, core * 512 + H_OFF[s], H_UNIT[s], ORDERS[s]))
    tall_ref[core * TOK + block_index(me, ORDERS[2])] = tgt_ref[...]
    streams.append((tall_ref, core * TOK, 1, ORDERS[2]))
    for c in gather_streams(me, streams, [(h_ref, 512), (tall_ref, TOK)], send_sem, recv_sem):
        c.wait_send()


def reduce_stats(me, st_ref, recv, cur, send_sem, recv_sem):
    sent = []
    pending = [None] * 3
    for phase in range(5):
        for s in range(3):
            g0, ng = H_FIRST[s], H_UNIT[s]
            if phase:
                for c in pending[s]:
                    c.wait_recv()
                base = 8 * (0, 3, 6, 9)[phase - 1]
                npart = len(pending[s])

                def merge(g, carry, phase=phase, base=base, npart=npart):
                    old = st_ref[g] if phase == 1 else cur[8 * (phase - 2) + g]
                    parts = [recv[base + 8 * k + g] for k in range(npart)]
                    top, z = old[0], old[2]
                    for p in parts:
                        top = jnp.maximum(top, p[0])
                        z = jnp.maximum(z, p[2])
                    total = old[1] * jnp.exp(old[0] - top)
                    for p in parts:
                        total = total + p[1] * jnp.exp(p[0] - top)
                    row = 8 * (phase - 1) + g
                    cur[row, 0] = top
                    cur[row, 1] = total
                    cur[row, 2] = z
                    return carry

                lax.fori_loop(g0, g0 + ng, merge, 0)
            if phase == 4:
                continue
            axis = (ORDERS[s] + ("core",))[phase]
            src = st_ref.at[pl.ds(g0, ng)] if phase == 0 else cur.at[pl.ds(8 * (phase - 1) + g0, ng)]
            base = 8 * (0, 3, 6, 9)[phase]
            pending[s] = []
            for k in range(1, COORD[axis][1]):
                n = s * NPEER + phase * 3 + k - 1
                c = remote(src, recv.at[pl.ds(base + 8 * (k - 1) + g0, ng)], send_sem.at[n], recv_sem.at[n], peer(me, axis, k))
                c.start()
                pending[s].append(c)
                sent.append(c)
    return sent


TILE = KILO


def score_kernel(h_ref, blk_ref, cand_ref, cid_ref, logq_ref, tgt_ref, e_ref, mc_ref, st_ref, pos_ref, row_ref, hc_ref, te_ref, zd, cidb, logqb, part):
    step = pl.program_id(0)
    block_rows = blk_ref.shape[0]
    base = lax.axis_index("dp") * block_rows

    @pl.when(step == 0)
    def _():
        cidb[...] = jnp.broadcast_to(cid_ref[...], cidb.shape)
        logqb[...] = jnp.broadcast_to(logq_ref[...], logqb.shape)
        local = tgt_ref[...] - base
        own = (local >= 0) & (local < block_rows)
        own_f = jnp.where(own, 1.0, 0.0)
        own_b = own_f.astype(BF16)
        up = lax.broadcasted_iota(jnp.int32, (LANE, LANE), 0) < lax.broadcasted_iota(jnp.int32, (LANE, LANE), 1)
        prefix = jnp.dot(own_b, jnp.where(up, 1.0, 0.0).astype(BF16), preferred_element_type=F32)
        total = jnp.dot(own_b, jnp.ones((LANE, LANE), BF16), preferred_element_type=F32)
        low = lax.broadcasted_iota(jnp.int32, (TOK, TOK), 0) > lax.broadcasted_iota(jnp.int32, (TOK, TOK), 1)
        offset = jnp.dot(jnp.where(low, 1.0, 0.0).astype(BF16), total.astype(BF16), preferred_element_type=F32)
        pos_ref[...] = jnp.where(own, prefix + offset, -1.0)
        zd[...] = jnp.zeros_like(zd)
        te_ref[...] = jnp.zeros_like(te_ref)
        chunks = (jnp.sum(own_f).astype(jnp.int32) + 127) // LANE
        slot0 = lax.broadcasted_iota(jnp.int32, (LANE, LANE), 0).astype(F32)
        lane = lax.broadcasted_iota(jnp.int32, (1, LANE), 1)

        def chunk(c, carry):
            slot = slot0 + (c * LANE).astype(F32)

            def collect(i, acc):
                hsum, code = acc
                picks = []
                for u in range(8):
                    r = i * 8 + u
                    hit = pos_ref[one(r), :] == slot
                    code = code + jnp.where(hit, tgt_ref[one(r), :] - base, 0)
                    picks.append(jnp.where(hit, 1.0, 0.0).astype(BF16))
                pick = jnp.concatenate(picks, axis=1)
                tok = pl.ds(pl.multiple_of(i * KILO, KILO), KILO)
                return hsum + jnp.dot(pick, h_ref[tok, :], preferred_element_type=F32), code

            hsum, code = lax.fori_loop(0, 8, collect, (jnp.zeros((LANE, LANE), F32), jnp.zeros((LANE, LANE), jnp.int32)))
            rowb = jnp.broadcast_to(jnp.sum(code.astype(F32), axis=1, keepdims=True), (LANE, LANE))
            row_ref[one(c), :] = jnp.transpose(rowb)[0:1, :].astype(jnp.int32)

            def fetch(i, acc):
                picks = []
                for u in range(8):
                    hit = rowb == (lane + (i * 8 + u) * LANE).astype(F32)
                    picks.append(jnp.where(hit, 1.0, 0.0).astype(BF16))
                rows = pl.ds(pl.multiple_of(i * KILO, KILO), KILO)
                return acc + jnp.dot(jnp.concatenate(picks, axis=1), blk_ref[rows, :], preferred_element_type=F32)

            tsum = lax.fori_loop(0, block_rows // KILO, fetch, jnp.zeros((LANE, LANE), F32))
            hc_ref[pl.ds(c * LANE, LANE), :] = hsum.astype(BF16)
            z = jnp.transpose(jnp.broadcast_to(jnp.sum(hsum * tsum, axis=1, keepdims=True) / WIDE, (LANE, LANE)))[0:8, :]
            hi = z.astype(BF16).astype(F32)
            mid = (z - hi).astype(BF16).astype(F32)
            parts = jnp.concatenate([jnp.transpose(tsum), hi, mid, z - hi - mid], axis=0).astype(BF16)

            def spread(i, carry2):
                picks = []
                for u in range(4):
                    hit = pos_ref[one(i * 4 + u), :] == slot
                    picks.append(jnp.where(hit, 1.0, 0.0).astype(BF16))
                got = jnp.dot(parts, jnp.concatenate(picks, axis=1), preferred_element_type=F32)
                te_ref[i] = (te_ref[i].astype(F32) + got[0:LANE, :]).astype(BF16)
                zrow = (got[LANE : LANE + 1, :] + got[LANE + 8 : LANE + 9, :] + got[LANE + 16 : LANE + 17, :]) * WIDE
                for u in range(4):
                    zd[one(i * 4 + u), :] += zrow[:, LANE * u : LANE * u + LANE]
                return carry2

            lax.fori_loop(0, 16, spread, 0)
            return carry

        lax.fori_loop(0, chunks, chunk, 0)

    for j in range(4):
        col = pl.multiple_of(step * TILE + WIDE * j, WIDE)
        dots = nt_dot(cand_ref[...], h_ref[pl.ds(col, WIDE), :])
        for half in range(2):
            q = 2 * j + half
            cols = slice(LANE * (q % 4), LANE * (q % 4) + LANE)
            tgt = tgt_ref[one(step * 8 + q), :]
            for c in range(8):
                rows = slice(LANE * c, LANE * c + LANE)
                s = dots[rows, LANE * half : LANE * half + LANE] - logqb[rows, :]
                s = jnp.where(cidb[rows, :] == tgt, -1e9, s)
                m = jnp.max(s, axis=0, keepdims=True)
                e = jnp.exp(s - m)
                e_ref[q // 4, rows, cols] = e
                mc_ref[q, c : c + 1, :] = m
                part[q, c : c + 1, :] = jnp.sum(e, axis=0, keepdims=True)
            top = jnp.max(mc_ref[q], axis=0, keepdims=True)
            st_ref[0, 0, q : q + 1, :] = top
            st_ref[0, 1, q : q + 1, :] = jnp.sum(part[q] * jnp.exp(mc_ref[q] - top), axis=0, keepdims=True)
    grp = pl.ds(pl.multiple_of(step * 8, 8), 8)
    st_ref[0, 2] = jnp.where(pos_ref[grp, :] >= 0.0, zd[grp, :], -jnp.inf)


def table_kernel(cidx_ref, row_ref, g_ref, dcand_ref, pos_ref, hc_ref, de_ref, gh):
    def clear(i, carry):
        de_ref[pl.ds(pl.multiple_of(i * TOK, TOK), TOK), :] = jnp.zeros((TOK, LANE), F32)
        return carry

    lax.fori_loop(0, de_ref.shape[0] // TOK, clear, 0)

    def place(i, carry):
        for u in range(8):
            de_ref[one(cidx_ref[i * 8 + u]), :] = dcand_ref[one(i * 8 + u), :]
        return carry

    lax.fori_loop(0, dcand_ref.shape[0] // 8, place, 0)
    count = jnp.sum(jnp.where(pos_ref[...] >= 0.0, 1.0, 0.0)).astype(jnp.int32)
    slot0 = lax.broadcasted_iota(jnp.int32, (LANE, LANE), 0).astype(F32)

    def chunk(c, carry):
        slot = slot0 + (c * LANE).astype(F32)

        def collect(r, acc):
            return acc + jnp.where(pos_ref[one(r), :] == slot, g_ref[one(r), :], 0.0)

        g = jnp.sum(lax.fori_loop(0, 64, collect, jnp.zeros((LANE, LANE), F32), unroll=8), axis=1, keepdims=True)
        gh[...] = g * hc_ref[pl.ds(c * LANE, LANE), :].astype(F32)

        def put(i, carry2):
            de_ref[one(row_ref[c, i]), :] += gh[one(i), :]
            return carry2

        lax.fori_loop(0, jnp.minimum(count - c * LANE, LANE), put, 0)
        return carry

    lax.fori_loop(0, (count + 127) // LANE, chunk, 0)


LAST = 27
PART = 512


def core_exchange(me, ref, half, rref, send, recv):
    mine = coord(me, "core")
    c = remote(ref.at[pl.ds((1 - mine) * half, half)], rref.at[pl.ds(0, half)], send, recv, peer(me, "core", 1))
    c.start()
    c.wait_recv()
    add_rows(ref, mine * half, rref, 0, half, 1)
    return [c]


def grad_kernel(e_ref, mc_ref, st_ref, te_ref, h_ref, candt_ref, x_ref, wout_ref, pre_ref, dwin_ref, dwout_ref, g_ref, loss_ref, dcand_ref,
                ebuf, srecv, cur, norm, acc, recv, tiles, trecv, whole, e_sem, core_send, core_recv, send_sem, recv_sem):
    me = lax.axis_index("dp")
    core = coord(me, "core")
    entry_barrier(me)

    def load(i):
        return pltpu.make_async_copy(e_ref.at[i], ebuf.at[i], e_sem.at[i])

    def load_start(i, carry):
        load(i).start()
        return carry

    lax.fori_loop(0, 16, load_start, 0)
    sent = reduce_stats(me, st_ref, srecv, cur, send_sem.at[3], recv_sem.at[3])
    total = jnp.zeros((8, LANE), F32)
    for g in range(8):
        m, t, z = cur[24 + g, 0], cur[24 + g, 1], cur[24 + g, 2]
        top = jnp.maximum(m, z)
        log_norm = top + jnp.log(t * jnp.exp(m - top) + jnp.exp(z - top))
        total = total + (log_norm - z)
        norm[8 * g : 8 * g + 8, :] = log_norm
        g_ref[8 * g : 8 * g + 8, :] = (jnp.exp(z - log_norm) - 1.0) / ALL
    loss_ref[...] = jnp.broadcast_to(jnp.sum(total, keepdims=True) / ALL, loss_ref.shape)

    def probs(t):
        blocks = []
        for q in range(4):
            r = t * 4 + q
            scale = jnp.exp(mc_ref[r] - norm[one(r), :]) / ALL
            blocks.append(jnp.concatenate([
                (ebuf[t, LANE * c : LANE * c + LANE, LANE * q : LANE * q + LANE] * scale[c : c + 1, :]).astype(BF16) for c in range(8)], axis=0))
        return jnp.concatenate(blocks, axis=1)

    def query_grad(t):
        dqt = jnp.dot(candt_ref[...], probs(t), preferred_element_type=F32)
        grow = jnp.concatenate([g_ref[one(t * 4 + q), :] for q in range(4)], axis=1)
        dqt = dqt + grow * te_ref[t].astype(F32)
        return jnp.transpose(dqt).reshape(TOK, 8, LANE)

    def swap(i):
        return remote(acc.at[pl.ds(((1 - core) * 8 + i) * TOK, TOK)], recv.at[pl.ds(i * TOK, TOK)], core_send.at[i], core_recv.at[i], peer(me, "core", 1))

    def give(i, carry):
        t = (1 - core) * 8 + i
        load(t).wait()
        acc[pl.ds(t * TOK, TOK)] = query_grad(t)
        swap(i).start()
        return carry

    def keep(i, carry):
        t = core * 8 + i
        load(t).wait()
        val = query_grad(t)
        swap(i).wait_recv()
        acc[pl.ds(t * TOK, TOK)] = val + recv[pl.ds(i * TOK, TOK)]
        return carry

    lax.fori_loop(0, 8, give, 0)
    lax.fori_loop(0, 8, keep, 0)

    def cand_grad():
        dcand_ref[...] = jnp.zeros_like(dcand_ref)

        def accumulate(t, carry):
            dcand_ref[...] += jnp.dot(probs(t), h_ref[pl.ds(pl.multiple_of(t * PART, PART), PART), :], preferred_element_type=F32)
            return carry

        lax.fori_loop(0, 16, accumulate, 0)

    streams = [(H_OFF[s], H_UNIT[s], ORDERS[s]) for s in range(3)]
    sent += scatter_streams(me, acc, core * 512, recv, 512, streams, send_sem.at[0], recv_sem.at[0], cand_grad)
    rows = []
    for s in range(3):
        idx = block_index(me, ORDERS[s])
        for g in range(H_UNIT[s]):
            rows.append(acc[core * 512 + H_OFF[s] + idx * H_UNIT[s] + g])
    dh = jnp.concatenate(rows, axis=0).astype(BF16)
    act, slope = gelu_parts(pre_ref[...])
    d_pre = (slope * nt_dot(dh, wout_ref[...])).astype(BF16)
    dw_out = tn_dot(act.astype(BF16), dh)
    tiles[0:LANE] = dw_out.reshape(LANE, 8, LANE)
    dw_in = tn_dot(x_ref[...], d_pre)
    for j in range(8):
        tiles[LANE + 32 * j : 160 + 32 * j] = dw_in[:, LANE * j : LANE * j + LANE].reshape(32, 8, LANE)
    streams = [(TOK * s, 1, ORDERS[s]) for s in range(3)]
    half = core_exchange(me, tiles, 192, trecv, send_sem.at[1, LAST], recv_sem.at[1, LAST])
    sent += half + scatter_streams(me, tiles, core * 192, trecv, 192, streams, send_sem.at[1], recv_sem.at[1], lambda: None)
    streams = []
    for s in range(3):
        own = core * 192 + TOK * s + block_index(me, ORDERS[s])
        whole[own] = tiles[own]
        streams.append((whole, core * 192 + TOK * s, 1, ORDERS[s]))
    sent += gather_streams(me, streams, [(whole, 192)], send_sem.at[2], recv_sem.at[2])
    dwout_ref[...] = whole[0:LANE].reshape(KILO, LANE)
    for j in range(8):
        dwin_ref[:, LANE * j : LANE * j + LANE] = whole[LANE + 32 * j : 160 + 32 * j].reshape(WIDE, LANE)
    for c in sent:
        c.wait_send()

    def swap_done(i, carry):
        swap(i).wait_send()
        return carry

    lax.fori_loop(0, 8, swap_done, 0)


def vmem(n):
    return [pl.BlockSpec(memory_space=pltpu.VMEM)] * n


def params(cid):
    return pltpu.CompilerParams(collective_id=cid, has_side_effects=True, vmem_limit_bytes=63 * KILO * KILO)


def dma(*shape):
    return pltpu.SemaphoreType.DMA(shape)


def solution(mesh):
    num_dev = mesh.shape["dp"]

    def local_step(features, w_in, w_out, table_blk, cand_ids, log_q, targets):
        dev_index = lax.axis_index("dp")
        block_rows = table_blk.shape[0]
        cand_dev = cand_ids.shape[0] // num_dev
        tok_total = features.shape[0] * num_dev
        tgt_row = jnp.pad(targets[None, :], ((0, 0), (0, TOK)))
        h_all, tall, pre = pl.pallas_call(
            query_kernel,
            out_shape=[jax.ShapeDtypeStruct((KILO, 8, LANE), BF16), jax.ShapeDtypeStruct((LANE, 1, LANE), jnp.int32), jax.ShapeDtypeStruct((TOK, KILO), F32)],
            in_specs=vmem(4), out_specs=vmem(3),
            scratch_shapes=[dma(4 * NPEER), dma(4 * NPEER)],
            compiler_params=params(0), name="query_gather",
        )(features, w_in, w_out, tgt_row)
        query_all = h_all.reshape(ALL, LANE)
        t5 = tall[:, 0, :TOK].reshape(2, 4, 4, 4, TOK)
        tgt_all = jnp.concatenate([
            t5.transpose(0, 3, 1, 2, 4)[..., 0:24].reshape(2, -1),
            t5.transpose(0, 2, 3, 1, 4)[..., 24:48].reshape(2, -1),
            t5[..., 48:TOK].reshape(2, -1)], axis=1).reshape(TOK, LANE)
        own_cands = lax.dynamic_slice_in_dim(cand_ids, dev_index * cand_dev, cand_dev)
        own_logq = lax.dynamic_slice_in_dim(log_q, dev_index * cand_dev, cand_dev)
        cand_index = own_cands - dev_index * block_rows
        cand_rows = table_blk[cand_index]
        steps = tok_total // TILE
        whole = lambda *shape: pl.BlockSpec(shape, lambda i: (0,) * len(shape))
        smem = pl.BlockSpec(memory_space=pltpu.SMEM)
        e, mc, stats, pos, rows, hc, te = pl.pallas_call(
            score_kernel, grid=(steps,),
            out_shape=[
                jax.ShapeDtypeStruct((16, cand_dev, PART), F32), jax.ShapeDtypeStruct((TOK, 8, LANE), F32), jax.ShapeDtypeStruct((steps, 3, 8, LANE), F32),
                jax.ShapeDtypeStruct((TOK, LANE), F32), jax.ShapeDtypeStruct((TOK, LANE), jnp.int32),
                jax.ShapeDtypeStruct((tok_total, LANE), BF16), jax.ShapeDtypeStruct((16, LANE, PART), BF16)],
            in_specs=[whole(tok_total, LANE), whole(block_rows, LANE), whole(cand_dev, LANE), whole(cand_dev, 1), whole(cand_dev, 1), whole(TOK, LANE)],
            out_specs=[
                pl.BlockSpec((2, cand_dev, PART), lambda i: (i, 0, 0)), pl.BlockSpec((8, 8, LANE), lambda i: (i, 0, 0)),
                pl.BlockSpec((1, 3, 8, LANE), lambda i: (i, 0, 0, 0)), whole(TOK, LANE), whole(TOK, LANE), whole(tok_total, LANE), whole(16, LANE, PART)],
            scratch_shapes=[pltpu.VMEM((TOK, LANE), F32), pltpu.VMEM((cand_dev, LANE), jnp.int32), pltpu.VMEM((cand_dev, LANE), F32), pltpu.VMEM((8, 8, LANE), F32)],
            compiler_params=pltpu.CompilerParams(dimension_semantics=("arbitrary",), vmem_limit_bytes=48 * KILO * KILO), name="score",
        )(query_all, table_blk, cand_rows, own_cands[:, None], own_logq[:, None], tgt_all)
        grad_w_in, grad_w_out, grad_tgt, loss, dcand = pl.pallas_call(
            grad_kernel,
            out_shape=[
                jax.ShapeDtypeStruct((WIDE, KILO), F32), jax.ShapeDtypeStruct((KILO, LANE), F32), jax.ShapeDtypeStruct((TOK, LANE), F32),
                jax.ShapeDtypeStruct((8, LANE), F32), jax.ShapeDtypeStruct((cand_dev, LANE), F32)],
            in_specs=[pl.BlockSpec(memory_space=pl.ANY)] + vmem(8), out_specs=vmem(5),
            scratch_shapes=[
                pltpu.VMEM((16, cand_dev, PART), F32), pltpu.VMEM((80, 3, 8, LANE), F32), pltpu.VMEM((32, 3, 8, LANE), F32), pltpu.VMEM((TOK, LANE), F32),
                pltpu.VMEM((KILO, 8, LANE), F32), pltpu.VMEM((KILO, 8, LANE), F32),
                pltpu.VMEM((384, 8, LANE), F32), pltpu.VMEM((384, 8, LANE), F32), pltpu.VMEM((384, 8, LANE), F32),
                dma(16), dma(8), dma(8), dma(4, 3 * NPEER), dma(4, 3 * NPEER)],
            compiler_params=params(1), name="grad_reduce",
        )(e, mc, stats, te, query_all, cand_rows.T, features, w_out, pre)
        grad_blk = pl.pallas_call(
            table_kernel,
            out_shape=jax.ShapeDtypeStruct((block_rows, LANE), F32),
            in_specs=[smem, smem] + vmem(4), out_specs=vmem(1)[0],
            scratch_shapes=[pltpu.VMEM((LANE, LANE), F32)],
            compiler_params=pltpu.CompilerParams(vmem_limit_bytes=48 * KILO * KILO), name="table_grad",
        )(cand_index, rows, grad_tgt, dcand, pos, hc)
        loss = loss[0, 0]
        return loss, grad_blk, grad_w_in, grad_w_out

    return jax.shard_map(local_step, mesh=mesh, in_specs=(P("dp", None), P(), P(), P("dp", None), P(), P(), P("dp")), out_specs=(P(), P("dp", None), P(), P()), check_vma=False)
```

time: 280 us -> 169 us (0.60)
  other arithmetic: 108 us -> 0.7 us
  Pallas kernels: 100 us -> 144 us
  matrix products: 25.3 us -> 0 us
  local copies, waits for them, and re-layouts: 42.7 us -> 22.9 us
    scatter-add x2 -> x0, other arithmetic: 72.8 us -> none  [local_step(): jnp.zeros(table_blk.shape, F32).at[cand_index].add(grad_cand).at[tgt_index]]
    pallas_call x3 -> x4, Pallas kernels: 100 us -> 144 us  [the longest x1 84.9 us: local_step(): pl.pallas_call(grad_kernel, out_shape=[jax.ShapeDtypeStruct((WIDE, KILO),...]
    gather x1 -> x0, local copies, waits for them, and re-layouts: 29.7 us -> none  [local_step(): tgt_rows = table_blk[tgt_index]]
    dot_general x3 -> x0, matrix products: 25.3 us -> none  [the longest x1 12.5 us: local_step(): jnp.einsum('td,cd->tc', query_all, cand_rows, preferred_element_type=F32)]
    convert_element_type x1 -> x0, other arithmetic: 15.4 us -> none  [local_step(): (jnp.exp(cand_logit - log_norm[:, None]) / tok_total).astype(BF16)]
    reduce_sum x1 -> x0, other arithmetic: 14.9 us -> none  [local_step(): part = jnp.sum(jnp.exp(cand_logit - top[:, None]), axis=1)]
    dot_general x1 -> x0, other arithmetic: 3.52 us -> none  [local_step(): jnp.einsum('td,td->t', query_all, tgt_rows, preferred_element_type=F32)]
    slice x1 -> x3, local copies, waits for them, and re-layouts: 0.09 us -> 2.98 us  [the longest x1 1.19 us: local_step(): loss = loss[0, 0]]
where the time goes in v3:
time: 169 us; the launch traced here: 168 us
  Pallas kernels  144 us (85%)
  local copies, waits for them, and re-layouts  22.9 us (14%)
    pallas_call x1, Pallas kernels, local_step(): pl.pallas_call(grad_kernel, out_shape=[jax.ShapeDtypeStruct((WIDE, KILO),...  84.9 us
    pallas_call x1, Pallas kernels, local_step(): pl.pallas_call(query_kernel, out_shape=[jax.ShapeDtypeStruct((KILO, 8, LA...  26.6 us
    pallas_call x1, Pallas kernels, local_step(): pl.pallas_call(score_kernel, grid=(steps,), out_shape=[jax.ShapeDtypeStru...  25.4 us
    unnamed x22, local copies, waits for them, and re-layouts  10.6 us
    pallas_call x1, Pallas kernels, local_step(): pl.pallas_call(table_kernel, out_shape=jax.ShapeDtypeStruct((block_rows,...  6.69 us
    gather x2, local copies, waits for them, and re-layouts, local_step(): cand_rows = table_blk[cand_index]  5.59 us

profile of v3, /device:TPU:1, one launch (start us, length us, event | category | flops | bytes accessed | tf_op | source)
XLA Modules:
  0.0 167.9 jit_solution(18077165131366584858)
XLA Ops:
  0.6 0.0 dynamic-slice-start
  0.6 1.2 pad.4.tgt_ref
  1.8 0.7 fusion
  2.5 4.7 %gather_fusion = bf16[1024,128]{1,0:T(8,128)(2,1)S(1)} fusion(bf16[8192,128]{1,0:T(8,128)(2,1)} %blk_ref.1, s32[1024]{0:T(1024)S(1)} %get-tuple-element.34), kind=kCustom, calls=%fused_computation | custom fusion | bytes 528384 | tf_op jit(solution)/shard_map/gather | solution.py:506
  7.3 0.8 copy.18
  8.1 0.0 dynamic-slice-done
  8.1 0.2 copy.17.logq_ref
  8.3 1.0 copy.16.cid_ref
  9.4 26.6 %query_gather.1 = (bf16[1024,8,128]{2,1,0:T(8,128)(2,1)}, s32[128,1,128]{2,1,0:T(1,128)}, f32[64,1024]{1,0:T(8,128)}) custom-call(bf16[64,256]{1,0:T(8,128)(2,1)} %x_ref.3, bf16[256,1024]{1,0:T(8,128)(2,1)} %win_ref.1, bf16[1024,128]{1,0:T(8,128)(2,1)} %wout_ref.3, s32[1,128]{1,0:T(1,128)} %pad.4.tgt_ref), custom_call_target="tpu_custom_call" | custom-call | tf_op jit(solution)/shard_map/query_gather/pallas_call | solution.py:490
  36.0 0.9 slice.24
  36.9 0.1 reshape.26
  37.0 0.9 copy.14
  37.9 0.1 reshape.24
  38.0 0.9 slice.23
  39.0 0.1 reshape.25
  39.1 0.0 copy-start.3
  39.2 1.0 copy-done.3
  40.2 25.4 %score.1 = (f32[16,1024,512]{2,1,0:T(8,128)}, f32[64,8,128]{2,1,0:T(8,128)S(1)}, f32[8,3,8,128]{3,2,1,0:T(8,128)S(1)}, f32[64,128]{1,0:T(8,128)S(1)}, s32[64,128...) custom-call(bf16[8192,128]{1,0:T(8,128)(2,1)} %bitcast.13, ...), custom_call_target="tpu_custom_call" | custom-call | tf_op jit(solution)/shard_map/score/pallas_call | solution.py:510
  65.6 0.0 copy-start
  65.6 1.3 copy-done
  66.9 0.0 copy-start.2
  66.9 1.3 copy-done.2
  68.2 0.0 copy-start.5
  68.2 0.7 copy-done.5
  68.9 0.0 copy-start.6
  68.9 0.6 copy-done.6
  69.6 84.9 %grad_reduce.1 = (f32[256,1024]{1,0:T(8,128)}, f32[1024,128]{1,0:T(8,128)}, f32[64,128]{1,0:T(8,128)}, f32[8,128]{1,0:T(8,128)}, f32[1024,128]{1,0:T(8,128)}) custom-call(f32[16,1024,512]{2,1,0:T(8,128)} %get-tuple-element.21.e_ref, f32[64,8,128]{2,1,0:T(8,128)} %copy-done.5, f32[8,3,8,128]{3,2,1,0:T(8,128)} %copy-done.6, bf16[16,128,512]{2,1,0:T(8,128)(2,1)} %copy-done.2, ...), custom_call_target="tpu_custom_call" | custom-call | tf_op jit(solution)/shard_map/grad_reduce/pallas_call | solution.py:523
  154.4 1.2 slice.19
  155.6 0.0 copy-start.1
  155.6 1.6 copy-done.1
  157.2 0.0 copy-start.4
  157.2 1.0 copy-done.4
  158.3 0.0 copy-start.7
  158.3 0.8 copy-done.7
  159.0 0.0 copy-start.8
  159.0 6.7 %table_grad.1 = f32[8192,128]{1,0:T(8,128)} custom-call(s32[1024]{0:T(1024)S(1)} %get-tuple-element.35.cidx_ref, s32[64,128]{1,0:T(8,128)S(1)} %get-tuple-element.27.row_ref, f32[64,128]{1,0:T(8,128)S(1)} %copy-done.7, f32[1024,128]{1,0:T(8,128)S(1)} %copy-done.4, f32[64,128]{1,0:T(8,128)S(1)} %get-tuple-element.30.pos_ref, bf16[8192,128]{1,0:T(8,128)(2,1)S(1)} %copy-done.1), custom_call_target="tpu_custom_call" | custom-call | tf_op jit(solution)/shard_map/table_grad/pallas_call | solution.py:536
  165.7 0.0 copy-done.8
  165.7 0.0 copy-start.9
  165.7 1.0 copy.21
  166.7 0.4 copy-done.9
  167.1 0.8 copy.22
  (3 shorter events, 0.1 us)
Async XLA Ops:
  0.6 7.5 %dynamic-slice-start = ((f32[131072]{0:T(1024)}, s32[]{:T(128)}), f32[1024]{0:T(1024)S(1)}, s32[]{:S(2)}) async-start(f32[131072]{0:T(1024)} %param.12, s32[]{:T(128)} %select_n.7), calls=%async_computation | async-start | bytes 8704 | tf_op jit(solution)/shard_map/dynamic_slice | solution.py:504
  39.1 1.0 copy-start.3
  65.6 1.3 copy-start
  66.9 1.3 copy-start.2
  68.2 0.7 copy-start.5
  68.9 0.6 copy-start.6
  155.6 1.6 copy-start.1
  157.2 1.0 copy-start.4
  158.3 0.8 copy-start.7
  159.0 6.7 %copy-start.8 = (f32[256,1024]{1,0:T(8,128)S(1)}, f32[256,1024]{1,0:T(8,128)}, u32[]{:S(2)}) copy-start(f32[256,1024]{1,0:T(8,128)} %get-tuple-element.43) | copy-start | bytes 3145732
  165.7 1.4 copy-start.9

commit v4 on v3

--- a/solution.py
+++ b/solution.py
@@ -19,6 +19,14 @@
     return pl.ds(i, 1)
 
 
+def flag(mask):
+    return jnp.where(mask, 1.0, 0.0)
+
+
+def iota(shape, dim):
+    return lax.broadcasted_iota(jnp.int32, shape, dim)
+
+
 def coord(me, axis):
     stride, radix = COORD[axis]
     return (me // stride) % radix
@@ -50,7 +58,7 @@
     return pltpu.make_async_remote_copy(src_ref=src, dst_ref=dst, send_sem=send, recv_sem=recv, device_id=(dev,), device_id_type=MESH)
 
 
-def gather_streams(me, streams, bulk, send_sem, recv_sem):
+def gather_streams(me, streams, bulk, send_sem, recv_sem, between=None):
     pending, sent = [None] * len(streams), []
     for phase in range(4):
         for s, (ref, off, unit, order) in enumerate(streams):
@@ -69,6 +77,8 @@
                 c.start()
                 pending[s].append(c)
                 sent.append(c)
+        if between and phase < 3:
+            between(phase)
     last = []
     for i, (ref, count) in enumerate(bulk):
         n = len(streams) * 9 + i
@@ -144,8 +154,19 @@
 H_FIRST = (0, 3, 6)
 
 
-def query_kernel(x_ref, win_ref, wout_ref, tgt_ref, h_ref, tall_ref, pre_ref, send_sem, recv_sem):
+def column(row):
+    return jnp.transpose(jnp.broadcast_to(row, (LANE, LANE)))
+
+
+def query_kernel(x_ref, win_ref, wout_ref, tgt_ref, blk_ref, cid_ref, logq_ref, h_ref, tall_ref, pre_ref, cand_ref, candt_ref, cidb_ref, logqb_ref,
+                 blk, ids, lqs, rows, load_sem, send_sem, recv_sem):
     me = lax.axis_index("dp")
+    mine = pl.ds(pl.multiple_of(me * 8, 8), 8)
+    loads = [
+        pltpu.make_async_copy(cid_ref.at[mine], ids, load_sem.at[0]), pltpu.make_async_copy(logq_ref.at[mine], lqs, load_sem.at[1]),
+        pltpu.make_async_copy(blk_ref, blk, load_sem.at[2])]
+    for c in loads:
+        c.start()
     entry_barrier(me)
     pre = jnp.dot(x_ref[...], win_ref[...], preferred_element_type=F32)
     pre_ref[...] = pre
@@ -161,7 +182,32 @@
         streams.append((h_ref, core * 512 + H_OFF[s], H_UNIT[s], ORDERS[s]))
     tall_ref[core * TOK + block_index(me, ORDERS[2])] = tgt_ref[...]
     streams.append((tall_ref, core * TOK, 1, ORDERS[2]))
-    for c in gather_streams(me, streams, [(h_ref, 512), (tall_ref, TOK)], send_sem, recv_sem):
+    lane = iota((1, LANE), 1)
+
+    def pick(n, carry):
+        part = pl.ds(pl.multiple_of(n // 8 * WIDE, WIDE), WIDE)
+        first = n % 8 * KILO
+        want = cidb_ref[part, :]
+        picks = [flag(want == (lane + (first + u * LANE)).astype(F32)).astype(BF16) for u in range(8)]
+        rows[part, :] += jnp.dot(jnp.concatenate(picks, axis=1), blk[pl.ds(pl.multiple_of(first, KILO), KILO), :], preferred_element_type=F32)
+        return carry
+
+    def fill(phase):
+        if phase == 0:
+            for c in loads:
+                c.wait()
+            for c in range(8):
+                at = slice(c * LANE, c * LANE + LANE)
+                cidb_ref[at, :] = column((ids[c : c + 1, :] - me * ALL).astype(F32))
+                logqb_ref[at, :] = column(lqs[c : c + 1, :])
+            rows[...] = jnp.zeros_like(rows)
+        bounds = (0, 8, 17, 32)
+        lax.fori_loop(bounds[phase], bounds[phase + 1], pick, 0)
+        if phase == 2:
+            cand_ref[...] = rows[...].astype(BF16)
+            candt_ref[...] = jnp.transpose(rows[...]).astype(BF16)
+
+    for c in gather_streams(me, streams, [(h_ref, 512), (tall_ref, TOK)], send_sem, recv_sem, fill):
         c.wait_send()
 
 
@@ -212,81 +258,79 @@
 TILE = KILO
 
 
-def score_kernel(h_ref, blk_ref, cand_ref, cid_ref, logq_ref, tgt_ref, e_ref, mc_ref, st_ref, pos_ref, row_ref, hc_ref, te_ref, zd, cidb, logqb, part):
+def score_kernel(h_ref, blk_ref, cand_ref, cidb, logqb, tgt_ref, e_ref, mc_ref, st_ref, pos_ref, code_ref, hc_ref, te_ref, zd, part, local, hs, es, codes, sem):
     step = pl.program_id(0)
     block_rows = blk_ref.shape[0]
-    base = lax.axis_index("dp") * block_rows
 
     @pl.when(step == 0)
     def _():
-        cidb[...] = jnp.broadcast_to(cid_ref[...], cidb.shape)
-        logqb[...] = jnp.broadcast_to(logq_ref[...], logqb.shape)
-        local = tgt_ref[...] - base
-        own = (local >= 0) & (local < block_rows)
-        own_f = jnp.where(own, 1.0, 0.0)
+        rel = tgt_ref[...] - lax.axis_index("dp") * block_rows
+        own = (rel >= 0) & (rel < block_rows)
+        local[...] = rel.astype(F32)
+        own_f = flag(own)
         own_b = own_f.astype(BF16)
-        up = lax.broadcasted_iota(jnp.int32, (LANE, LANE), 0) < lax.broadcasted_iota(jnp.int32, (LANE, LANE), 1)
-        prefix = jnp.dot(own_b, jnp.where(up, 1.0, 0.0).astype(BF16), preferred_element_type=F32)
+        up = iota((LANE, LANE), 0) < iota((LANE, LANE), 1)
+        prefix = jnp.dot(own_b, flag(up).astype(BF16), preferred_element_type=F32)
         total = jnp.dot(own_b, jnp.ones((LANE, LANE), BF16), preferred_element_type=F32)
-        low = lax.broadcasted_iota(jnp.int32, (TOK, TOK), 0) > lax.broadcasted_iota(jnp.int32, (TOK, TOK), 1)
-        offset = jnp.dot(jnp.where(low, 1.0, 0.0).astype(BF16), total.astype(BF16), preferred_element_type=F32)
+        low = iota((TOK, TOK), 0) > iota((TOK, TOK), 1)
+        offset = jnp.dot(flag(low).astype(BF16), total.astype(BF16), preferred_element_type=F32)
         pos_ref[...] = jnp.where(own, prefix + offset, -1.0)
         zd[...] = jnp.zeros_like(zd)
-        te_ref[...] = jnp.zeros_like(te_ref)
-        chunks = (jnp.sum(own_f).astype(jnp.int32) + 127) // LANE
-        slot0 = lax.broadcasted_iota(jnp.int32, (LANE, LANE), 0).astype(F32)
-        lane = lax.broadcasted_iota(jnp.int32, (1, LANE), 1)
+
+        def clear(i, carry):
+            te_ref[pl.ds(pl.multiple_of(i * LANE, LANE), LANE), :] = jnp.zeros((LANE, LANE), F32)
+            return carry
+
+        lax.fori_loop(0, TOK, clear, 0)
+        count = jnp.sum(own_f).astype(jnp.int32)
+        slot0 = iota((LANE, LANE), 0).astype(F32)
+        lane = iota((1, LANE), 1)
+        sub = iota((16, LANE), 0)
+
+        def one_row(ref, i):
+            tile = ref[pl.ds(pl.multiple_of(i // 16 * 16, 16), 16), :].astype(F32)
+            return jnp.sum(jnp.where(sub == i % 16, tile, 0.0), axis=0, keepdims=True)
 
         def chunk(c, carry):
             slot = slot0 + (c * LANE).astype(F32)
 
-            def collect(i, acc):
-                hsum, code = acc
-                picks = []
+            def collect(r, code):
+                mark = (tgt_ref[one(r), :] % block_rows) * ALL + (lane + r * LANE)
+                return code + jnp.where(pos_ref[one(r), :] == slot, mark, 0)
+
+            code = lax.fori_loop(0, TOK, collect, jnp.zeros((LANE, LANE), jnp.int32), unroll=8)
+            row = jnp.sum((code // ALL).astype(F32), axis=1, keepdims=True)
+            tok = jnp.sum((code % ALL).astype(F32), axis=1, keepdims=True)
+            both = row.astype(jnp.int32) * ALL + tok.astype(jnp.int32)
+            code_ref[one(c), :] = jnp.transpose(jnp.broadcast_to(both, (LANE, LANE)))[0:1, :]
+            copy = pltpu.make_async_copy(code_ref.at[one(c)], codes, sem)
+            copy.start()
+            copy.wait()
+            left = count - c * LANE
+
+            def fetch(i, carry2):
                 for u in range(8):
-                    r = i * 8 + u
-                    hit = pos_ref[one(r), :] == slot
-                    code = code + jnp.where(hit, tgt_ref[one(r), :] - base, 0)
-                    picks.append(jnp.where(hit, 1.0, 0.0).astype(BF16))
-                pick = jnp.concatenate(picks, axis=1)
-                tok = pl.ds(pl.multiple_of(i * KILO, KILO), KILO)
-                return hsum + jnp.dot(pick, h_ref[tok, :], preferred_element_type=F32), code
-
-            hsum, code = lax.fori_loop(0, 8, collect, (jnp.zeros((LANE, LANE), F32), jnp.zeros((LANE, LANE), jnp.int32)))
-            rowb = jnp.broadcast_to(jnp.sum(code.astype(F32), axis=1, keepdims=True), (LANE, LANE))
-            row_ref[one(c), :] = jnp.transpose(rowb)[0:1, :].astype(jnp.int32)
-
-            def fetch(i, acc):
-                picks = []
-                for u in range(8):
-                    hit = rowb == (lane + (i * 8 + u) * LANE).astype(F32)
-                    picks.append(jnp.where(hit, 1.0, 0.0).astype(BF16))
-                rows = pl.ds(pl.multiple_of(i * KILO, KILO), KILO)
-                return acc + jnp.dot(jnp.concatenate(picks, axis=1), blk_ref[rows, :], preferred_element_type=F32)
-
-            tsum = lax.fori_loop(0, block_rows // KILO, fetch, jnp.zeros((LANE, LANE), F32))
-            hc_ref[pl.ds(c * LANE, LANE), :] = hsum.astype(BF16)
-            z = jnp.transpose(jnp.broadcast_to(jnp.sum(hsum * tsum, axis=1, keepdims=True) / WIDE, (LANE, LANE)))[0:8, :]
-            hi = z.astype(BF16).astype(F32)
-            mid = (z - hi).astype(BF16).astype(F32)
-            parts = jnp.concatenate([jnp.transpose(tsum), hi, mid, z - hi - mid], axis=0).astype(BF16)
-
-            def spread(i, carry2):
-                picks = []
-                for u in range(4):
-                    hit = pos_ref[one(i * 4 + u), :] == slot
-                    picks.append(jnp.where(hit, 1.0, 0.0).astype(BF16))
-                got = jnp.dot(parts, jnp.concatenate(picks, axis=1), preferred_element_type=F32)
-                te_ref[i] = (te_ref[i].astype(F32) + got[0:LANE, :]).astype(BF16)
-                zrow = (got[LANE : LANE + 1, :] + got[LANE + 8 : LANE + 9, :] + got[LANE + 16 : LANE + 17, :]) * WIDE
-                for u in range(4):
-                    zd[one(i * 4 + u), :] += zrow[:, LANE * u : LANE * u + LANE]
+                    n = i * 8 + u
+                    v = codes[0, n]
+                    hs[one(n), :] = one_row(h_ref, v % ALL)
+                    row = one_row(blk_ref, v // ALL)
+                    es[one(n), :] = row
+                    te_ref[one(jnp.where(n < left, v % ALL, ALL)), :] = row
                 return carry2
 
-            lax.fori_loop(0, 16, spread, 0)
+            lax.fori_loop(0, (jnp.minimum(left, LANE) + 7) // 8, fetch, 0)
+            hc_ref[pl.ds(c * LANE, LANE), :] = hs[...]
+            z = jnp.broadcast_to(jnp.sum(hs[...] * es[...], axis=1, keepdims=True), (LANE, LANE))
+
+            def spread(r, carry2):
+                hit = pos_ref[one(r), :] == slot
+                zd[one(r), :] += jnp.sum(jnp.where(hit, z, 0.0), axis=0, keepdims=True)
+                return carry2
+
+            lax.fori_loop(0, TOK, spread, 0, unroll=8)
             return carry
 
-        lax.fori_loop(0, chunks, chunk, 0)
+        lax.fori_loop(0, (count + 127) // LANE, chunk, 0)
 
     for j in range(4):
         col = pl.multiple_of(step * TILE + WIDE * j, WIDE)
@@ -294,7 +338,7 @@
         for half in range(2):
             q = 2 * j + half
             cols = slice(LANE * (q % 4), LANE * (q % 4) + LANE)
-            tgt = tgt_ref[one(step * 8 + q), :]
+            tgt = local[one(step * 8 + q), :]
             for c in range(8):
                 rows = slice(LANE * c, LANE * c + LANE)
                 s = dots[rows, LANE * half : LANE * half + LANE] - logqb[rows, :]
@@ -311,39 +355,55 @@
     st_ref[0, 2] = jnp.where(pos_ref[grp, :] >= 0.0, zd[grp, :], -jnp.inf)
 
 
-def table_kernel(cidx_ref, row_ref, g_ref, dcand_ref, pos_ref, hc_ref, de_ref, gh):
+def table_kernel(cidx_ref, code_ref, g_ref, pos_ref, lossrow_ref, dcand_hbm, tiles_hbm, hc_ref, de_ref, dwin_ref, dwout_ref, loss_ref, dcand, whole, hc, gh, sem):
+    loads = [pltpu.make_async_copy(dcand_hbm, dcand, sem.at[0]), pltpu.make_async_copy(tiles_hbm, whole, sem.at[1])]
+    for c in loads:
+        c.start()
+    loss_ref[0, 0] = jnp.max(lossrow_ref[...])
+
     def clear(i, carry):
-        de_ref[pl.ds(pl.multiple_of(i * TOK, TOK), TOK), :] = jnp.zeros((TOK, LANE), F32)
-        return carry
-
-    lax.fori_loop(0, de_ref.shape[0] // TOK, clear, 0)
+        de_ref[pl.ds(pl.multiple_of(i * LANE, LANE), LANE), :] = jnp.zeros((LANE, LANE), F32)
+        return carry
+
+    lax.fori_loop(0, de_ref.shape[0] // LANE, clear, 0)
+    for c in loads:
+        c.wait()
+
+    base = lax.axis_index("dp") * ALL
 
     def place(i, carry):
         for u in range(8):
-            de_ref[one(cidx_ref[i * 8 + u]), :] = dcand_ref[one(i * 8 + u), :]
-        return carry
-
-    lax.fori_loop(0, dcand_ref.shape[0] // 8, place, 0)
-    count = jnp.sum(jnp.where(pos_ref[...] >= 0.0, 1.0, 0.0)).astype(jnp.int32)
-    slot0 = lax.broadcasted_iota(jnp.int32, (LANE, LANE), 0).astype(F32)
+            n = i * 8 + u
+            de_ref[one(cidx_ref[0, n] - base), :] = dcand[one(n), :]
+        return carry
+
+    lax.fori_loop(0, dcand.shape[0] // 8, place, 0)
+    count = jnp.sum(flag(pos_ref[...] >= 0.0)).astype(jnp.int32)
+    slot0 = iota((LANE, LANE), 0).astype(F32)
 
     def chunk(c, carry):
         slot = slot0 + (c * LANE).astype(F32)
+        copy = pltpu.make_async_copy(hc_ref.at[pl.ds(pl.multiple_of(c * LANE, LANE), LANE)], hc, sem.at[2])
+        copy.start()
 
         def collect(r, acc):
             return acc + jnp.where(pos_ref[one(r), :] == slot, g_ref[one(r), :], 0.0)
 
-        g = jnp.sum(lax.fori_loop(0, 64, collect, jnp.zeros((LANE, LANE), F32), unroll=8), axis=1, keepdims=True)
-        gh[...] = g * hc_ref[pl.ds(c * LANE, LANE), :].astype(F32)
+        g = jnp.sum(lax.fori_loop(0, TOK, collect, jnp.zeros((LANE, LANE), F32), unroll=8), axis=1, keepdims=True)
+        copy.wait()
+        gh[...] = g * hc[...]
 
         def put(i, carry2):
-            de_ref[one(row_ref[c, i]), :] += gh[one(i), :]
+            de_ref[one(code_ref[c, i] // ALL), :] += gh[one(i), :]
             return carry2
 
         lax.fori_loop(0, jnp.minimum(count - c * LANE, LANE), put, 0)
         return carry
 
     lax.fori_loop(0, (count + 127) // LANE, chunk, 0)
+    dwout_ref[...] = whole[0:LANE].reshape(KILO, LANE)
+    for j in range(8):
+        dwin_ref[:, LANE * j : LANE * j + LANE] = whole[LANE + 32 * j : 160 + 32 * j].reshape(WIDE, LANE)
 
 
 LAST = 27
@@ -359,10 +419,16 @@
     return [c]
 
 
-def grad_kernel(e_ref, mc_ref, st_ref, te_ref, h_ref, candt_ref, x_ref, wout_ref, pre_ref, dwin_ref, dwout_ref, g_ref, loss_ref, dcand_ref,
-                ebuf, srecv, cur, norm, acc, recv, tiles, trecv, whole, e_sem, core_send, core_recv, send_sem, recv_sem):
+def grad_kernel(e_ref, mc_ref, st_ref, te_hbm, h_hbm, candt_hbm, x_hbm, wout_hbm, pre_hbm, whole, g_ref, loss_ref, dcand_ref,
+                ebuf, srecv, cur, norm, acc, recv, tiles, trecv, te_ref, h_ref, candt_ref, x_ref, wout_ref, pre_ref,
+                load_sem, e_sem, core_send, core_recv, send_sem, recv_sem):
     me = lax.axis_index("dp")
     core = coord(me, "core")
+    loads = [
+        pltpu.make_async_copy(a, b, load_sem.at[i]) for i, (a, b) in enumerate([
+            (candt_hbm, candt_ref), (te_hbm.at[pl.ds(0, ALL)], te_ref), (h_hbm, h_ref), (x_hbm, x_ref), (wout_hbm, wout_ref), (pre_hbm, pre_ref)])]
+    for c in loads:
+        c.start()
     entry_barrier(me)
 
     def load(i):
@@ -393,11 +459,14 @@
                 (ebuf[t, LANE * c : LANE * c + LANE, LANE * q : LANE * q + LANE] * scale[c : c + 1, :]).astype(BF16) for c in range(8)], axis=0))
         return jnp.concatenate(blocks, axis=1)
 
+    for c in loads:
+        c.wait()
+
     def query_grad(t):
         dqt = jnp.dot(candt_ref[...], probs(t), preferred_element_type=F32)
-        grow = jnp.concatenate([g_ref[one(t * 4 + q), :] for q in range(4)], axis=1)
-        dqt = dqt + grow * te_ref[t].astype(F32)
-        return jnp.transpose(dqt).reshape(TOK, 8, LANE)
+        gcol = jnp.concatenate([column(g_ref[one(t * 4 + q), :]) for q in range(4)], axis=0)
+        dq = jnp.transpose(dqt) + gcol * te_ref[pl.ds(pl.multiple_of(t * PART, PART), PART), :]
+        return dq.reshape(TOK, 8, LANE)
 
     def swap(i):
         return remote(acc.at[pl.ds(((1 - core) * 8 + i) * TOK, TOK)], recv.at[pl.ds(i * TOK, TOK)], core_send.at[i], core_recv.at[i], peer(me, "core", 1))
@@ -453,9 +522,6 @@
         whole[own] = tiles[own]
         streams.append((whole, core * 192 + TOK * s, 1, ORDERS[s]))
     sent += gather_streams(me, streams, [(whole, 192)], send_sem.at[2], recv_sem.at[2])
-    dwout_ref[...] = whole[0:LANE].reshape(KILO, LANE)
-    for j in range(8):
-        dwin_ref[:, LANE * j : LANE * j + LANE] = whole[LANE + 32 * j : 160 + 32 * j].reshape(WIDE, LANE)
     for c in sent:
         c.wait_send()
 
@@ -486,61 +552,70 @@
         block_rows = table_blk.shape[0]
         cand_dev = cand_ids.shape[0] // num_dev
         tok_total = features.shape[0] * num_dev
-        tgt_row = jnp.pad(targets[None, :], ((0, 0), (0, TOK)))
-        h_all, tall, pre = pl.pallas_call(
+        anyspec = pl.BlockSpec(memory_space=pl.ANY)
+        cid_rows, logq_rows = cand_ids.reshape(KILO, LANE), log_q.reshape(KILO, LANE)
+        h_all, tall, pre, cand_rows, cand_t, cidb, logqb = pl.pallas_call(
             query_kernel,
-            out_shape=[jax.ShapeDtypeStruct((KILO, 8, LANE), BF16), jax.ShapeDtypeStruct((LANE, 1, LANE), jnp.int32), jax.ShapeDtypeStruct((TOK, KILO), F32)],
-            in_specs=vmem(4), out_specs=vmem(3),
-            scratch_shapes=[dma(4 * NPEER), dma(4 * NPEER)],
+            out_shape=[
+                jax.ShapeDtypeStruct((KILO, 8, LANE), BF16), jax.ShapeDtypeStruct((LANE, 1, TOK), jnp.int32), jax.ShapeDtypeStruct((TOK, KILO), F32),
+                jax.ShapeDtypeStruct((cand_dev, LANE), BF16), jax.ShapeDtypeStruct((LANE, cand_dev), BF16),
+                jax.ShapeDtypeStruct((cand_dev, LANE), F32), jax.ShapeDtypeStruct((cand_dev, LANE), F32)],
+            in_specs=vmem(4) + [anyspec] * 3, out_specs=vmem(7),
+            scratch_shapes=[
+                pltpu.VMEM((block_rows, LANE), BF16), pltpu.VMEM((8, LANE), jnp.int32), pltpu.VMEM((8, LANE), F32), pltpu.VMEM((cand_dev, LANE), F32),
+                dma(3), dma(4 * NPEER), dma(4 * NPEER)],
             compiler_params=params(0), name="query_gather",
-        )(features, w_in, w_out, tgt_row)
+        )(features, w_in, w_out, targets[None, :], table_blk, cid_rows, logq_rows)
         query_all = h_all.reshape(ALL, LANE)
-        t5 = tall[:, 0, :TOK].reshape(2, 4, 4, 4, TOK)
+        t5 = tall.reshape(2, 4, 4, 4, TOK)
         tgt_all = jnp.concatenate([
             t5.transpose(0, 3, 1, 2, 4)[..., 0:24].reshape(2, -1),
             t5.transpose(0, 2, 3, 1, 4)[..., 24:48].reshape(2, -1),
             t5[..., 48:TOK].reshape(2, -1)], axis=1).reshape(TOK, LANE)
-        own_cands = lax.dynamic_slice_in_dim(cand_ids, dev_index * cand_dev, cand_dev)
-        own_logq = lax.dynamic_slice_in_dim(log_q, dev_index * cand_dev, cand_dev)
-        cand_index = own_cands - dev_index * block_rows
-        cand_rows = table_blk[cand_index]
         steps = tok_total // TILE
         whole = lambda *shape: pl.BlockSpec(shape, lambda i: (0,) * len(shape))
         smem = pl.BlockSpec(memory_space=pltpu.SMEM)
-        e, mc, stats, pos, rows, hc, te = pl.pallas_call(
+        e, mc, stats, pos, codes, hc, te = pl.pallas_call(
             score_kernel, grid=(steps,),
             out_shape=[
                 jax.ShapeDtypeStruct((16, cand_dev, PART), F32), jax.ShapeDtypeStruct((TOK, 8, LANE), F32), jax.ShapeDtypeStruct((steps, 3, 8, LANE), F32),
                 jax.ShapeDtypeStruct((TOK, LANE), F32), jax.ShapeDtypeStruct((TOK, LANE), jnp.int32),
-                jax.ShapeDtypeStruct((tok_total, LANE), BF16), jax.ShapeDtypeStruct((16, LANE, PART), BF16)],
-            in_specs=[whole(tok_total, LANE), whole(block_rows, LANE), whole(cand_dev, LANE), whole(cand_dev, 1), whole(cand_dev, 1), whole(TOK, LANE)],
+                jax.ShapeDtypeStruct((tok_total, LANE), F32), jax.ShapeDtypeStruct((tok_total + 8, LANE), F32)],
+            in_specs=[whole(tok_total, LANE), whole(block_rows, LANE)] + [whole(cand_dev, LANE)] * 3 + [whole(TOK, LANE)],
             out_specs=[
                 pl.BlockSpec((2, cand_dev, PART), lambda i: (i, 0, 0)), pl.BlockSpec((8, 8, LANE), lambda i: (i, 0, 0)),
-                pl.BlockSpec((1, 3, 8, LANE), lambda i: (i, 0, 0, 0)), whole(TOK, LANE), whole(TOK, LANE), whole(tok_total, LANE), whole(16, LANE, PART)],
-            scratch_shapes=[pltpu.VMEM((TOK, LANE), F32), pltpu.VMEM((cand_dev, LANE), jnp.int32), pltpu.VMEM((cand_dev, LANE), F32), pltpu.VMEM((8, 8, LANE), F32)],
+                pl.BlockSpec((1, 3, 8, LANE), lambda i: (i, 0, 0, 0)), whole(TOK, LANE), whole(TOK, LANE), whole(tok_total, LANE), whole(tok_total + 8, LANE)],
+            scratch_shapes=[
+                pltpu.VMEM((TOK, LANE), F32), pltpu.VMEM((8, 8, LANE), F32), pltpu.VMEM((TOK, LANE), F32), pltpu.VMEM((LANE, LANE), F32), pltpu.VMEM((LANE, LANE), F32),
+                pltpu.SMEM((1, LANE), jnp.int32), pltpu.SemaphoreType.DMA],
             compiler_params=pltpu.CompilerParams(dimension_semantics=("arbitrary",), vmem_limit_bytes=48 * KILO * KILO), name="score",
-        )(query_all, table_blk, cand_rows, own_cands[:, None], own_logq[:, None], tgt_all)
-        grad_w_in, grad_w_out, grad_tgt, loss, dcand = pl.pallas_call(
+        )(query_all, table_blk, cand_rows, cidb, logqb, tgt_all)
+        tiles, grad_tgt, loss_row, dcand = pl.pallas_call(
             grad_kernel,
             out_shape=[
-                jax.ShapeDtypeStruct((WIDE, KILO), F32), jax.ShapeDtypeStruct((KILO, LANE), F32), jax.ShapeDtypeStruct((TOK, LANE), F32),
+                jax.ShapeDtypeStruct((384, 8, LANE), F32), jax.ShapeDtypeStruct((TOK, LANE), F32),
                 jax.ShapeDtypeStruct((8, LANE), F32), jax.ShapeDtypeStruct((cand_dev, LANE), F32)],
-            in_specs=[pl.BlockSpec(memory_space=pl.ANY)] + vmem(8), out_specs=vmem(5),
+            in_specs=[anyspec] + vmem(2) + [anyspec] * 6, out_specs=vmem(4),
             scratch_shapes=[
                 pltpu.VMEM((16, cand_dev, PART), F32), pltpu.VMEM((80, 3, 8, LANE), F32), pltpu.VMEM((32, 3, 8, LANE), F32), pltpu.VMEM((TOK, LANE), F32),
                 pltpu.VMEM((KILO, 8, LANE), F32), pltpu.VMEM((KILO, 8, LANE), F32),
-                pltpu.VMEM((384, 8, LANE), F32), pltpu.VMEM((384, 8, LANE), F32), pltpu.VMEM((384, 8, LANE), F32),
-                dma(16), dma(8), dma(8), dma(4, 3 * NPEER), dma(4, 3 * NPEER)],
+                pltpu.VMEM((384, 8, LANE), F32), pltpu.VMEM((384, 8, LANE), F32),
+                pltpu.VMEM((tok_total, LANE), F32), pltpu.VMEM((tok_total, LANE), BF16), pltpu.VMEM((LANE, cand_dev), BF16),
+                pltpu.VMEM(features.shape, BF16), pltpu.VMEM(w_out.shape, BF16), pltpu.VMEM(pre.shape, F32),
+                dma(6), dma(16), dma(8), dma(8), dma(4, 3 * NPEER), dma(4, 3 * NPEER)],
             compiler_params=params(1), name="grad_reduce",
-        )(e, mc, stats, te, query_all, cand_rows.T, features, w_out, pre)
-        grad_blk = pl.pallas_call(
+        )(e, mc, stats, te, query_all, cand_t, features, w_out, pre)
+        grad_blk, grad_w_in, grad_w_out, loss = pl.pallas_call(
             table_kernel,
-            out_shape=jax.ShapeDtypeStruct((block_rows, LANE), F32),
-            in_specs=[smem, smem] + vmem(4), out_specs=vmem(1)[0],
-            scratch_shapes=[pltpu.VMEM((LANE, LANE), F32)],
+            out_shape=[
+                jax.ShapeDtypeStruct((block_rows, LANE), F32), jax.ShapeDtypeStruct(w_in.shape, F32), jax.ShapeDtypeStruct(w_out.shape, F32),
+                jax.ShapeDtypeStruct((1, 1), F32)],
+            in_specs=[smem, smem] + vmem(3) + [anyspec] * 3,
+            out_specs=vmem(3) + [smem],
+            scratch_shapes=[pltpu.VMEM((cand_dev, LANE), F32), pltpu.VMEM((384, 8, LANE), F32), pltpu.VMEM((LANE, LANE), F32), pltpu.VMEM((LANE, LANE), F32), dma(3)],
             compiler_params=pltpu.CompilerParams(vmem_limit_bytes=48 * KILO * KILO), name="table_grad",
-        )(cand_index, rows, grad_tgt, dcand, pos, hc)
-        loss = loss[0, 0]
+        )(lax.dynamic_slice_in_dim(cand_ids, dev_index * cand_dev, cand_dev)[None, :], codes, grad_tgt, pos, loss_row, dcand, tiles, hc)
+        loss = loss.reshape(())
         return loss, grad_blk, grad_w_in, grad_w_out
 
     return jax.shard_map(local_step, mesh=mesh, in_specs=(P("dp", None), P(), P(), P("dp", None), P(), P(), P("dp")), out_specs=(P(), P("dp", None), P(), P()), check_vma=False)

time: 169 us -> 155 us (0.917)
  local copies, waits for them, and re-layouts: 22.9 us -> 15.3 us
  Pallas kernels: 144 us -> 138 us
    gather x2 -> x0, local copies, waits for them, and re-layouts: 5.59 us -> none  [local_step(): cand_rows = table_blk[cand_index]]
    pallas_call x2, Pallas kernels: 91.6 us -> 87.9 us  [the longest x1 79.3 us: local_step(): pl.pallas_call(grad_kernel, out_shape=[jax.ShapeDtypeStruct((384, 8, LANE...]
    pallas_call x1, Pallas kernels: 25.4 us -> 23.2 us  [local_step(): pl.pallas_call(score_kernel, grid=(steps,), out_shape=[jax.ShapeDtypeStru...]
where the time goes in v4:
time: 155 us; the launch traced here: 154 us
  Pallas kernels  138 us (89%)
  local copies, waits for them, and re-layouts  15.3 us (10%)
    pallas_call x1, Pallas kernels, local_step(): pl.pallas_call(grad_kernel, out_shape=[jax.ShapeDtypeStruct((384, 8, LANE...  79.3 us
    pallas_call x1, Pallas kernels, local_step(): pl.pallas_call(query_kernel, out_shape=[jax.ShapeDtypeStruct((KILO, 8, LA...  27.1 us
    pallas_call x1, Pallas kernels, local_step(): pl.pallas_call(score_kernel, grid=(steps,), out_shape=[jax.ShapeDtypeStru...  23.2 us
    unnamed x22, local copies, waits for them, and re-layouts  11.4 us
    pallas_call x1, Pallas kernels, local_step(): pl.pallas_call(table_kernel, out_shape=[jax.ShapeDtypeStruct((block_rows,...  8.59 us

profile of v4, /device:TPU:1, one launch (start us, length us, event | category | flops | bytes accessed | tf_op | source)
XLA Modules:
  0.0 154.3 jit_solution(8809426841778138300)
XLA Ops:
  0.6 27.1 %query_gather.1 = (bf16[1024,8,128]{2,1,0:T(8,128)(2,1)}, s32[128,1,64]{2,1,0:T(1,128)}, f32[64,1024]{1,0:T(8,128)}, bf16[1024,128]{1,0:T(8,128)(2,1)}, bf16[128...) custom-call(bf16[64,256]{1,0:T(8,128)(2,1)} %x_hbm.1, bf16[256,1024]{1,0:T(8,128)(2,1)} %win_ref.1, ...), custom_call_target="tpu_custom_call" | custom-call | tf_op jit(solution)/shard_map/query_gather/pallas_call | solution.py:557
  27.8 0.9 slice.13
  28.7 0.1 reshape.40
  28.9 0.9 copy.11
  29.7 0.1 reshape.39
  29.9 0.9 slice.14
  30.8 0.1 reshape.41
  31.0 0.0 copy-start
  31.0 1.6 %copy-done = bf16[8192,128]{1,0:T(8,128)(2,1)S(1)} copy-done((bf16[8192,128]{1,0:T(8,128)(2,1)S(1)}, bf16[8192,128]{1,0:T(8,128)(2,1)}, u32[]{:S(2)}) %copy-start) | copy-done | bytes 2097176
  32.6 0.0 copy-start.1
  32.6 1.6 %copy-done.1 = bf16[1024,8,128]{2,1,0:T(8,128)(2,1)S(1)} copy-done((bf16[1024,8,128]{2,1,0:T(8,128)(2,1)S(1)}, bf16[1024,8,128]{2,1,0:T(8,128)(2,1)}, u32[]{:S(2)}) %copy-start.1) | copy-done | bytes 2097176
  34.1 0.0 copy-start.4
  34.2 1.0 copy-done.4
  35.2 0.0 copy-start.5
  35.2 1.0 copy-done.5
  36.2 0.0 copy-start.7
  36.2 0.9 copy-done.7
  37.2 23.2 %score.1 = (f32[16,1024,512]{2,1,0:T(8,128)}, f32[64,8,128]{2,1,0:T(8,128)S(1)}, f32[8,3,8,128]{3,2,1,0:T(8,128)S(1)}, f32[64,128]{1,0:T(8,128)S(1)}, s32[64,128...) custom-call(bf16[8192,128]{1,0:T(8,128)(2,1)S(1)} %bitcast.13, bf16[8192,128]{1,0:T(8,128)(2,1)S(1)} %copy-done, ...), custom_call_target="tpu_custom_call" | custom-call | tf_op jit(solution)/shard_map/score/pallas_call | solution.py:578
  60.4 0.0 copy-start.6
  60.4 0.7 copy-done.6
  61.1 0.0 copy-start.8
  61.1 0.6 copy-done.8
  61.7 79.3 %grad_reduce.1 = (f32[384,8,128]{2,1,0:T(8,128)}, f32[64,128]{1,0:T(8,128)}, f32[8,128]{1,0:T(8,128)}, f32[1024,128]{1,0:T(8,128)}) custom-call(f32[16,1024,512]{2,1,0:T(8,128)} %get-tuple-element.32.e_ref, f32[64,8,128]{2,1,0:T(8,128)} %copy-done.6, f32[8,3,8,128]{3,2,1,0:T(8,128)} %copy-done.8, f32[8200,128]{1,0:T(8,128)} %get-tuple-element.35.te_hbm, ...), custom_call_target="tpu_custom_call" | custom-call | tf_op jit(solution)/shard_map/grad_reduce/pallas_call | solution.py:593
  141.1 0.7 dynamic_slice.3
  141.8 0.0 copy-start.2
  141.8 1.4 copy-done.2
  143.2 0.0 copy-start.3
  143.2 1.0 copy-done.3
  144.2 0.0 copy-start.9
  144.2 0.8 copy-done.9
  145.0 0.0 copy-start.10
  145.0 0.7 copy-done.10
  145.7 8.6 %table_grad.1 = (f32[8192,128]{1,0:T(8,128)}, f32[256,1024]{1,0:T(8,128)}, f32[1024,128]{1,0:T(8,128)}, f32[1,1]{1,0:T(1,128)}) custom-call(s32[1,1024]{1,0:T(1,128)S(1)} %bitcast.14, s32[64,128]{1,0:T(8,128)S(1)} %get-tuple-element.31.code_ref, f32[64,128]{1,0:T(8,128)S(1)} %copy-done.9, f32[64,128]{1,0:T(8,128)S(1)} %get-tuple-element.39.pos_ref, ...), custom_call_target="tpu_custom_call" | custom-call | tf_op jit(solution)/shard_map/table_grad/pallas_call | solution.py:608
  (3 shorter events, 0.1 us)
Async XLA Ops:
  31.0 1.6 %copy-start = (bf16[8192,128]{1,0:T(8,128)(2,1)S(1)}, bf16[8192,128]{1,0:T(8,128)(2,1)}, u32[]{:S(2)}) copy-start(bf16[8192,128]{1,0:T(8,128)(2,1)} %blk_ref.3) | copy-start | bytes 6291460
  32.6 1.6 %copy-start.1 = (bf16[1024,8,128]{2,1,0:T(8,128)(2,1)S(1)}, bf16[1024,8,128]{2,1,0:T(8,128)(2,1)}, u32[]{:S(2)}) copy-start(bf16[1024,8,128]{2,1,0:T(8,128)(2,1)} %get-tuple-element.26) | copy-start | bytes 6291460
  34.1 1.0 copy-start.4
  35.2 1.0 copy-start.5
  36.2 0.9 copy-start.7
  60.4 0.7 copy-start.6
  61.1 0.6 copy-start.8
  141.8 1.4 copy-start.2
  143.2 1.0 copy-start.3
  144.2 0.8 copy-start.9
  145.0 0.7 copy-start.10

commit v5 on v4

--- a/solution.py
+++ b/solution.py
@@ -19,6 +19,18 @@
     return pl.ds(i, 1)
 
 
+def down(v):
+    return jnp.sum(v, axis=0, keepdims=True)
+
+
+def across(v):
+    return jnp.sum(v, axis=1, keepdims=True)
+
+
+def peak(v):
+    return jnp.max(v, axis=0, keepdims=True)
+
+
 def flag(mask):
     return jnp.where(mask, 1.0, 0.0)
 
@@ -46,12 +58,12 @@
     return idx
 
 
-def entry_barrier(me):
+def greet(me):
     barrier = pltpu.get_barrier_semaphore()
     for axis in COORD:
         for k in range(1, COORD[axis][1]):
             pl.semaphore_signal(barrier, inc=1, device_id=(peer(me, axis, k),), device_id_type=MESH)
-    pl.semaphore_wait(barrier, NPEER)
+    return barrier
 
 
 def remote(src, dst, send, recv, dev):
@@ -86,6 +98,8 @@
         c = remote(where, where, send_sem.at[n], recv_sem.at[n], peer(me, "core", 1))
         c.start()
         last.append(c)
+    if between:
+        between(3)
     for c in last:
         c.wait_recv()
     return sent + last
@@ -102,7 +116,7 @@
     lax.fori_loop(0, count, add, 0, unroll=4)
 
 
-def scatter_streams(me, ref, first, rref, rbase, streams, send_sem, recv_sem, between):
+def scatter_streams(me, ref, first, rref, rbase, streams, send_sem, recv_sem, prepare=None, between=None):
     sent = []
     pending = [None] * 3
     for step in range(4):
@@ -114,6 +128,8 @@
                 add_rows(ref, pending[s][1], rref, pending[s][2], pending[s][3], 3)
             if step == 3:
                 continue
+            if step == 0 and prepare:
+                prepare(s)
             span = 4 ** (2 - step)
             axis = order[2 - step]
             start = first + off + (idx - idx % (4 * span)) * unit
@@ -129,7 +145,7 @@
             sent += copies
             pending[s] = (copies, start + d * span * unit, rbase, span * unit)
             rbase += 3 * span * unit
-        if step == 0:
+        if step == 0 and between:
             between()
     return sent
 
@@ -158,8 +174,8 @@
     return jnp.transpose(jnp.broadcast_to(row, (LANE, LANE)))
 
 
-def query_kernel(x_ref, win_ref, wout_ref, tgt_ref, blk_ref, cid_ref, logq_ref, h_ref, tall_ref, pre_ref, cand_ref, candt_ref, cidb_ref, logqb_ref,
-                 blk, ids, lqs, rows, load_sem, send_sem, recv_sem):
+def query_kernel(x_ref, win_ref, wout_ref, tgt_ref, blk_ref, cid_ref, logq_ref, tall_ref, h_out, pre_out, cand_out, candt_out, cidb_out, logqb_out,
+                 blk, ids, lqs, rows, h_ref, pre_ref, cand_ref, candt_ref, cidb_ref, logqb_ref, load_sem, out_sem, send_sem, recv_sem):
     me = lax.axis_index("dp")
     mine = pl.ds(pl.multiple_of(me * 8, 8), 8)
     loads = [
@@ -167,7 +183,7 @@
         pltpu.make_async_copy(blk_ref, blk, load_sem.at[2])]
     for c in loads:
         c.start()
-    entry_barrier(me)
+    pl.semaphore_wait(greet(me), NPEER)
     pre = jnp.dot(x_ref[...], win_ref[...], preferred_element_type=F32)
     pre_ref[...] = pre
     act = gelu_parts(pre)[0].astype(BF16)
@@ -201,14 +217,32 @@
                 cidb_ref[at, :] = column((ids[c : c + 1, :] - me * ALL).astype(F32))
                 logqb_ref[at, :] = column(lqs[c : c + 1, :])
             rows[...] = jnp.zeros_like(rows)
-        bounds = (0, 8, 17, 32)
+        bounds = (0, 8, 17, 32, 32)
         lax.fori_loop(bounds[phase], bounds[phase + 1], pick, 0)
         if phase == 2:
             cand_ref[...] = rows[...].astype(BF16)
             candt_ref[...] = jnp.transpose(rows[...]).astype(BF16)
-
-    for c in gather_streams(me, streams, [(h_ref, 512), (tall_ref, TOK)], send_sem, recv_sem, fill):
+            for c in outs:
+                c.start()
+        if phase == 3:
+            half(core).start()
+
+    outs = [
+        pltpu.make_async_copy(a, b, out_sem.at[i]) for i, (a, b) in enumerate([
+            (pre_ref, pre_out), (cand_ref, cand_out), (candt_ref, candt_out), (cidb_ref, cidb_out), (logqb_ref, logqb_out)])]
+
+    def half(c):
+        where = pl.ds(c * 512, 512)
+        return pltpu.make_async_copy(h_ref.at[where], h_out.at[where], out_sem.at[5 + c])
+
+    sent = gather_streams(me, streams, [(h_ref, 512), (tall_ref, TOK)], send_sem, recv_sem, fill)
+    half(1 - core).start()
+    for c in outs:
+        c.wait()
+    for c in sent:
         c.wait_send()
+    half(core).wait()
+    half(1 - core).wait()
 
 
 def reduce_stats(me, st_ref, recv, cur, send_sem, recv_sem):
@@ -258,105 +292,90 @@
 TILE = KILO
 
 
-def score_kernel(h_ref, blk_ref, cand_ref, cidb, logqb, tgt_ref, e_ref, mc_ref, st_ref, pos_ref, code_ref, hc_ref, te_ref, zd, part, local, hs, es, codes, sem):
-    step = pl.program_id(0)
+def target_kernel(tgt_ref, h_hbm, blk_hbm, zst_ref, pos_ref, code_ref, hc_ref, te_out, h_ref, blk_ref, te_ref, zd, hs, es, codes, load_sem, sem):
     block_rows = blk_ref.shape[0]
-
-    @pl.when(step == 0)
-    def _():
-        rel = tgt_ref[...] - lax.axis_index("dp") * block_rows
-        own = (rel >= 0) & (rel < block_rows)
-        local[...] = rel.astype(F32)
-        own_f = flag(own)
-        own_b = own_f.astype(BF16)
-        up = iota((LANE, LANE), 0) < iota((LANE, LANE), 1)
-        prefix = jnp.dot(own_b, flag(up).astype(BF16), preferred_element_type=F32)
-        total = jnp.dot(own_b, jnp.ones((LANE, LANE), BF16), preferred_element_type=F32)
-        low = iota((TOK, TOK), 0) > iota((TOK, TOK), 1)
-        offset = jnp.dot(flag(low).astype(BF16), total.astype(BF16), preferred_element_type=F32)
-        pos_ref[...] = jnp.where(own, prefix + offset, -1.0)
-        zd[...] = jnp.zeros_like(zd)
-
-        def clear(i, carry):
-            te_ref[pl.ds(pl.multiple_of(i * LANE, LANE), LANE), :] = jnp.zeros((LANE, LANE), F32)
-            return carry
-
-        lax.fori_loop(0, TOK, clear, 0)
-        count = jnp.sum(own_f).astype(jnp.int32)
-        slot0 = iota((LANE, LANE), 0).astype(F32)
-        lane = iota((1, LANE), 1)
-        sub = iota((16, LANE), 0)
-
-        def one_row(ref, i):
-            tile = ref[pl.ds(pl.multiple_of(i // 16 * 16, 16), 16), :].astype(F32)
-            return jnp.sum(jnp.where(sub == i % 16, tile, 0.0), axis=0, keepdims=True)
-
-        def chunk(c, carry):
-            slot = slot0 + (c * LANE).astype(F32)
-
-            def collect(r, code):
-                mark = (tgt_ref[one(r), :] % block_rows) * ALL + (lane + r * LANE)
-                return code + jnp.where(pos_ref[one(r), :] == slot, mark, 0)
-
-            code = lax.fori_loop(0, TOK, collect, jnp.zeros((LANE, LANE), jnp.int32), unroll=8)
-            row = jnp.sum((code // ALL).astype(F32), axis=1, keepdims=True)
-            tok = jnp.sum((code % ALL).astype(F32), axis=1, keepdims=True)
-            both = row.astype(jnp.int32) * ALL + tok.astype(jnp.int32)
-            code_ref[one(c), :] = jnp.transpose(jnp.broadcast_to(both, (LANE, LANE)))[0:1, :]
-            copy = pltpu.make_async_copy(code_ref.at[one(c)], codes, sem)
-            copy.start()
-            copy.wait()
-            left = count - c * LANE
-
-            def fetch(i, carry2):
-                for u in range(8):
-                    n = i * 8 + u
-                    v = codes[0, n]
-                    hs[one(n), :] = one_row(h_ref, v % ALL)
-                    row = one_row(blk_ref, v // ALL)
-                    es[one(n), :] = row
-                    te_ref[one(jnp.where(n < left, v % ALL, ALL)), :] = row
-                return carry2
-
-            lax.fori_loop(0, (jnp.minimum(left, LANE) + 7) // 8, fetch, 0)
-            hc_ref[pl.ds(c * LANE, LANE), :] = hs[...]
-            z = jnp.broadcast_to(jnp.sum(hs[...] * es[...], axis=1, keepdims=True), (LANE, LANE))
-
-            def spread(r, carry2):
-                hit = pos_ref[one(r), :] == slot
-                zd[one(r), :] += jnp.sum(jnp.where(hit, z, 0.0), axis=0, keepdims=True)
-                return carry2
-
-            lax.fori_loop(0, TOK, spread, 0, unroll=8)
-            return carry
-
-        lax.fori_loop(0, (count + 127) // LANE, chunk, 0)
-
-    for j in range(4):
-        col = pl.multiple_of(step * TILE + WIDE * j, WIDE)
-        dots = nt_dot(cand_ref[...], h_ref[pl.ds(col, WIDE), :])
-        for half in range(2):
-            q = 2 * j + half
-            cols = slice(LANE * (q % 4), LANE * (q % 4) + LANE)
-            tgt = local[one(step * 8 + q), :]
-            for c in range(8):
-                rows = slice(LANE * c, LANE * c + LANE)
-                s = dots[rows, LANE * half : LANE * half + LANE] - logqb[rows, :]
-                s = jnp.where(cidb[rows, :] == tgt, -1e9, s)
-                m = jnp.max(s, axis=0, keepdims=True)
-                e = jnp.exp(s - m)
-                e_ref[q // 4, rows, cols] = e
-                mc_ref[q, c : c + 1, :] = m
-                part[q, c : c + 1, :] = jnp.sum(e, axis=0, keepdims=True)
-            top = jnp.max(mc_ref[q], axis=0, keepdims=True)
-            st_ref[0, 0, q : q + 1, :] = top
-            st_ref[0, 1, q : q + 1, :] = jnp.sum(part[q] * jnp.exp(mc_ref[q] - top), axis=0, keepdims=True)
-    grp = pl.ds(pl.multiple_of(step * 8, 8), 8)
-    st_ref[0, 2] = jnp.where(pos_ref[grp, :] >= 0.0, zd[grp, :], -jnp.inf)
-
-
-def table_kernel(cidx_ref, code_ref, g_ref, pos_ref, lossrow_ref, dcand_hbm, tiles_hbm, hc_ref, de_ref, dwin_ref, dwout_ref, loss_ref, dcand, whole, hc, gh, sem):
-    loads = [pltpu.make_async_copy(dcand_hbm, dcand, sem.at[0]), pltpu.make_async_copy(tiles_hbm, whole, sem.at[1])]
+    loads = [pltpu.make_async_copy(h_hbm, h_ref, load_sem.at[0]), pltpu.make_async_copy(blk_hbm, blk_ref, load_sem.at[1])]
+    for c in loads:
+        c.start()
+    rel = tgt_ref[...] - lax.axis_index("dp") * block_rows
+    own = (rel >= 0) & (rel < block_rows)
+    own_f = flag(own)
+    own_b = own_f.astype(BF16)
+    up = iota((LANE, LANE), 0) < iota((LANE, LANE), 1)
+    prefix = jnp.dot(own_b, flag(up).astype(BF16), preferred_element_type=F32)
+    total = jnp.dot(own_b, jnp.ones((LANE, LANE), BF16), preferred_element_type=F32)
+    low = iota((TOK, TOK), 0) > iota((TOK, TOK), 1)
+    offset = jnp.dot(flag(low).astype(BF16), total.astype(BF16), preferred_element_type=F32)
+    pos_ref[...] = jnp.where(own, prefix + offset, -1.0)
+    zd[...] = jnp.zeros_like(zd)
+
+    def clear(i, carry):
+        te_ref[pl.ds(pl.multiple_of(i * LANE, LANE), LANE), :] = jnp.zeros((LANE, LANE), F32)
+        return carry
+
+    lax.fori_loop(0, TOK, clear, 0)
+    count = jnp.sum(own_f).astype(jnp.int32)
+    for c in loads:
+        c.wait()
+    slot0 = iota((LANE, LANE), 0).astype(F32)
+    lane = iota((1, LANE), 1)
+    sub = iota((16, LANE), 0)
+
+    def one_row(ref, i):
+        tile = ref[pl.ds(pl.multiple_of(i // 16 * 16, 16), 16), :].astype(F32)
+        return down(jnp.where(sub == i % 16, tile, 0.0))
+
+    def chunk(c, carry):
+        slot = slot0 + (c * LANE).astype(F32)
+
+        def collect(r, code):
+            mark = (tgt_ref[one(r), :] % block_rows) * ALL + (lane + r * LANE)
+            return code + jnp.where(pos_ref[one(r), :] == slot, mark, 0)
+
+        code = lax.fori_loop(0, TOK, collect, jnp.zeros((LANE, LANE), jnp.int32), unroll=8)
+        row = across((code // ALL).astype(F32))
+        tok = across((code % ALL).astype(F32))
+        both = row.astype(jnp.int32) * ALL + tok.astype(jnp.int32)
+        code_ref[one(c), :] = jnp.transpose(jnp.broadcast_to(both, (LANE, LANE)))[0:1, :]
+        copy = pltpu.make_async_copy(code_ref.at[one(c)], codes, sem)
+        copy.start()
+        copy.wait()
+        left = count - c * LANE
+
+        def fetch(i, carry2):
+            for u in range(8):
+                n = i * 8 + u
+                v = codes[0, n]
+                hs[one(n), :] = one_row(h_ref, v % ALL)
+                row = one_row(blk_ref, v // ALL)
+                es[one(n), :] = row
+                te_ref[one(jnp.where(n < left, v % ALL, ALL)), :] = row
+            return carry2
+
+        lax.fori_loop(0, (jnp.minimum(left, LANE) + 7) // 8, fetch, 0)
+        keep = pltpu.make_async_copy(hs, hc_ref.at[pl.ds(pl.multiple_of(c * LANE, LANE), LANE)], load_sem.at[3])
+        keep.start()
+        z = jnp.broadcast_to(across(hs[...] * es[...]), (LANE, LANE))
+
+        def spread(r, carry2):
+            hit = pos_ref[one(r), :] == slot
+            zd[one(r), :] += down(jnp.where(hit, z, 0.0))
+            return carry2
+
+        lax.fori_loop(0, TOK, spread, 0, unroll=8)
+        keep.wait()
+        return carry
+
+    lax.fori_loop(0, (count + 127) // LANE, chunk, 0)
+    copy = pltpu.make_async_copy(te_ref.at[pl.ds(0, ALL)], te_out, load_sem.at[2])
+    copy.start()
+    zst_ref[...] = jnp.where(pos_ref[...] >= 0.0, zd[...], -jnp.inf)
+    copy.wait()
+
+
+def table_kernel(code_ref, g_ref, pos_ref, lossrow_ref, cid_hbm, dcand_hbm, tiles_hbm, hc_ref, de_ref, dwin_ref, dwout_ref, loss_ref, cidx, dcand, whole, hc, gh, sem):
+    me = lax.axis_index("dp")
+    loads = [pltpu.make_async_copy(cid_hbm.at[pl.ds(pl.multiple_of(me * 8, 8), 8)], cidx, sem.at[3]), pltpu.make_async_copy(dcand_hbm, dcand, sem.at[0]), pltpu.make_async_copy(tiles_hbm, whole, sem.at[1])]
     for c in loads:
         c.start()
     loss_ref[0, 0] = jnp.max(lossrow_ref[...])
@@ -369,12 +388,12 @@
     for c in loads:
         c.wait()
 
-    base = lax.axis_index("dp") * ALL
+    base = me * ALL
 
     def place(i, carry):
         for u in range(8):
             n = i * 8 + u
-            de_ref[one(cidx_ref[0, n] - base), :] = dcand[one(n), :]
+            de_ref[one(cidx[i // 16, i % 16 * 8 + u] - base), :] = dcand[one(n), :]
         return carry
 
     lax.fori_loop(0, dcand.shape[0] // 8, place, 0)
@@ -419,26 +438,50 @@
     return [c]
 
 
-def grad_kernel(e_ref, mc_ref, st_ref, te_hbm, h_hbm, candt_hbm, x_hbm, wout_hbm, pre_hbm, whole, g_ref, loss_ref, dcand_ref,
-                ebuf, srecv, cur, norm, acc, recv, tiles, trecv, te_ref, h_ref, candt_ref, x_ref, wout_ref, pre_ref,
-                load_sem, e_sem, core_send, core_recv, send_sem, recv_sem):
+def grad_kernel(tgt_ref, zst_ref, h_hbm, cand_hbm, cidb_hbm, logqb_hbm, candt_hbm, te_hbm, x_hbm, wout_hbm, pre_hbm, g_ref, loss_ref, tiles_out, dcand_out,
+                ebuf, mc_ref, st_ref, part, local, srecv, cur, norm, acc, recv, tiles, trecv, whole, dcand_ref,
+                h_ref, cand_ref, cidb, logqb, candt_ref, te_ref, x_ref, wout_ref, pre_ref,
+                load_sem, core_send, core_recv, send_sem, recv_sem):
     me = lax.axis_index("dp")
     core = coord(me, "core")
     loads = [
         pltpu.make_async_copy(a, b, load_sem.at[i]) for i, (a, b) in enumerate([
-            (candt_hbm, candt_ref), (te_hbm.at[pl.ds(0, ALL)], te_ref), (h_hbm, h_ref), (x_hbm, x_ref), (wout_hbm, wout_ref), (pre_hbm, pre_ref)])]
+            (cand_hbm, cand_ref), (cidb_hbm, cidb), (logqb_hbm, logqb), (h_hbm, h_ref),
+            (candt_hbm, candt_ref), (te_hbm, te_ref), (x_hbm, x_ref), (wout_hbm, wout_ref), (pre_hbm, pre_ref)])]
     for c in loads:
         c.start()
-    entry_barrier(me)
-
-    def load(i):
-        return pltpu.make_async_copy(e_ref.at[i], ebuf.at[i], e_sem.at[i])
-
-    def load_start(i, carry):
-        load(i).start()
-        return carry
-
-    lax.fori_loop(0, 16, load_start, 0)
+    barrier = greet(me)
+    local[...] = (tgt_ref[...] - me * ALL).astype(F32)
+    for g in range(8):
+        st_ref[g, 2] = zst_ref[8 * g : 8 * g + 8, :]
+    for c in loads[:4]:
+        c.wait()
+
+    def score(t, carry):
+        for j in range(2):
+            dots = nt_dot(cand_ref[...], h_ref[pl.ds(pl.multiple_of(t * PART + WIDE * j, WIDE), WIDE), :])
+            for half in range(2):
+                q = 2 * j + half
+                r = t * 4 + q
+                tgt = local[one(r), :]
+                for c in range(8):
+                    rows = slice(LANE * c, LANE * c + LANE)
+                    s = dots[rows, LANE * half : LANE * half + LANE] - logqb[rows, :]
+                    s = jnp.where(cidb[rows, :] == tgt, -1e9, s)
+                    m = peak(s)
+                    e = jnp.exp(s - m)
+                    ebuf[t, rows, LANE * q : LANE * q + LANE] = e
+                    mc_ref[r, c : c + 1, :] = m
+                    part[q, c : c + 1, :] = down(e)
+                most = mc_ref[r]
+                top = peak(most)
+                row = one(t % 2 * 4 + q)
+                st_ref[t // 2, 0, row, :] = top
+                st_ref[t // 2, 1, row, :] = down(part[q] * jnp.exp(most - top))
+        return carry
+
+    lax.fori_loop(0, 16, score, 0)
+    pl.semaphore_wait(barrier, NPEER)
     sent = reduce_stats(me, st_ref, srecv, cur, send_sem.at[3], recv_sem.at[3])
     total = jnp.zeros((8, LANE), F32)
     for g in range(8):
@@ -459,7 +502,7 @@
                 (ebuf[t, LANE * c : LANE * c + LANE, LANE * q : LANE * q + LANE] * scale[c : c + 1, :]).astype(BF16) for c in range(8)], axis=0))
         return jnp.concatenate(blocks, axis=1)
 
-    for c in loads:
+    for c in loads[4:]:
         c.wait()
 
     def query_grad(t):
@@ -473,21 +516,21 @@
 
     def give(i, carry):
         t = (1 - core) * 8 + i
-        load(t).wait()
         acc[pl.ds(t * TOK, TOK)] = query_grad(t)
         swap(i).start()
         return carry
 
     def keep(i, carry):
         t = core * 8 + i
-        load(t).wait()
         val = query_grad(t)
         swap(i).wait_recv()
         acc[pl.ds(t * TOK, TOK)] = val + recv[pl.ds(i * TOK, TOK)]
         return carry
 
     lax.fori_loop(0, 8, give, 0)
-    lax.fori_loop(0, 8, keep, 0)
+
+    def prepare(s):
+        lax.fori_loop(H_FIRST[s], H_FIRST[s] + H_UNIT[s], keep, 0)
 
     def cand_grad():
         dcand_ref[...] = jnp.zeros_like(dcand_ref)
@@ -497,9 +540,11 @@
             return carry
 
         lax.fori_loop(0, 16, accumulate, 0)
-
+        dcand_copy.start()
+
+    dcand_copy = pltpu.make_async_copy(dcand_ref, dcand_out, load_sem.at[9])
     streams = [(H_OFF[s], H_UNIT[s], ORDERS[s]) for s in range(3)]
-    sent += scatter_streams(me, acc, core * 512, recv, 512, streams, send_sem.at[0], recv_sem.at[0], cand_grad)
+    sent += scatter_streams(me, acc, core * 512, recv, 512, streams, send_sem.at[0], recv_sem.at[0], prepare, cand_grad)
     rows = []
     for s in range(3):
         idx = block_index(me, ORDERS[s])
@@ -515,13 +560,16 @@
         tiles[LANE + 32 * j : 160 + 32 * j] = dw_in[:, LANE * j : LANE * j + LANE].reshape(32, 8, LANE)
     streams = [(TOK * s, 1, ORDERS[s]) for s in range(3)]
     half = core_exchange(me, tiles, 192, trecv, send_sem.at[1, LAST], recv_sem.at[1, LAST])
-    sent += half + scatter_streams(me, tiles, core * 192, trecv, 192, streams, send_sem.at[1], recv_sem.at[1], lambda: None)
+    sent += half + scatter_streams(me, tiles, core * 192, trecv, 192, streams, send_sem.at[1], recv_sem.at[1])
     streams = []
     for s in range(3):
         own = core * 192 + TOK * s + block_index(me, ORDERS[s])
         whole[own] = tiles[own]
         streams.append((whole, core * 192 + TOK * s, 1, ORDERS[s]))
     sent += gather_streams(me, streams, [(whole, 192)], send_sem.at[2], recv_sem.at[2])
+    tiles_copy = pltpu.make_async_copy(whole, tiles_out, load_sem.at[10])
+    tiles_copy.start()
+    dcand_copy.wait()
     for c in sent:
         c.wait_send()
 
@@ -530,6 +578,7 @@
         return carry
 
     lax.fori_loop(0, 8, swap_done, 0)
+    tiles_copy.wait()
 
 
 def vmem(n):
@@ -554,16 +603,18 @@
         tok_total = features.shape[0] * num_dev
         anyspec = pl.BlockSpec(memory_space=pl.ANY)
         cid_rows, logq_rows = cand_ids.reshape(KILO, LANE), log_q.reshape(KILO, LANE)
-        h_all, tall, pre, cand_rows, cand_t, cidb, logqb = pl.pallas_call(
+        tall, h_all, pre, cand_rows, cand_t, cidb, logqb = pl.pallas_call(
             query_kernel,
             out_shape=[
-                jax.ShapeDtypeStruct((KILO, 8, LANE), BF16), jax.ShapeDtypeStruct((LANE, 1, TOK), jnp.int32), jax.ShapeDtypeStruct((TOK, KILO), F32),
+                jax.ShapeDtypeStruct((LANE, 1, TOK), jnp.int32), jax.ShapeDtypeStruct((KILO, 8, LANE), BF16), jax.ShapeDtypeStruct((TOK, KILO), F32),
                 jax.ShapeDtypeStruct((cand_dev, LANE), BF16), jax.ShapeDtypeStruct((LANE, cand_dev), BF16),
                 jax.ShapeDtypeStruct((cand_dev, LANE), F32), jax.ShapeDtypeStruct((cand_dev, LANE), F32)],
-            in_specs=vmem(4) + [anyspec] * 3, out_specs=vmem(7),
+            in_specs=vmem(4) + [anyspec] * 3, out_specs=vmem(1) + [anyspec] * 6,
             scratch_shapes=[
                 pltpu.VMEM((block_rows, LANE), BF16), pltpu.VMEM((8, LANE), jnp.int32), pltpu.VMEM((8, LANE), F32), pltpu.VMEM((cand_dev, LANE), F32),
-                dma(3), dma(4 * NPEER), dma(4 * NPEER)],
+                pltpu.VMEM((KILO, 8, LANE), BF16), pltpu.VMEM((TOK, KILO), F32), pltpu.VMEM((cand_dev, LANE), BF16), pltpu.VMEM((LANE, cand_dev), BF16),
+                pltpu.VMEM((cand_dev, LANE), F32), pltpu.VMEM((cand_dev, LANE), F32),
+                dma(3), dma(7), dma(4 * NPEER), dma(4 * NPEER)],
             compiler_params=params(0), name="query_gather",
         )(features, w_in, w_out, targets[None, :], table_blk, cid_rows, logq_rows)
         query_all = h_all.reshape(ALL, LANE)
@@ -572,49 +623,46 @@
             t5.transpose(0, 3, 1, 2, 4)[..., 0:24].reshape(2, -1),
             t5.transpose(0, 2, 3, 1, 4)[..., 24:48].reshape(2, -1),
             t5[..., 48:TOK].reshape(2, -1)], axis=1).reshape(TOK, LANE)
-        steps = tok_total // TILE
-        whole = lambda *shape: pl.BlockSpec(shape, lambda i: (0,) * len(shape))
         smem = pl.BlockSpec(memory_space=pltpu.SMEM)
-        e, mc, stats, pos, codes, hc, te = pl.pallas_call(
-            score_kernel, grid=(steps,),
+        square = pltpu.VMEM((LANE, LANE), F32)
+        big = pltpu.CompilerParams(vmem_limit_bytes=48 * KILO * KILO)
+        zst, pos, codes, hc, te = pl.pallas_call(
+            target_kernel,
             out_shape=[
-                jax.ShapeDtypeStruct((16, cand_dev, PART), F32), jax.ShapeDtypeStruct((TOK, 8, LANE), F32), jax.ShapeDtypeStruct((steps, 3, 8, LANE), F32),
-                jax.ShapeDtypeStruct((TOK, LANE), F32), jax.ShapeDtypeStruct((TOK, LANE), jnp.int32),
-                jax.ShapeDtypeStruct((tok_total, LANE), F32), jax.ShapeDtypeStruct((tok_total + 8, LANE), F32)],
-            in_specs=[whole(tok_total, LANE), whole(block_rows, LANE)] + [whole(cand_dev, LANE)] * 3 + [whole(TOK, LANE)],
-            out_specs=[
-                pl.BlockSpec((2, cand_dev, PART), lambda i: (i, 0, 0)), pl.BlockSpec((8, 8, LANE), lambda i: (i, 0, 0)),
-                pl.BlockSpec((1, 3, 8, LANE), lambda i: (i, 0, 0, 0)), whole(TOK, LANE), whole(TOK, LANE), whole(tok_total, LANE), whole(tok_total + 8, LANE)],
+                jax.ShapeDtypeStruct((TOK, LANE), F32), jax.ShapeDtypeStruct((TOK, LANE), F32), jax.ShapeDtypeStruct((TOK, LANE), jnp.int32),
+                jax.ShapeDtypeStruct((tok_total, LANE), F32), jax.ShapeDtypeStruct((tok_total, LANE), F32)],
+            in_specs=vmem(1) + [anyspec] * 2, out_specs=vmem(3) + [anyspec] * 2,
             scratch_shapes=[
-                pltpu.VMEM((TOK, LANE), F32), pltpu.VMEM((8, 8, LANE), F32), pltpu.VMEM((TOK, LANE), F32), pltpu.VMEM((LANE, LANE), F32), pltpu.VMEM((LANE, LANE), F32),
-                pltpu.SMEM((1, LANE), jnp.int32), pltpu.SemaphoreType.DMA],
-            compiler_params=pltpu.CompilerParams(dimension_semantics=("arbitrary",), vmem_limit_bytes=48 * KILO * KILO), name="score",
-        )(query_all, table_blk, cand_rows, cidb, logqb, tgt_all)
-        tiles, grad_tgt, loss_row, dcand = pl.pallas_call(
+                pltpu.VMEM((tok_total, LANE), BF16), pltpu.VMEM((block_rows, LANE), BF16), pltpu.VMEM((tok_total + 8, LANE), F32), pltpu.VMEM((TOK, LANE), F32),
+                square, square, pltpu.SMEM((1, LANE), jnp.int32), dma(4), pltpu.SemaphoreType.DMA],
+            compiler_params=big, name="target_rows",
+        )(tgt_all, query_all, table_blk)
+        grad_tgt, loss_row, tiles, dcand = pl.pallas_call(
             grad_kernel,
             out_shape=[
-                jax.ShapeDtypeStruct((384, 8, LANE), F32), jax.ShapeDtypeStruct((TOK, LANE), F32),
-                jax.ShapeDtypeStruct((8, LANE), F32), jax.ShapeDtypeStruct((cand_dev, LANE), F32)],
-            in_specs=[anyspec] + vmem(2) + [anyspec] * 6, out_specs=vmem(4),
+                jax.ShapeDtypeStruct((TOK, LANE), F32), jax.ShapeDtypeStruct((8, LANE), F32),
+                jax.ShapeDtypeStruct((384, 8, LANE), F32), jax.ShapeDtypeStruct((cand_dev, LANE), F32)],
+            in_specs=vmem(2) + [anyspec] * 9, out_specs=vmem(2) + [anyspec] * 2,
             scratch_shapes=[
-                pltpu.VMEM((16, cand_dev, PART), F32), pltpu.VMEM((80, 3, 8, LANE), F32), pltpu.VMEM((32, 3, 8, LANE), F32), pltpu.VMEM((TOK, LANE), F32),
+                pltpu.VMEM((16, cand_dev, PART), F32), pltpu.VMEM((TOK, 8, LANE), F32), pltpu.VMEM((8, 3, 8, LANE), F32), pltpu.VMEM((4, 8, LANE), F32), pltpu.VMEM((TOK, LANE), F32),
+                pltpu.VMEM((80, 3, 8, LANE), F32), pltpu.VMEM((32, 3, 8, LANE), F32), pltpu.VMEM((TOK, LANE), F32),
                 pltpu.VMEM((KILO, 8, LANE), F32), pltpu.VMEM((KILO, 8, LANE), F32),
-                pltpu.VMEM((384, 8, LANE), F32), pltpu.VMEM((384, 8, LANE), F32),
-                pltpu.VMEM((tok_total, LANE), F32), pltpu.VMEM((tok_total, LANE), BF16), pltpu.VMEM((LANE, cand_dev), BF16),
+                pltpu.VMEM((384, 8, LANE), F32), pltpu.VMEM((384, 8, LANE), F32), pltpu.VMEM((384, 8, LANE), F32), pltpu.VMEM((cand_dev, LANE), F32),
+                pltpu.VMEM((tok_total, LANE), BF16), pltpu.VMEM((cand_dev, LANE), BF16), pltpu.VMEM((cand_dev, LANE), F32), pltpu.VMEM((cand_dev, LANE), F32),
+                pltpu.VMEM((LANE, cand_dev), BF16), pltpu.VMEM((tok_total, LANE), F32),
                 pltpu.VMEM(features.shape, BF16), pltpu.VMEM(w_out.shape, BF16), pltpu.VMEM(pre.shape, F32),
-                dma(6), dma(16), dma(8), dma(8), dma(4, 3 * NPEER), dma(4, 3 * NPEER)],
+                dma(11), dma(8), dma(8), dma(4, 3 * NPEER), dma(4, 3 * NPEER)],
             compiler_params=params(1), name="grad_reduce",
-        )(e, mc, stats, te, query_all, cand_t, features, w_out, pre)
+        )(tgt_all, zst, query_all, cand_rows, cidb, logqb, cand_t, te, features, w_out, pre)
         grad_blk, grad_w_in, grad_w_out, loss = pl.pallas_call(
             table_kernel,
             out_shape=[
                 jax.ShapeDtypeStruct((block_rows, LANE), F32), jax.ShapeDtypeStruct(w_in.shape, F32), jax.ShapeDtypeStruct(w_out.shape, F32),
                 jax.ShapeDtypeStruct((1, 1), F32)],
-            in_specs=[smem, smem] + vmem(3) + [anyspec] * 3,
-            out_specs=vmem(3) + [smem],
-            scratch_shapes=[pltpu.VMEM((cand_dev, LANE), F32), pltpu.VMEM((384, 8, LANE), F32), pltpu.VMEM((LANE, LANE), F32), pltpu.VMEM((LANE, LANE), F32), dma(3)],
-            compiler_params=pltpu.CompilerParams(vmem_limit_bytes=48 * KILO * KILO), name="table_grad",
-        )(lax.dynamic_slice_in_dim(cand_ids, dev_index * cand_dev, cand_dev)[None, :], codes, grad_tgt, pos, loss_row, dcand, tiles, hc)
+            in_specs=[smem] + vmem(3) + [anyspec] * 4, out_specs=vmem(3) + [smem],
+            scratch_shapes=[pltpu.SMEM((8, LANE), jnp.int32), pltpu.VMEM((cand_dev, LANE), F32), pltpu.VMEM((384, 8, LANE), F32), square, square, dma(4)],
+            compiler_params=big, name="table_grad",
+        )(codes, grad_tgt, pos, loss_row, cid_rows, dcand, tiles, hc)
         loss = loss.reshape(())
         return loss, grad_blk, grad_w_in, grad_w_out
 

time: 155 us -> 148 us (0.955); the launches traced: 154 us -> 149 us
  local copies, waits for them, and re-layouts: 15.3 us -> 10.8 us
    unnamed x22 -> x18, local copies, waits for them, and re-layouts: 11.4 us -> 7.68 us
    pallas_call x3, Pallas kernels: 130 us -> 126 us  [the longest x1 89.4 us: local_step(): pl.pallas_call(grad_kernel, out_shape=[jax.ShapeDtypeStruct((TOK, LANE),...]
    pallas_call x1, Pallas kernels: 8.59 us -> 11.5 us  [local_step(): pl.pallas_call(table_kernel, out_shape=[jax.ShapeDtypeStruct((block_rows,...]
where the time goes in v5:
time: 148 us; the launch traced here: 149 us
  Pallas kernels  138 us (93%)
  local copies, waits for them, and re-layouts  10.8 us (7%)
    pallas_call x1, Pallas kernels, local_step(): pl.pallas_call(grad_kernel, out_shape=[jax.ShapeDtypeStruct((TOK, LANE),...  89.4 us
    pallas_call x1, Pallas kernels, local_step(): pl.pallas_call(query_kernel, out_shape=[jax.ShapeDtypeStruct((LANE, 1, TO...  26.7 us
    pallas_call x1, Pallas kernels, local_step(): pl.pallas_call(table_kernel, out_shape=[jax.ShapeDtypeStruct((block_rows,...  11.5 us
    pallas_call x1, Pallas kernels, local_step(): pl.pallas_call(target_kernel, out_shape=[jax.ShapeDtypeStruct((TOK, LANE)...  10.1 us
    unnamed x18, local copies, waits for them, and re-layouts  7.68 us

profile of v5, /device:TPU:1, one launch (start us, length us, event | category | flops | bytes accessed | tf_op | source)
XLA Modules:
  0.0 149.2 jit_solution(14446090783803494250)
XLA Ops:
  0.6 26.7 %query_gather.1 = (s32[128,1,64]{2,1,0:T(1,128)}, bf16[1024,8,128]{2,1,0:T(8,128)(2,1)}, f32[64,1024]{1,0:T(8,128)}, bf16[1024,128]{1,0:T(8,128)(2,1)}, bf16[128...) custom-call(bf16[64,256]{1,0:T(8,128)(2,1)} %x_hbm.1, bf16[256,1024]{1,0:T(8,128)(2,1)} %win_ref.1, ...), custom_call_target="tpu_custom_call" | custom-call | tf_op jit(solution)/shard_map/query_gather/pallas_call | solution.py:606
  27.4 0.9 slice.14
  28.3 0.1 reshape.40
  28.4 0.9 copy.11
  29.3 0.1 reshape.38
  29.4 0.9 slice.13
  30.4 0.1 reshape.39
  30.6 0.0 copy-start
  30.6 1.6 %copy-done = bf16[8192,128]{1,0:T(8,128)(2,1)S(1)} copy-done((bf16[8192,128]{1,0:T(8,128)(2,1)S(1)}, bf16[8192,128]{1,0:T(8,128)(2,1)}, u32[]{:S(2)}) %copy-start) | copy-done | bytes 2097176
  32.1 0.0 copy-start.1
  32.2 1.6 %copy-done.1 = bf16[1024,8,128]{2,1,0:T(8,128)(2,1)S(1)} copy-done((bf16[1024,8,128]{2,1,0:T(8,128)(2,1)S(1)}, bf16[1024,8,128]{2,1,0:T(8,128)(2,1)}, u32[]{:S(2)}) %copy-start.1) | copy-done | bytes 2097176
  33.7 0.0 copy-start.5
  33.7 10.1 %target_rows.1 = (f32[64,128]{1,0:T(8,128)S(1)}, f32[64,128]{1,0:T(8,128)S(1)}, s32[64,128]{1,0:T(8,128)S(1)}, f32[8192,128]{1,0:T(8,128)}, f32[8192,128]{1,0:T(8,128)}) custom-call(s32[64,128]{1,0:T(8,128)S(1)} %reshape.41.tgt_ref, bf16[8192,128]{1,0:T(8,128)(2,1)S(1)} %bitcast.12, bf16[8192,128]{1,0:T(8,128)(2,1)S(1)} %copy-done), custom_call_target="tpu_custom_call" | custom-call | tf_op jit(solution)/shard_map/target_rows/pallas_call | solution.py:629
  43.8 0.0 copy-start.7
  43.8 0.6 copy-done.7
  44.4 0.0 copy-done.5
  44.4 0.0 copy-start.2
  44.4 89.4 %grad_reduce.1 = (f32[64,128]{1,0:T(8,128)}, f32[8,128]{1,0:T(8,128)}, f32[384,8,128]{2,1,0:T(8,128)}, f32[1024,128]{1,0:T(8,128)}) custom-call(s32[64,128]{1,0:T(8,128)} %copy-done.5, f32[64,128]{1,0:T(8,128)} %copy-done.7, bf16[8192,128]{1,0:T(8,128)(2,1)} %bitcast.11, bf16[1024,128]{1,0:T(8,128)(2,1)} %get-tuple-element.28.cand_hbm, ...), custom_call_target="tpu_custom_call" | custom-call | tf_op jit(solution)/shard_map/grad_reduce/pallas_call | solution.py:640
  133.8 0.0 copy-done.2
  133.8 0.0 copy-start.3
  133.9 1.4 copy-done.3
  135.3 0.0 copy-start.4
  135.3 1.0 copy-done.4
  136.3 0.0 copy-start.6
  136.3 0.8 copy-done.6
  137.1 0.0 copy-start.8
  137.1 0.7 copy-done.8
  137.7 11.5 %table_grad.1 = (f32[8192,128]{1,0:T(8,128)}, f32[256,1024]{1,0:T(8,128)}, f32[1024,128]{1,0:T(8,128)}, f32[1,1]{1,0:T(1,128)}) custom-call(s32[64,128]{1,0:T(8,128)S(1)} %get-tuple-element.26.code_ref, f32[64,128]{1,0:T(8,128)S(1)} %copy-done.6, f32[64,128]{1,0:T(8,128)S(1)} %get-tuple-element.35.pos_ref, f32[8,128]{1,0:T(8,128)S(1)} %copy-done.8, ...), custom_call_target="tpu_custom_call" | custom-call | tf_op jit(solution)/shard_map/table_grad/pallas_call | solution.py:657
  (3 shorter events, 0.1 us)
Async XLA Ops:
  30.6 1.6 %copy-start = (bf16[8192,128]{1,0:T(8,128)(2,1)S(1)}, bf16[8192,128]{1,0:T(8,128)(2,1)}, u32[]{:S(2)}) copy-start(bf16[8192,128]{1,0:T(8,128)(2,1)} %blk_hbm.1) | copy-start | bytes 6291460
  32.1 1.6 %copy-start.1 = (bf16[1024,8,128]{2,1,0:T(8,128)(2,1)S(1)}, bf16[1024,8,128]{2,1,0:T(8,128)(2,1)}, u32[]{:S(2)}) copy-start(bf16[1024,8,128]{2,1,0:T(8,128)(2,1)} %get-tuple-element.25) | copy-start | bytes 6291460
  33.7 10.7 %copy-start.5 = (s32[64,128]{1,0:T(8,128)}, s32[64,128]{1,0:T(8,128)S(1)}, u32[]{:S(2)}) copy-start(s32[64,128]{1,0:T(8,128)S(1)} %reshape.41.tgt_ref) | copy-start | bytes 98308
  43.8 0.6 copy-start.7
  44.4 89.4 %copy-start.2 = (s32[131072]{0:T(1024)S(1)}, s32[131072]{0:T(1024)}, u32[]{:S(2)}) copy-start(s32[131072]{0:T(1024)} %param.11) | copy-start | bytes 1572868
  133.8 1.4 copy-start.3
  135.3 1.0 copy-start.4
  136.3 0.8 copy-start.6
  137.1 0.7 copy-start.8

commit v6 on v5

--- a/solution.py
+++ b/solution.py
@@ -116,38 +116,45 @@
     lax.fori_loop(0, count, add, 0, unroll=4)
 
 
-def scatter_streams(me, ref, first, rref, rbase, streams, send_sem, recv_sem, prepare=None, between=None):
-    sent = []
-    pending = [None] * 3
-    for step in range(4):
-        for s, (off, unit, order) in enumerate(streams):
-            idx = block_index(me, order)
-            if pending[s]:
-                for c in pending[s][0]:
-                    c.wait_recv()
-                add_rows(ref, pending[s][1], rref, pending[s][2], pending[s][3], 3)
-            if step == 3:
-                continue
-            if step == 0 and prepare:
-                prepare(s)
-            span = 4 ** (2 - step)
-            axis = order[2 - step]
-            start = first + off + (idx - idx % (4 * span)) * unit
-            d = coord(me, axis)
-            copies = []
-            for k in range(1, 4):
-                n = s * 9 + step * 3 + k - 1
-                src = ref.at[pl.ds(start + (d + k) % 4 * span * unit, span * unit)]
-                dst = rref.at[pl.ds(rbase + (k - 1) * span * unit, span * unit)]
-                c = remote(src, dst, send_sem.at[n], recv_sem.at[n], peer(me, axis, k))
-                c.start()
-                copies.append(c)
-            sent += copies
-            pending[s] = (copies, start + d * span * unit, rbase, span * unit)
-            rbase += 3 * span * unit
-        if step == 0 and between:
-            between()
-    return sent
+class Scatter:
+    def __init__(self, me, ref, first, rref, rbase, streams, send_sem, recv_sem):
+        self.me, self.ref, self.first, self.rref, self.rbase = me, ref, first, rref, rbase
+        self.streams, self.sems = streams, (send_sem, recv_sem)
+        self.step, self.pending, self.sent = [0] * 3, [None] * 3, []
+
+    def send(self, s):
+        off, unit, order = self.streams[s]
+        step, me = self.step[s], self.me
+        span = 4 ** (2 - step)
+        axis = order[2 - step]
+        idx = block_index(me, order)
+        start = self.first + off + (idx - idx % (4 * span)) * unit
+        d = coord(me, axis)
+        copies = []
+        for k in range(1, 4):
+            n = s * 9 + step * 3 + k - 1
+            src = self.ref.at[pl.ds(start + (d + k) % 4 * span * unit, span * unit)]
+            dst = self.rref.at[pl.ds(self.rbase + (k - 1) * span * unit, span * unit)]
+            c = remote(src, dst, self.sems[0].at[n], self.sems[1].at[n], peer(me, axis, k))
+            c.start()
+            copies.append(c)
+        self.sent += copies
+        self.pending[s] = (copies, start + d * span * unit, self.rbase, span * unit)
+        self.rbase += 3 * span * unit
+        self.step[s] += 1
+
+    def receive(self, s):
+        copies, start, base, count = self.pending[s]
+        for c in copies:
+            c.wait_recv()
+        add_rows(self.ref, start, self.rref, base, count, 3)
+
+    def rest(self):
+        for step in range(3):
+            for s in range(3):
+                self.receive(s)
+                if step < 2:
+                    self.send(s)
 
 
 def gelu_parts(a):
@@ -245,51 +252,51 @@
     half(1 - core).wait()
 
 
-def reduce_stats(me, st_ref, recv, cur, send_sem, recv_sem):
-    sent = []
-    pending = [None] * 3
-    for phase in range(5):
-        for s in range(3):
-            g0, ng = H_FIRST[s], H_UNIT[s]
-            if phase:
-                for c in pending[s]:
-                    c.wait_recv()
-                base = 8 * (0, 3, 6, 9)[phase - 1]
-                npart = len(pending[s])
-
-                def merge(g, carry, phase=phase, base=base, npart=npart):
-                    old = st_ref[g] if phase == 1 else cur[8 * (phase - 2) + g]
-                    parts = [recv[base + 8 * k + g] for k in range(npart)]
-                    top, z = old[0], old[2]
-                    for p in parts:
-                        top = jnp.maximum(top, p[0])
-                        z = jnp.maximum(z, p[2])
-                    total = old[1] * jnp.exp(old[0] - top)
-                    for p in parts:
-                        total = total + p[1] * jnp.exp(p[0] - top)
-                    row = 8 * (phase - 1) + g
-                    cur[row, 0] = top
-                    cur[row, 1] = total
-                    cur[row, 2] = z
-                    return carry
-
-                lax.fori_loop(g0, g0 + ng, merge, 0)
-            if phase == 4:
-                continue
-            axis = (ORDERS[s] + ("core",))[phase]
-            src = st_ref.at[pl.ds(g0, ng)] if phase == 0 else cur.at[pl.ds(8 * (phase - 1) + g0, ng)]
-            base = 8 * (0, 3, 6, 9)[phase]
-            pending[s] = []
-            for k in range(1, COORD[axis][1]):
-                n = s * NPEER + phase * 3 + k - 1
-                c = remote(src, recv.at[pl.ds(base + 8 * (k - 1) + g0, ng)], send_sem.at[n], recv_sem.at[n], peer(me, axis, k))
-                c.start()
-                pending[s].append(c)
-                sent.append(c)
-    return sent
-
-
-TILE = KILO
+class Stats:
+    def __init__(self, me, recv, cur, send_sem, recv_sem):
+        self.me, self.recv, self.cur, self.sems = me, recv, cur, (send_sem, recv_sem)
+        self.phase, self.pending, self.sent = [0] * 3, [None] * 3, []
+
+    def send(self, s):
+        phase, g0, ng = self.phase[s], H_FIRST[s], H_UNIT[s]
+        axis = (ORDERS[s] + ("core",))[phase]
+        src = self.cur.at[pl.ds(8 * phase + g0, ng)]
+        self.pending[s] = []
+        for k in range(1, COORD[axis][1]):
+            n = s * NPEER + phase * 3 + k - 1
+            dst = self.recv.at[pl.ds(8 * (3 * phase + k - 1) + g0, ng)]
+            c = remote(src, dst, self.sems[0].at[n], self.sems[1].at[n], peer(self.me, axis, k))
+            c.start()
+            self.pending[s].append(c)
+        self.sent += self.pending[s]
+
+    def receive(self, s):
+        phase, cur, recv, npart = self.phase[s], self.cur, self.recv, len(self.pending[s])
+        for c in self.pending[s]:
+            c.wait_recv()
+
+        def merge(g, carry):
+            old = cur[8 * phase + g]
+            parts = [recv[8 * (3 * phase + k) + g] for k in range(npart)]
+            top, z = old[0], old[2]
+            for p in parts:
+                top = jnp.maximum(top, p[0])
+                z = jnp.maximum(z, p[2])
+            total = old[1] * jnp.exp(old[0] - top)
+            for p in parts:
+                total = total + p[1] * jnp.exp(p[0] - top)
+            row = 8 * (phase + 1) + g
+            cur[row, 0] = top
+            cur[row, 1] = total
+            cur[row, 2] = z
+            return carry
+
+        lax.fori_loop(H_FIRST[s], H_FIRST[s] + H_UNIT[s], merge, 0)
+        self.phase[s] += 1
+
+    def advance(self, s):
+        self.receive(s)
+        self.send(s)
 
 
 def target_kernel(tgt_ref, h_hbm, blk_hbm, zst_ref, pos_ref, code_ref, hc_ref, te_out, h_ref, blk_ref, te_ref, zd, hs, es, codes, load_sem, sem):
@@ -322,8 +329,8 @@
     sub = iota((16, LANE), 0)
 
     def one_row(ref, i):
-        tile = ref[pl.ds(pl.multiple_of(i // 16 * 16, 16), 16), :].astype(F32)
-        return down(jnp.where(sub == i % 16, tile, 0.0))
+        tile = ref[pl.ds(pl.multiple_of(i & -16, 16), 16), :].astype(F32)
+        return down(jnp.where(sub == (i & 15), tile, 0.0))
 
     def chunk(c, carry):
         slot = slot0 + (c * LANE).astype(F32)
@@ -346,10 +353,11 @@
             for u in range(8):
                 n = i * 8 + u
                 v = codes[0, n]
-                hs[one(n), :] = one_row(h_ref, v % ALL)
-                row = one_row(blk_ref, v // ALL)
+                tok, at = v & (ALL - 1), lax.shift_right_logical(v, 13)
+                hs[one(n), :] = one_row(h_ref, tok)
+                row = one_row(blk_ref, at)
                 es[one(n), :] = row
-                te_ref[one(jnp.where(n < left, v % ALL, ALL)), :] = row
+                te_ref[one(jnp.where(n < left, tok, ALL)), :] = row
             return carry2
 
         lax.fori_loop(0, (jnp.minimum(left, LANE) + 7) // 8, fetch, 0)
@@ -391,12 +399,11 @@
     base = me * ALL
 
     def place(i, carry):
-        for u in range(8):
-            n = i * 8 + u
-            de_ref[one(cidx[i // 16, i % 16 * 8 + u] - base), :] = dcand[one(n), :]
-        return carry
-
-    lax.fori_loop(0, dcand.shape[0] // 8, place, 0)
+        for u in range(32):
+            de_ref[one(cidx[lax.shift_right_logical(i, 2), (i & 3) * 32 + u] - base), :] = dcand[one(i * 32 + u), :]
+        return carry
+
+    lax.fori_loop(0, 32, place, 0)
     count = jnp.sum(flag(pos_ref[...] >= 0.0)).astype(jnp.int32)
     slot0 = iota((LANE, LANE), 0).astype(F32)
 
@@ -413,7 +420,7 @@
         gh[...] = g * hc[...]
 
         def put(i, carry2):
-            de_ref[one(code_ref[c, i] // ALL), :] += gh[one(i), :]
+            de_ref[one(lax.shift_right_logical(code_ref[c, i], 13)), :] += gh[one(i), :]
             return carry2
 
         lax.fori_loop(0, jnp.minimum(count - c * LANE, LANE), put, 0)
@@ -439,7 +446,7 @@
 
 
 def grad_kernel(tgt_ref, zst_ref, h_hbm, cand_hbm, cidb_hbm, logqb_hbm, candt_hbm, te_hbm, x_hbm, wout_hbm, pre_hbm, g_ref, loss_ref, tiles_out, dcand_out,
-                ebuf, mc_ref, st_ref, part, local, srecv, cur, norm, acc, recv, tiles, trecv, whole, dcand_ref,
+                ebuf, mc_ref, part, local, total, srecv, cur, norm, acc, recv, tiles, trecv, whole, dcand_ref,
                 h_ref, cand_ref, cidb, logqb, candt_ref, te_ref, x_ref, wout_ref, pre_ref,
                 load_sem, core_send, core_recv, send_sem, recv_sem):
     me = lax.axis_index("dp")
@@ -453,7 +460,8 @@
     barrier = greet(me)
     local[...] = (tgt_ref[...] - me * ALL).astype(F32)
     for g in range(8):
-        st_ref[g, 2] = zst_ref[8 * g : 8 * g + 8, :]
+        for half in range(2):
+            cur[g, 2, 4 * half : 4 * half + 4, :] = zst_ref[32 * half + 4 * g : 32 * half + 4 * g + 4, :]
     for c in loads[:4]:
         c.wait()
 
@@ -475,23 +483,36 @@
                     part[q, c : c + 1, :] = down(e)
                 most = mc_ref[r]
                 top = peak(most)
-                row = one(t % 2 * 4 + q)
-                st_ref[t // 2, 0, row, :] = top
-                st_ref[t // 2, 1, row, :] = down(part[q] * jnp.exp(most - top))
-        return carry
-
-    lax.fori_loop(0, 16, score, 0)
-    pl.semaphore_wait(barrier, NPEER)
-    sent = reduce_stats(me, st_ref, srecv, cur, send_sem.at[3], recv_sem.at[3])
-    total = jnp.zeros((8, LANE), F32)
-    for g in range(8):
-        m, t, z = cur[24 + g, 0], cur[24 + g, 1], cur[24 + g, 2]
-        top = jnp.maximum(m, z)
-        log_norm = top + jnp.log(t * jnp.exp(m - top) + jnp.exp(z - top))
-        total = total + (log_norm - z)
-        norm[8 * g : 8 * g + 8, :] = log_norm
-        g_ref[8 * g : 8 * g + 8, :] = (jnp.exp(z - log_norm) - 1.0) / ALL
-    loss_ref[...] = jnp.broadcast_to(jnp.sum(total, keepdims=True) / ALL, loss_ref.shape)
+                row = one(t // 8 * 4 + q)
+                cur[t % 8, 0, row, :] = top
+                cur[t % 8, 1, row, :] = down(part[q] * jnp.exp(most - top))
+        return carry
+
+    def part_loop(s, base, body):
+        lax.fori_loop(base + H_FIRST[s], base + H_FIRST[s] + H_UNIT[s], body, 0)
+
+    def score_part(s):
+        part_loop(s, 0, score)
+        part_loop(s, 8, score)
+
+    def finish(s):
+        stats.receive(s)
+
+        def norms(g, carry):
+            m, t, z = cur[32 + g, 0], cur[32 + g, 1], cur[32 + g, 2]
+            top = jnp.maximum(m, z)
+            log_norm = top + jnp.log(t * jnp.exp(m - top) + jnp.exp(z - top))
+            grad = (jnp.exp(z - log_norm) - 1.0) / ALL
+            total[...] += log_norm - z
+            for half in range(2):
+                rows = pl.ds(32 * half + 4 * g, 4)
+                norm[rows, :] = log_norm[4 * half : 4 * half + 4, :]
+                g_ref[rows, :] = grad[4 * half : 4 * half + 4, :]
+            return carry
+
+        part_loop(s, 0, norms)
+
+    total[...] = jnp.zeros_like(total)
 
     def probs(t):
         blocks = []
@@ -502,9 +523,6 @@
                 (ebuf[t, LANE * c : LANE * c + LANE, LANE * q : LANE * q + LANE] * scale[c : c + 1, :]).astype(BF16) for c in range(8)], axis=0))
         return jnp.concatenate(blocks, axis=1)
 
-    for c in loads[4:]:
-        c.wait()
-
     def query_grad(t):
         dqt = jnp.dot(candt_ref[...], probs(t), preferred_element_type=F32)
         gcol = jnp.concatenate([column(g_ref[one(t * 4 + q), :]) for q in range(4)], axis=0)
@@ -527,11 +545,6 @@
         acc[pl.ds(t * TOK, TOK)] = val + recv[pl.ds(i * TOK, TOK)]
         return carry
 
-    lax.fori_loop(0, 8, give, 0)
-
-    def prepare(s):
-        lax.fori_loop(H_FIRST[s], H_FIRST[s] + H_UNIT[s], keep, 0)
-
     def cand_grad():
         dcand_ref[...] = jnp.zeros_like(dcand_ref)
 
@@ -544,7 +557,44 @@
 
     dcand_copy = pltpu.make_async_copy(dcand_ref, dcand_out, load_sem.at[9])
     streams = [(H_OFF[s], H_UNIT[s], ORDERS[s]) for s in range(3)]
-    sent += scatter_streams(me, acc, core * 512, recv, 512, streams, send_sem.at[0], recv_sem.at[0], prepare, cand_grad)
+    scatter = Scatter(me, acc, core * 512, recv, 512, streams, send_sem.at[0], recv_sem.at[0])
+    stats = Stats(me, srecv, cur, send_sem.at[3], recv_sem.at[3])
+    a, b, c = range(3)
+
+    def keep_part(s):
+        part_loop(s, 0, keep)
+        scatter.send(s)
+
+    score_part(a)
+    pl.semaphore_wait(barrier, NPEER)
+    stats.send(a)
+    score_part(b)
+    stats.advance(a)
+    stats.send(b)
+    score_part(c)
+    stats.advance(a)
+    stats.advance(b)
+    stats.send(c)
+    for s in (a, b, c):
+        stats.advance(s)
+    finish(a)
+    for load in loads[4:]:
+        load.wait()
+    part_loop(a, 0, give)
+    stats.advance(b)
+    stats.advance(c)
+    keep_part(a)
+    finish(b)
+    part_loop(b, 0, give)
+    stats.advance(c)
+    keep_part(b)
+    finish(c)
+    part_loop(c, 0, give)
+    keep_part(c)
+    loss_ref[...] = jnp.broadcast_to(jnp.sum(total[...], keepdims=True) / ALL, loss_ref.shape)
+    cand_grad()
+    scatter.rest()
+    sent = stats.sent + scatter.sent
     rows = []
     for s in range(3):
         idx = block_index(me, ORDERS[s])
@@ -560,7 +610,11 @@
         tiles[LANE + 32 * j : 160 + 32 * j] = dw_in[:, LANE * j : LANE * j + LANE].reshape(32, 8, LANE)
     streams = [(TOK * s, 1, ORDERS[s]) for s in range(3)]
     half = core_exchange(me, tiles, 192, trecv, send_sem.at[1, LAST], recv_sem.at[1, LAST])
-    sent += half + scatter_streams(me, tiles, core * 192, trecv, 192, streams, send_sem.at[1], recv_sem.at[1])
+    scatter = Scatter(me, tiles, core * 192, trecv, 192, streams, send_sem.at[1], recv_sem.at[1])
+    for s in range(3):
+        scatter.send(s)
+    scatter.rest()
+    sent += half + scatter.sent
     streams = []
     for s in range(3):
         own = core * 192 + TOK * s + block_index(me, ORDERS[s])
@@ -625,7 +679,7 @@
             t5[..., 48:TOK].reshape(2, -1)], axis=1).reshape(TOK, LANE)
         smem = pl.BlockSpec(memory_space=pltpu.SMEM)
         square = pltpu.VMEM((LANE, LANE), F32)
-        big = pltpu.CompilerParams(vmem_limit_bytes=48 * KILO * KILO)
+        big = pltpu.CompilerParams(vmem_limit_bytes=63 * KILO * KILO)
         zst, pos, codes, hc, te = pl.pallas_call(
             target_kernel,
             out_shape=[
@@ -644,8 +698,8 @@
                 jax.ShapeDtypeStruct((384, 8, LANE), F32), jax.ShapeDtypeStruct((cand_dev, LANE), F32)],
             in_specs=vmem(2) + [anyspec] * 9, out_specs=vmem(2) + [anyspec] * 2,
             scratch_shapes=[
-                pltpu.VMEM((16, cand_dev, PART), F32), pltpu.VMEM((TOK, 8, LANE), F32), pltpu.VMEM((8, 3, 8, LANE), F32), pltpu.VMEM((4, 8, LANE), F32), pltpu.VMEM((TOK, LANE), F32),
-                pltpu.VMEM((80, 3, 8, LANE), F32), pltpu.VMEM((32, 3, 8, LANE), F32), pltpu.VMEM((TOK, LANE), F32),
+                pltpu.VMEM((16, cand_dev, PART), F32), pltpu.VMEM((TOK, 8, LANE), F32), pltpu.VMEM((4, 8, LANE), F32), pltpu.VMEM((TOK, LANE), F32), pltpu.VMEM((8, LANE), F32),
+                pltpu.VMEM((80, 3, 8, LANE), F32), pltpu.VMEM((40, 3, 8, LANE), F32), pltpu.VMEM((TOK, LANE), F32),
                 pltpu.VMEM((KILO, 8, LANE), F32), pltpu.VMEM((KILO, 8, LANE), F32),
                 pltpu.VMEM((384, 8, LANE), F32), pltpu.VMEM((384, 8, LANE), F32), pltpu.VMEM((384, 8, LANE), F32), pltpu.VMEM((cand_dev, LANE), F32),
                 pltpu.VMEM((tok_total, LANE), BF16), pltpu.VMEM((cand_dev, LANE), BF16), pltpu.VMEM((cand_dev, LANE), F32), pltpu.VMEM((cand_dev, LANE), F32),

time: 148 us -> 138 us (0.932)
  local copies, waits for them, and re-layouts: 10.8 us -> 3.74 us
  Pallas kernels: 138 us -> 133 us
    unnamed x18 -> x0, local copies, waits for them, and re-layouts: 7.68 us -> none
    pallas_call x1, Pallas kernels: 89.4 us -> 85 us  [local_step(): pl.pallas_call(grad_kernel, out_shape=[jax.ShapeDtypeStruct((TOK, LANE),...]
where the time goes in v6:
time: 138 us
  Pallas kernels  133 us (96%)
  local copies, waits for them, and re-layouts  3.74 us (3%)
    pallas_call x1, Pallas kernels, local_step(): pl.pallas_call(grad_kernel, out_shape=[jax.ShapeDtypeStruct((TOK, LANE),...  85 us
    pallas_call x1, Pallas kernels, local_step(): pl.pallas_call(query_kernel, out_shape=[jax.ShapeDtypeStruct((LANE, 1, TO...  26.7 us
    pallas_call x1, Pallas kernels, local_step(): pl.pallas_call(table_kernel, out_shape=[jax.ShapeDtypeStruct((block_rows,...  10.9 us
    pallas_call x1, Pallas kernels, local_step(): pl.pallas_call(target_kernel, out_shape=[jax.ShapeDtypeStruct((TOK, LANE)...  10.7 us

profile of v6, /device:TPU:1, one launch (start us, length us, event | category | flops | bytes accessed | tf_op | source)
XLA Modules:
  0.0 138.0 jit_solution(5691738521799894095)
XLA Ops:
  0.6 26.7 %query_gather.1 = (s32[128,1,64]{2,1,0:T(1,128)}, bf16[1024,8,128]{2,1,0:T(8,128)(2,1)}, f32[64,1024]{1,0:T(8,128)}, bf16[1024,128]{1,0:T(8,128)(2,1)}, bf16[128...) custom-call(bf16[64,256]{1,0:T(8,128)(2,1)} %x_hbm.1, bf16[256,1024]{1,0:T(8,128)(2,1)} %win_ref.1, ...), custom_call_target="tpu_custom_call" | custom-call | tf_op jit(solution)/shard_map/query_gather/pallas_call | solution.py:660
  27.4 0.9 slice.14
  28.3 0.1 reshape.40
  28.4 0.9 copy.11
  29.3 0.1 reshape.38
  29.4 0.9 slice.13
  30.4 0.1 reshape.39
  30.5 0.6 reshape.41.tgt_ref
  31.2 10.7 %target_rows.1 = (f32[64,128]{1,0:T(8,128)}, f32[64,128]{1,0:T(8,128)}, s32[64,128]{1,0:T(8,128)}, f32[8192,128]{1,0:T(8,128)}, f32[8192,128]{1,0:T(8,128)}) custom-call(s32[64,128]{1,0:T(8,128)} %reshape.41.tgt_ref, bf16[8192,128]{1,0:T(8,128)(2,1)} %bitcast.11, bf16[8192,128]{1,0:T(8,128)(2,1)} %blk_hbm.1), custom_call_target="tpu_custom_call" | custom-call | tf_op jit(solution)/shard_map/target_rows/pallas_call | solution.py:683
  41.9 85.0 %grad_reduce.1 = (f32[64,128]{1,0:T(8,128)}, f32[8,128]{1,0:T(8,128)}, f32[384,8,128]{2,1,0:T(8,128)}, f32[1024,128]{1,0:T(8,128)}) custom-call(s32[64,128]{1,0:T(8,128)} %reshape.41.tgt_ref, f32[64,128]{1,0:T(8,128)} %get-tuple-element.27.zst_ref, bf16[8192,128]{1,0:T(8,128)(2,1)} %bitcast.12, bf16[1024,128]{1,0:T(8,128)(2,1)} %get-tuple-element.28.cand_hbm, ...), custom_call_target="tpu_custom_call" | custom-call | tf_op jit(solution)/shard_map/grad_reduce/pallas_call | solution.py:694
  126.9 10.9 %table_grad.1 = (f32[8192,128]{1,0:T(8,128)}, f32[256,1024]{1,0:T(8,128)}, f32[1024,128]{1,0:T(8,128)}, f32[1,1]{1,0:T(1,128)}) custom-call(s32[64,128]{1,0:T(8,128)} %get-tuple-element.26.code_ref, f32[64,128]{1,0:T(8,128)} %get-tuple-element.34.g_ref, f32[64,128]{1,0:T(8,128)} %get-tuple-element.35.pos_ref, f32[8,128]{1,0:T(8,128)} %get-tuple-element.36.lossrow_ref, ...), custom_call_target="tpu_custom_call" | custom-call | tf_op jit(solution)/shard_map/table_grad/pallas_call | solution.py:711
  (2 shorter events, 0.0 us)

commit v7 on v6

--- a/solution.py
+++ b/solution.py
@@ -17,6 +17,10 @@
 
 def one(i):
     return pl.ds(i, 1)
+
+
+def repeat(n, body, unroll=1):
+    lax.fori_loop(0, n, body, 0, unroll=unroll)
 
 
 def down(v):
@@ -190,7 +194,7 @@
         pltpu.make_async_copy(blk_ref, blk, load_sem.at[2])]
     for c in loads:
         c.start()
-    pl.semaphore_wait(greet(me), NPEER)
+    barrier = greet(me)
     pre = jnp.dot(x_ref[...], win_ref[...], preferred_element_type=F32)
     pre_ref[...] = pre
     act = gelu_parts(pre)[0].astype(BF16)
@@ -206,6 +210,7 @@
     tall_ref[core * TOK + block_index(me, ORDERS[2])] = tgt_ref[...]
     streams.append((tall_ref, core * TOK, 1, ORDERS[2]))
     lane = iota((1, LANE), 1)
+    pl.semaphore_wait(barrier, NPEER)
 
     def pick(n, carry):
         part = pl.ds(pl.multiple_of(n // 8 * WIDE, WIDE), WIDE)
@@ -299,12 +304,50 @@
         self.send(s)
 
 
-def target_kernel(tgt_ref, h_hbm, blk_hbm, zst_ref, pos_ref, code_ref, hc_ref, te_out, h_ref, blk_ref, te_ref, zd, hs, es, codes, load_sem, sem):
+def arrange(tall_ref, square, tok_ref):
+    def row(b, carry):
+        square[one(b), :] = tall_ref[b]
+        return carry
+
+    repeat(LANE, row)
+    ids = square[...]
+    pieces = jnp.concatenate([lax.shift_right_logical(ids, 14), lax.shift_right_logical(ids, 7) & 127, ids & 127], axis=0).astype(F32).astype(BF16)
+    b = iota((LANE, 1), 0)
+    bt = iota((1, LANE), 1)
+
+    def place(v, s):
+        c = [lax.shift_right_logical(v, n) & 3 for n in (0, 2, 4)]
+        z, x, y = c
+        first, second, third = ((x, y, z), (y, z, x), (z, x, y))[s]
+        return (v & TOK) + first + 4 * second + 16 * third
+
+    for s in range(3):
+        width, per = 8 * H_UNIT[s], (16, 16, 8)[s]
+        span = width * per
+        pick = iota((TOK, span), 0) == iota((TOK, span), 1) % width + 8 * H_FIRST[s]
+        lanes = jnp.dot(pieces, flag(pick).astype(BF16), preferred_element_type=F32)
+        mask = place(b, s) % per == iota((LANE, span), 1) // width
+        group = flag(place(bt, s) // per == iota((LANE // per, LANE), 0)).astype(BF16)
+        got = [
+            jnp.dot(group, jnp.where(mask, lanes[LANE * p : LANE * p + LANE, :], 0.0).astype(BF16), preferred_element_type=F32).astype(jnp.int32)
+            for p in range(3)]
+        full = (got[0] * LANE + got[1]) * LANE + got[2]
+        rows = span // LANE
+        for a in range(LANE // per):
+            half, rest = divmod(a, TOK // per)
+            for r in range(rows):
+                at = 32 * half + H_OFF[s] // 16 + rest * rows + r
+                tok_ref[at : at + 1, :] = full[a : a + 1, LANE * r : LANE * r + LANE]
+
+
+def target_kernel(tall_ref, h_hbm, blk_hbm, zst_ref, pos_ref, code_ref, local_ref, hc_ref, te_out, h_ref, blk_ref, te_ref, zd, hs, es, square, tgt_ref, codes, load_sem, sem):
     block_rows = blk_ref.shape[0]
     loads = [pltpu.make_async_copy(h_hbm, h_ref, load_sem.at[0]), pltpu.make_async_copy(blk_hbm, blk_ref, load_sem.at[1])]
     for c in loads:
         c.start()
+    arrange(tall_ref, square, tgt_ref)
     rel = tgt_ref[...] - lax.axis_index("dp") * block_rows
+    local_ref[...] = rel.astype(F32)
     own = (rel >= 0) & (rel < block_rows)
     own_f = flag(own)
     own_b = own_f.astype(BF16)
@@ -320,10 +363,8 @@
         te_ref[pl.ds(pl.multiple_of(i * LANE, LANE), LANE), :] = jnp.zeros((LANE, LANE), F32)
         return carry
 
-    lax.fori_loop(0, TOK, clear, 0)
+    repeat(TOK, clear)
     count = jnp.sum(own_f).astype(jnp.int32)
-    for c in loads:
-        c.wait()
     slot0 = iota((LANE, LANE), 0).astype(F32)
     lane = iota((1, LANE), 1)
     sub = iota((16, LANE), 0)
@@ -332,7 +373,7 @@
         tile = ref[pl.ds(pl.multiple_of(i & -16, 16), 16), :].astype(F32)
         return down(jnp.where(sub == (i & 15), tile, 0.0))
 
-    def chunk(c, carry):
+    def compact(c, carry):
         slot = slot0 + (c * LANE).astype(F32)
 
         def collect(r, code):
@@ -344,15 +385,24 @@
         tok = across((code % ALL).astype(F32))
         both = row.astype(jnp.int32) * ALL + tok.astype(jnp.int32)
         code_ref[one(c), :] = jnp.transpose(jnp.broadcast_to(both, (LANE, LANE)))[0:1, :]
-        copy = pltpu.make_async_copy(code_ref.at[one(c)], codes, sem)
-        copy.start()
-        copy.wait()
+        return carry
+
+    chunks = (count + 127) // LANE
+    repeat(chunks, compact)
+    copy = pltpu.make_async_copy(code_ref, codes, sem)
+    copy.start()
+    for c in loads:
+        c.wait()
+    copy.wait()
+
+    def chunk(c, carry):
+        slot = slot0 + (c * LANE).astype(F32)
         left = count - c * LANE
 
         def fetch(i, carry2):
             for u in range(8):
                 n = i * 8 + u
-                v = codes[0, n]
+                v = codes[c, n]
                 tok, at = v & (ALL - 1), lax.shift_right_logical(v, 13)
                 hs[one(n), :] = one_row(h_ref, tok)
                 row = one_row(blk_ref, at)
@@ -360,7 +410,7 @@
                 te_ref[one(jnp.where(n < left, tok, ALL)), :] = row
             return carry2
 
-        lax.fori_loop(0, (jnp.minimum(left, LANE) + 7) // 8, fetch, 0)
+        repeat((jnp.minimum(left, LANE) + 7) // 8, fetch)
         keep = pltpu.make_async_copy(hs, hc_ref.at[pl.ds(pl.multiple_of(c * LANE, LANE), LANE)], load_sem.at[3])
         keep.start()
         z = jnp.broadcast_to(across(hs[...] * es[...]), (LANE, LANE))
@@ -370,11 +420,11 @@
             zd[one(r), :] += down(jnp.where(hit, z, 0.0))
             return carry2
 
-        lax.fori_loop(0, TOK, spread, 0, unroll=8)
+        repeat(TOK, spread, 8)
         keep.wait()
         return carry
 
-    lax.fori_loop(0, (count + 127) // LANE, chunk, 0)
+    repeat(chunks, chunk)
     copy = pltpu.make_async_copy(te_ref.at[pl.ds(0, ALL)], te_out, load_sem.at[2])
     copy.start()
     zst_ref[...] = jnp.where(pos_ref[...] >= 0.0, zd[...], -jnp.inf)
@@ -392,7 +442,7 @@
         de_ref[pl.ds(pl.multiple_of(i * LANE, LANE), LANE), :] = jnp.zeros((LANE, LANE), F32)
         return carry
 
-    lax.fori_loop(0, de_ref.shape[0] // LANE, clear, 0)
+    repeat(de_ref.shape[0] // LANE, clear)
     for c in loads:
         c.wait()
 
@@ -403,7 +453,7 @@
             de_ref[one(cidx[lax.shift_right_logical(i, 2), (i & 3) * 32 + u] - base), :] = dcand[one(i * 32 + u), :]
         return carry
 
-    lax.fori_loop(0, 32, place, 0)
+    repeat(32, place)
     count = jnp.sum(flag(pos_ref[...] >= 0.0)).astype(jnp.int32)
     slot0 = iota((LANE, LANE), 0).astype(F32)
 
@@ -423,10 +473,10 @@
             de_ref[one(lax.shift_right_logical(code_ref[c, i], 13)), :] += gh[one(i), :]
             return carry2
 
-        lax.fori_loop(0, jnp.minimum(count - c * LANE, LANE), put, 0)
-        return carry
-
-    lax.fori_loop(0, (count + 127) // LANE, chunk, 0)
+        repeat(jnp.minimum(count - c * LANE, LANE), put)
+        return carry
+
+    repeat((count + 127) // LANE, chunk)
     dwout_ref[...] = whole[0:LANE].reshape(KILO, LANE)
     for j in range(8):
         dwin_ref[:, LANE * j : LANE * j + LANE] = whole[LANE + 32 * j : 160 + 32 * j].reshape(WIDE, LANE)
@@ -445,8 +495,8 @@
     return [c]
 
 
-def grad_kernel(tgt_ref, zst_ref, h_hbm, cand_hbm, cidb_hbm, logqb_hbm, candt_hbm, te_hbm, x_hbm, wout_hbm, pre_hbm, g_ref, loss_ref, tiles_out, dcand_out,
-                ebuf, mc_ref, part, local, total, srecv, cur, norm, acc, recv, tiles, trecv, whole, dcand_ref,
+def grad_kernel(local, zst_ref, h_hbm, cand_hbm, cidb_hbm, logqb_hbm, candt_hbm, te_hbm, x_hbm, wout_hbm, pre_hbm, g_ref, loss_ref, tiles_out, dcand_out,
+                ebuf, mc_ref, part, total, srecv, cur, norm, acc, recv, tiles, trecv, whole, dcand_ref,
                 h_ref, cand_ref, cidb, logqb, candt_ref, te_ref, x_ref, wout_ref, pre_ref,
                 load_sem, core_send, core_recv, send_sem, recv_sem):
     me = lax.axis_index("dp")
@@ -458,7 +508,6 @@
     for c in loads:
         c.start()
     barrier = greet(me)
-    local[...] = (tgt_ref[...] - me * ALL).astype(F32)
     for g in range(8):
         for half in range(2):
             cur[g, 2, 4 * half : 4 * half + 4, :] = zst_ref[32 * half + 4 * g : 32 * half + 4 * g + 4, :]
@@ -552,7 +601,7 @@
             dcand_ref[...] += jnp.dot(probs(t), h_ref[pl.ds(pl.multiple_of(t * PART, PART), PART), :], preferred_element_type=F32)
             return carry
 
-        lax.fori_loop(0, 16, accumulate, 0)
+        repeat(16, accumulate)
         dcand_copy.start()
 
     dcand_copy = pltpu.make_async_copy(dcand_ref, dcand_out, load_sem.at[9])
@@ -631,7 +680,7 @@
         swap(i).wait_send()
         return carry
 
-    lax.fori_loop(0, 8, swap_done, 0)
+    repeat(8, swap_done)
     tiles_copy.wait()
 
 
@@ -672,25 +721,20 @@
             compiler_params=params(0), name="query_gather",
         )(features, w_in, w_out, targets[None, :], table_blk, cid_rows, logq_rows)
         query_all = h_all.reshape(ALL, LANE)
-        t5 = tall.reshape(2, 4, 4, 4, TOK)
-        tgt_all = jnp.concatenate([
-            t5.transpose(0, 3, 1, 2, 4)[..., 0:24].reshape(2, -1),
-            t5.transpose(0, 2, 3, 1, 4)[..., 24:48].reshape(2, -1),
-            t5[..., 48:TOK].reshape(2, -1)], axis=1).reshape(TOK, LANE)
         smem = pl.BlockSpec(memory_space=pltpu.SMEM)
         square = pltpu.VMEM((LANE, LANE), F32)
         big = pltpu.CompilerParams(vmem_limit_bytes=63 * KILO * KILO)
-        zst, pos, codes, hc, te = pl.pallas_call(
+        zst, pos, codes, local, hc, te = pl.pallas_call(
             target_kernel,
             out_shape=[
-                jax.ShapeDtypeStruct((TOK, LANE), F32), jax.ShapeDtypeStruct((TOK, LANE), F32), jax.ShapeDtypeStruct((TOK, LANE), jnp.int32),
+                jax.ShapeDtypeStruct((TOK, LANE), F32), jax.ShapeDtypeStruct((TOK, LANE), F32), jax.ShapeDtypeStruct((TOK, LANE), jnp.int32), jax.ShapeDtypeStruct((TOK, LANE), F32),
                 jax.ShapeDtypeStruct((tok_total, LANE), F32), jax.ShapeDtypeStruct((tok_total, LANE), F32)],
-            in_specs=vmem(1) + [anyspec] * 2, out_specs=vmem(3) + [anyspec] * 2,
+            in_specs=vmem(1) + [anyspec] * 2, out_specs=vmem(4) + [anyspec] * 2,
             scratch_shapes=[
                 pltpu.VMEM((tok_total, LANE), BF16), pltpu.VMEM((block_rows, LANE), BF16), pltpu.VMEM((tok_total + 8, LANE), F32), pltpu.VMEM((TOK, LANE), F32),
-                square, square, pltpu.SMEM((1, LANE), jnp.int32), dma(4), pltpu.SemaphoreType.DMA],
+                square, square, pltpu.VMEM((LANE, TOK), jnp.int32), pltpu.VMEM((TOK, LANE), jnp.int32), pltpu.SMEM((TOK, LANE), jnp.int32), dma(4), pltpu.SemaphoreType.DMA],
             compiler_params=big, name="target_rows",
-        )(tgt_all, query_all, table_blk)
+        )(tall, query_all, table_blk)
         grad_tgt, loss_row, tiles, dcand = pl.pallas_call(
             grad_kernel,
             out_shape=[
@@ -698,7 +742,7 @@
                 jax.ShapeDtypeStruct((384, 8, LANE), F32), jax.ShapeDtypeStruct((cand_dev, LANE), F32)],
             in_specs=vmem(2) + [anyspec] * 9, out_specs=vmem(2) + [anyspec] * 2,
             scratch_shapes=[
-                pltpu.VMEM((16, cand_dev, PART), F32), pltpu.VMEM((TOK, 8, LANE), F32), pltpu.VMEM((4, 8, LANE), F32), pltpu.VMEM((TOK, LANE), F32), pltpu.VMEM((8, LANE), F32),
+                pltpu.VMEM((16, cand_dev, PART), F32), pltpu.VMEM((TOK, 8, LANE), F32), pltpu.VMEM((4, 8, LANE), F32), pltpu.VMEM((8, LANE), F32),
                 pltpu.VMEM((80, 3, 8, LANE), F32), pltpu.VMEM((40, 3, 8, LANE), F32), pltpu.VMEM((TOK, LANE), F32),
                 pltpu.VMEM((KILO, 8, LANE), F32), pltpu.VMEM((KILO, 8, LANE), F32),
                 pltpu.VMEM((384, 8, LANE), F32), pltpu.VMEM((384, 8, LANE), F32), pltpu.VMEM((384, 8, LANE), F32), pltpu.VMEM((cand_dev, LANE), F32),
@@ -707,7 +751,7 @@
                 pltpu.VMEM(features.shape, BF16), pltpu.VMEM(w_out.shape, BF16), pltpu.VMEM(pre.shape, F32),
                 dma(11), dma(8), dma(8), dma(4, 3 * NPEER), dma(4, 3 * NPEER)],
             compiler_params=params(1), name="grad_reduce",
-        )(tgt_all, zst, query_all, cand_rows, cidb, logqb, cand_t, te, features, w_out, pre)
+        )(local, zst, query_all, cand_rows, cidb, logqb, cand_t, te, features, w_out, pre)
         grad_blk, grad_w_in, grad_w_out, loss = pl.pallas_call(
             table_kernel,
             out_shape=[

time: 138 us -> 134 us (0.971)
  local copies, waits for them, and re-layouts: 3.74 us -> 0 us
    slice x4 -> x0, local copies, waits for them, and re-layouts: 2.75 us -> none  [the longest x2 0.96 us: local_step(): t5.transpose(0, 2, 3, 1, 4)[..., 24:48].reshape(2, -1)]
where the time goes in v7:
time: 134 us; the launch traced here: 135 us
  Pallas kernels  134 us (100%)
    pallas_call x1, Pallas kernels, local_step(): pl.pallas_call(grad_kernel, out_shape=[jax.ShapeDtypeStruct((TOK, LANE),...  85.6 us
    pallas_call x1, Pallas kernels, local_step(): pl.pallas_call(query_kernel, out_shape=[jax.ShapeDtypeStruct((LANE, 1, TO...  26.3 us
    pallas_call x1, Pallas kernels, local_step(): pl.pallas_call(target_kernel, out_shape=[jax.ShapeDtypeStruct((TOK, LANE)...  11.1 us
    pallas_call x1, Pallas kernels, local_step(): pl.pallas_call(table_kernel, out_shape=[jax.ShapeDtypeStruct((block_rows,...  10.9 us

profile of v7, /device:TPU:1, one launch (start us, length us, event | category | flops | bytes accessed | tf_op | source)
XLA Modules:
  0.0 134.8 jit_solution(18149376405784086381)
XLA Ops:
  0.6 26.3 %query_gather.1 = (s32[128,1,64]{2,1,0:T(1,128)}, bf16[1024,8,128]{2,1,0:T(8,128)(2,1)}, f32[64,1024]{1,0:T(8,128)}, bf16[1024,128]{1,0:T(8,128)(2,1)}, bf16[128...) custom-call(bf16[64,256]{1,0:T(8,128)(2,1)} %x_hbm.1, bf16[256,1024]{1,0:T(8,128)(2,1)} %win_ref.1, ...), custom_call_target="tpu_custom_call" | custom-call | tf_op jit(solution)/shard_map/query_gather/pallas_call | solution.py:709
  27.0 11.1 %target_rows.1 = (f32[64,128]{1,0:T(8,128)}, f32[64,128]{1,0:T(8,128)}, s32[64,128]{1,0:T(8,128)}, f32[64,128]{1,0:T(8,128)}, f32[8192,128]{1,0:T(8,128)}, /*index=5*/f32[8192,128]{1,0:T(8,128)}) custom-call(s32[128,1,64]{2,1,0:T(1,128)} %get-tuple-element.25.tall_ref, bf16[8192,128]{1,0:T(8,128)(2,1)} %bitcast.5, bf16[8192,128]{1,0:T(8,128)(2,1)} %blk_hbm.1), custom_call_target="tpu_custom_call" | custom-call | tf_op jit(solution)/shard_map/target_rows/pallas_call | solution.py:727
  38.0 85.6 %grad_reduce.1 = (f32[64,128]{1,0:T(8,128)}, f32[8,128]{1,0:T(8,128)}, f32[384,8,128]{2,1,0:T(8,128)}, f32[1024,128]{1,0:T(8,128)}) custom-call(f32[64,128]{1,0:T(8,128)} %get-tuple-element.28.local, f32[64,128]{1,0:T(8,128)} %get-tuple-element.29.zst_ref, bf16[8192,128]{1,0:T(8,128)(2,1)} %bitcast.6, bf16[1024,128]{1,0:T(8,128)(2,1)} %get-tuple-element.30.cand_hbm, ...), custom_call_target="tpu_custom_call" | custom-call | tf_op jit(solution)/shard_map/grad_reduce/pallas_call | solution.py:738
  123.7 10.9 %table_grad.1 = (f32[8192,128]{1,0:T(8,128)}, f32[256,1024]{1,0:T(8,128)}, f32[1024,128]{1,0:T(8,128)}, f32[1,1]{1,0:T(1,128)}) custom-call(s32[64,128]{1,0:T(8,128)} %get-tuple-element.27.code_ref, f32[64,128]{1,0:T(8,128)} %get-tuple-element.36.g_ref, f32[64,128]{1,0:T(8,128)} %get-tuple-element.37.pos_ref, f32[8,128]{1,0:T(8,128)} %get-tuple-element.38.lossrow_ref, ...), custom_call_target="tpu_custom_call" | custom-call | tf_op jit(solution)/shard_map/table_grad/pallas_call | solution.py:755

commit v8 on v7

--- a/solution.py
+++ b/solution.py
@@ -185,18 +185,22 @@
     return jnp.transpose(jnp.broadcast_to(row, (LANE, LANE)))
 
 
-def query_kernel(x_ref, win_ref, wout_ref, tgt_ref, blk_ref, cid_ref, logq_ref, tall_ref, h_out, pre_out, cand_out, candt_out, cidb_out, logqb_out,
-                 blk, ids, lqs, rows, h_ref, pre_ref, cand_ref, candt_ref, cidb_ref, logqb_ref, load_sem, out_sem, send_sem, recv_sem):
+def query_kernel(x_hbm, win_hbm, wout_hbm, tgt_ref, blk_ref, cid_ref, logq_ref, tall_ref, h_out, pre_out, cand_out, candt_out, cidb_out, logqb_out,
+                 x_ref, win_ref, wout_ref, blk, ids, lqs, rows, h_ref, pre_ref, cand_ref, candt_ref, cidb_ref, logqb_ref, load_sem, out_sem, send_sem, recv_sem):
     me = lax.axis_index("dp")
     mine = pl.ds(pl.multiple_of(me * 8, 8), 8)
     loads = [
         pltpu.make_async_copy(cid_ref.at[mine], ids, load_sem.at[0]), pltpu.make_async_copy(logq_ref.at[mine], lqs, load_sem.at[1]),
         pltpu.make_async_copy(blk_ref, blk, load_sem.at[2])]
-    for c in loads:
+    tower = [pltpu.make_async_copy(a, b, load_sem.at[3 + i]) for i, (a, b) in enumerate([(x_hbm, x_ref), (win_hbm, win_ref), (wout_hbm, wout_ref)])]
+    for c in tower + loads:
         c.start()
     barrier = greet(me)
+    for c in tower:
+        c.wait()
     pre = jnp.dot(x_ref[...], win_ref[...], preferred_element_type=F32)
-    pre_ref[...] = pre
+    pre_ref[0] = pre[:, :PART]
+    pre_ref[1] = pre[:, PART:]
     act = gelu_parts(pre)[0].astype(BF16)
     query = jnp.dot(act, wout_ref[...], preferred_element_type=F32)
     core = coord(me, "core")
@@ -431,7 +435,7 @@
     copy.wait()
 
 
-def table_kernel(code_ref, g_ref, pos_ref, lossrow_ref, cid_hbm, dcand_hbm, tiles_hbm, hc_ref, de_ref, dwin_ref, dwout_ref, loss_ref, cidx, dcand, whole, hc, gh, sem):
+def table_kernel(code_ref, g_ref, pos_ref, lossrow_ref, cid_hbm, dcand_hbm, tiles_hbm, hc_ref, de_ref, dwin_out, dwout_out, loss_ref, cidx, dcand, whole, hc, gh, dwin_ref, dwout_ref, sem):
     me = lax.axis_index("dp")
     loads = [pltpu.make_async_copy(cid_hbm.at[pl.ds(pl.multiple_of(me * 8, 8), 8)], cidx, sem.at[3]), pltpu.make_async_copy(dcand_hbm, dcand, sem.at[0]), pltpu.make_async_copy(tiles_hbm, whole, sem.at[1])]
     for c in loads:
@@ -445,6 +449,16 @@
     repeat(de_ref.shape[0] // LANE, clear)
     for c in loads:
         c.wait()
+    for half in range(2):
+        base = 192 * half
+        dwout_ref[PART * half : PART * half + PART, :] = whole[base : base + TOK].reshape(PART, LANE)
+        for j in range(4):
+            at = base + TOK + 32 * j
+            col = PART * half + LANE * j
+            dwin_ref[:, col : col + LANE] = whole[at : at + 32].reshape(WIDE, LANE)
+    outs = [pltpu.make_async_copy(dwin_ref, dwin_out, sem.at[4]), pltpu.make_async_copy(dwout_ref, dwout_out, sem.at[5])]
+    for c in outs:
+        c.start()
 
     base = me * ALL
 
@@ -477,27 +491,17 @@
         return carry
 
     repeat((count + 127) // LANE, chunk)
-    dwout_ref[...] = whole[0:LANE].reshape(KILO, LANE)
-    for j in range(8):
-        dwin_ref[:, LANE * j : LANE * j + LANE] = whole[LANE + 32 * j : 160 + 32 * j].reshape(WIDE, LANE)
+    for c in outs:
+        c.wait()
 
 
 LAST = 27
 PART = 512
 
 
-def core_exchange(me, ref, half, rref, send, recv):
-    mine = coord(me, "core")
-    c = remote(ref.at[pl.ds((1 - mine) * half, half)], rref.at[pl.ds(0, half)], send, recv, peer(me, "core", 1))
-    c.start()
-    c.wait_recv()
-    add_rows(ref, mine * half, rref, 0, half, 1)
-    return [c]
-
-
 def grad_kernel(local, zst_ref, h_hbm, cand_hbm, cidb_hbm, logqb_hbm, candt_hbm, te_hbm, x_hbm, wout_hbm, pre_hbm, g_ref, loss_ref, tiles_out, dcand_out,
                 ebuf, mc_ref, part, total, srecv, cur, norm, acc, recv, tiles, trecv, whole, dcand_ref,
-                h_ref, cand_ref, cidb, logqb, candt_ref, te_ref, x_ref, wout_ref, pre_ref,
+                h_ref, cand_ref, cidb, logqb, candt_ref, te_ref, x_ref, wout_ref, pre_ref, xp_ref, prep_ref, dh_ref, dhp_ref,
                 load_sem, core_send, core_recv, send_sem, recv_sem):
     me = lax.axis_index("dp")
     core = coord(me, "core")
@@ -610,6 +614,11 @@
     stats = Stats(me, srecv, cur, send_sem.at[3], recv_sem.at[3])
     a, b, c = range(3)
 
+    def to_partner(src, dst, n):
+        return remote(src, dst, send_sem.at[n, LAST + 1], recv_sem.at[n, LAST + 1], peer(me, "core", 1))
+
+    give_x, give_pre = to_partner(x_ref, xp_ref, 0), to_partner(pre_ref.at[1 - core], prep_ref, 1)
+
     def keep_part(s):
         part_loop(s, 0, keep)
         scatter.send(s)
@@ -629,6 +638,8 @@
     finish(a)
     for load in loads[4:]:
         load.wait()
+    give_x.start()
+    give_pre.start()
     part_loop(a, 0, give)
     stats.advance(b)
     stats.advance(c)
@@ -640,30 +651,35 @@
     finish(c)
     part_loop(c, 0, give)
     keep_part(c)
+    give_x.wait_recv()
+    give_pre.wait_recv()
     loss_ref[...] = jnp.broadcast_to(jnp.sum(total[...], keepdims=True) / ALL, loss_ref.shape)
     cand_grad()
     scatter.rest()
     sent = stats.sent + scatter.sent
-    rows = []
     for s in range(3):
         idx = block_index(me, ORDERS[s])
         for g in range(H_UNIT[s]):
-            rows.append(acc[core * 512 + H_OFF[s] + idx * H_UNIT[s] + g])
-    dh = jnp.concatenate(rows, axis=0).astype(BF16)
-    act, slope = gelu_parts(pre_ref[...])
-    d_pre = (slope * nt_dot(dh, wout_ref[...])).astype(BF16)
+            dh_ref[H_FIRST[s] + g] = acc[core * 512 + H_OFF[s] + idx * H_UNIT[s] + g].astype(BF16)
+    give_dh = to_partner(dh_ref, dhp_ref, 2)
+    give_dh.start()
+    act, slope = gelu_parts(jnp.concatenate([pre_ref[core], prep_ref[...]], axis=0))
+    give_dh.wait_recv()
+    dh = jnp.concatenate([dh_ref[...].reshape(TOK, LANE), dhp_ref[...].reshape(TOK, LANE)], axis=0)
+    d_pre = (slope * nt_dot(dh, wout_ref[pl.ds(pl.multiple_of(core * PART, PART), PART), :])).astype(BF16)
     dw_out = tn_dot(act.astype(BF16), dh)
-    tiles[0:LANE] = dw_out.reshape(LANE, 8, LANE)
-    dw_in = tn_dot(x_ref[...], d_pre)
-    for j in range(8):
-        tiles[LANE + 32 * j : 160 + 32 * j] = dw_in[:, LANE * j : LANE * j + LANE].reshape(32, 8, LANE)
+    mine = core * 192
+    tiles[pl.ds(mine, TOK)] = dw_out.reshape(TOK, 8, LANE)
+    dw_in = tn_dot(jnp.concatenate([x_ref[...], xp_ref[...]], axis=0), d_pre)
+    for j in range(4):
+        tiles[pl.ds(mine + TOK + 32 * j, 32)] = dw_in[:, LANE * j : LANE * j + LANE].reshape(32, 8, LANE)
     streams = [(TOK * s, 1, ORDERS[s]) for s in range(3)]
-    half = core_exchange(me, tiles, 192, trecv, send_sem.at[1, LAST], recv_sem.at[1, LAST])
-    scatter = Scatter(me, tiles, core * 192, trecv, 192, streams, send_sem.at[1], recv_sem.at[1])
+    sent += [give_x, give_pre, give_dh]
+    scatter = Scatter(me, tiles, core * 192, trecv, 0, streams, send_sem.at[1], recv_sem.at[1])
     for s in range(3):
         scatter.send(s)
     scatter.rest()
-    sent += half + scatter.sent
+    sent += scatter.sent
     streams = []
     for s in range(3):
         own = core * 192 + TOK * s + block_index(me, ORDERS[s])
@@ -709,15 +725,16 @@
         tall, h_all, pre, cand_rows, cand_t, cidb, logqb = pl.pallas_call(
             query_kernel,
             out_shape=[
-                jax.ShapeDtypeStruct((LANE, 1, TOK), jnp.int32), jax.ShapeDtypeStruct((KILO, 8, LANE), BF16), jax.ShapeDtypeStruct((TOK, KILO), F32),
+                jax.ShapeDtypeStruct((LANE, 1, TOK), jnp.int32), jax.ShapeDtypeStruct((KILO, 8, LANE), BF16), jax.ShapeDtypeStruct((2, TOK, PART), F32),
                 jax.ShapeDtypeStruct((cand_dev, LANE), BF16), jax.ShapeDtypeStruct((LANE, cand_dev), BF16),
                 jax.ShapeDtypeStruct((cand_dev, LANE), F32), jax.ShapeDtypeStruct((cand_dev, LANE), F32)],
-            in_specs=vmem(4) + [anyspec] * 3, out_specs=vmem(1) + [anyspec] * 6,
+            in_specs=[anyspec] * 3 + vmem(1) + [anyspec] * 3, out_specs=vmem(1) + [anyspec] * 6,
             scratch_shapes=[
+                pltpu.VMEM(features.shape, BF16), pltpu.VMEM(w_in.shape, BF16), pltpu.VMEM(w_out.shape, BF16),
                 pltpu.VMEM((block_rows, LANE), BF16), pltpu.VMEM((8, LANE), jnp.int32), pltpu.VMEM((8, LANE), F32), pltpu.VMEM((cand_dev, LANE), F32),
-                pltpu.VMEM((KILO, 8, LANE), BF16), pltpu.VMEM((TOK, KILO), F32), pltpu.VMEM((cand_dev, LANE), BF16), pltpu.VMEM((LANE, cand_dev), BF16),
+                pltpu.VMEM((KILO, 8, LANE), BF16), pltpu.VMEM((2, TOK, PART), F32), pltpu.VMEM((cand_dev, LANE), BF16), pltpu.VMEM((LANE, cand_dev), BF16),
                 pltpu.VMEM((cand_dev, LANE), F32), pltpu.VMEM((cand_dev, LANE), F32),
-                dma(3), dma(7), dma(4 * NPEER), dma(4 * NPEER)],
+                dma(6), dma(7), dma(4 * NPEER), dma(4 * NPEER)],
             compiler_params=params(0), name="query_gather",
         )(features, w_in, w_out, targets[None, :], table_blk, cid_rows, logq_rows)
         query_all = h_all.reshape(ALL, LANE)
@@ -749,6 +766,7 @@
                 pltpu.VMEM((tok_total, LANE), BF16), pltpu.VMEM((cand_dev, LANE), BF16), pltpu.VMEM((cand_dev, LANE), F32), pltpu.VMEM((cand_dev, LANE), F32),
                 pltpu.VMEM((LANE, cand_dev), BF16), pltpu.VMEM((tok_total, LANE), F32),
                 pltpu.VMEM(features.shape, BF16), pltpu.VMEM(w_out.shape, BF16), pltpu.VMEM(pre.shape, F32),
+                pltpu.VMEM(features.shape, BF16), pltpu.VMEM((TOK, PART), F32), pltpu.VMEM((8, 8, LANE), BF16), pltpu.VMEM((8, 8, LANE), BF16),
                 dma(11), dma(8), dma(8), dma(4, 3 * NPEER), dma(4, 3 * NPEER)],
             compiler_params=params(1), name="grad_reduce",
         )(local, zst, query_all, cand_rows, cidb, logqb, cand_t, te, features, w_out, pre)
@@ -757,8 +775,8 @@
             out_shape=[
                 jax.ShapeDtypeStruct((block_rows, LANE), F32), jax.ShapeDtypeStruct(w_in.shape, F32), jax.ShapeDtypeStruct(w_out.shape, F32),
                 jax.ShapeDtypeStruct((1, 1), F32)],
-            in_specs=[smem] + vmem(3) + [anyspec] * 4, out_specs=vmem(3) + [smem],
-            scratch_shapes=[pltpu.SMEM((8, LANE), jnp.int32), pltpu.VMEM((cand_dev, LANE), F32), pltpu.VMEM((384, 8, LANE), F32), square, square, dma(4)],
+            in_specs=[smem] + vmem(3) + [anyspec] * 4, out_specs=vmem(1) + [anyspec] * 2 + [smem],
+            scratch_shapes=[pltpu.SMEM((8, LANE), jnp.int32), pltpu.VMEM((cand_dev, LANE), F32), pltpu.VMEM((384, 8, LANE), F32), square, square, pltpu.VMEM(w_in.shape, F32), pltpu.VMEM(w_out.shape, F32), dma(6)],
             compiler_params=big, name="table_grad",
         )(codes, grad_tgt, pos, loss_row, cid_rows, dcand, tiles, hc)
         loss = loss.reshape(())

time: 134 us -> 133 us (level); the launches traced: 135 us -> 131 us
  Pallas kernels: 134 us -> 131 us
    pallas_call x1, Pallas kernels: 11.1 us -> 9.51 us  [local_step(): pl.pallas_call(target_kernel, out_shape=[jax.ShapeDtypeStruct((TOK, LANE)...]
where the time goes in v8:
time: 133 us; the launch traced here: 131 us
  Pallas kernels  131 us (98%)
    pallas_call x1, Pallas kernels, local_step(): pl.pallas_call(grad_kernel, out_shape=[jax.ShapeDtypeStruct((TOK, LANE),...  85.3 us
    pallas_call x1, Pallas kernels, local_step(): pl.pallas_call(query_kernel, out_shape=[jax.ShapeDtypeStruct((LANE, 1, TO...  25.9 us
    pallas_call x1, Pallas kernels, local_step(): pl.pallas_call(table_kernel, out_shape=[jax.ShapeDtypeStruct((block_rows,...  9.76 us
    pallas_call x1, Pallas kernels, local_step(): pl.pallas_call(target_kernel, out_shape=[jax.ShapeDtypeStruct((TOK, LANE)...  9.51 us

profile of v8, /device:TPU:1, one launch (start us, length us, event | category | flops | bytes accessed | tf_op | source)
XLA Modules:
  0.0 131.4 jit_solution(11958348298712183196)
XLA Ops:
  0.6 25.9 %query_gather.1 = (s32[128,1,64]{2,1,0:T(1,128)}, bf16[1024,8,128]{2,1,0:T(8,128)(2,1)}, f32[2,64,512]{2,1,0:T(8,128)}, bf16[1024,128]{1,0:T(8,128)(2,1)}, bf16[...) custom-call(bf16[64,256]{1,0:T(8,128)(2,1)} %x_hbm.3, bf16[256,1024]{1,0:T(8,128)(2,1)} %win_hbm.1, ...), custom_call_target="tpu_custom_call" | custom-call | tf_op jit(solution)/shard_map/query_gather/pallas_call | solution.py:725
  26.6 9.5 %target_rows.1 = (f32[64,128]{1,0:T(8,128)}, f32[64,128]{1,0:T(8,128)}, s32[64,128]{1,0:T(8,128)}, f32[64,128]{1,0:T(8,128)}, f32[8192,128]{1,0:T(8,128)}, /*index=5*/f32[8192,128]{1,0:T(8,128)}) custom-call(s32[128,1,64]{2,1,0:T(1,128)} %get-tuple-element.25.tall_ref, bf16[8192,128]{1,0:T(8,128)(2,1)} %bitcast.5, bf16[8192,128]{1,0:T(8,128)(2,1)} %blk_hbm.1), custom_call_target="tpu_custom_call" | custom-call | tf_op jit(solution)/shard_map/target_rows/pallas_call | solution.py:744
  36.1 85.3 %grad_reduce.1 = (f32[64,128]{1,0:T(8,128)}, f32[8,128]{1,0:T(8,128)}, f32[384,8,128]{2,1,0:T(8,128)}, f32[1024,128]{1,0:T(8,128)}) custom-call(f32[64,128]{1,0:T(8,128)} %get-tuple-element.28.local, f32[64,128]{1,0:T(8,128)} %get-tuple-element.29.zst_ref, bf16[8192,128]{1,0:T(8,128)(2,1)} %bitcast.6, bf16[1024,128]{1,0:T(8,128)(2,1)} %get-tuple-element.30.cand_hbm, ...), custom_call_target="tpu_custom_call" | custom-call | tf_op jit(solution)/shard_map/grad_reduce/pallas_call | solution.py:755
  121.4 9.8 %table_grad.1 = (f32[8192,128]{1,0:T(8,128)}, f32[256,1024]{1,0:T(8,128)}, f32[1024,128]{1,0:T(8,128)}, f32[1,1]{1,0:T(1,128)}) custom-call(s32[64,128]{1,0:T(8,128)} %get-tuple-element.27.code_ref, f32[64,128]{1,0:T(8,128)} %get-tuple-element.36.g_ref, f32[64,128]{1,0:T(8,128)} %get-tuple-element.37.pos_ref, f32[8,128]{1,0:T(8,128)} %get-tuple-element.38.lossrow_ref, ...), custom_call_target="tpu_custom_call" | custom-call | tf_op jit(solution)/shard_map/table_grad/pallas_call | solution.py:773

commit v9 on v8

--- a/solution.py
+++ b/solution.py
@@ -13,6 +13,7 @@
 NDEV = 128
 NPEER = 10
 LANE, TOK, ALL, KILO, WIDE = 128, 64, 8192, 1024, 256
+HALF, SUB = 192, 32
 
 
 def one(i):
@@ -74,7 +75,7 @@
     return pltpu.make_async_remote_copy(src_ref=src, dst_ref=dst, send_sem=send, recv_sem=recv, device_id=(dev,), device_id_type=MESH)
 
 
-def gather_streams(me, streams, bulk, send_sem, recv_sem, between=None):
+def gather_streams(me, streams, bulk, send_sem, recv_sem, between=None, early=None):
     pending, sent = [None] * len(streams), []
     for phase in range(4):
         for s, (ref, off, unit, order) in enumerate(streams):
@@ -82,6 +83,8 @@
                 for c in pending[s]:
                     c.wait_recv()
             if phase == 3:
+                if early and s == 0:
+                    early()
                 continue
             span = 4 ** phase
             idx = block_index(me, order)
@@ -176,7 +179,7 @@
     return lax.dot_general(a, b, (((0,), (0,)), ((), ())), preferred_element_type=F32)
 
 
-H_OFF = (0, 192, 384)
+H_OFF = (0, HALF, 384)
 H_UNIT = (3, 3, 2)
 H_FIRST = (0, 3, 6)
 
@@ -185,8 +188,8 @@
     return jnp.transpose(jnp.broadcast_to(row, (LANE, LANE)))
 
 
-def query_kernel(x_hbm, win_hbm, wout_hbm, tgt_ref, blk_ref, cid_ref, logq_ref, tall_ref, h_out, pre_out, cand_out, candt_out, cidb_out, logqb_out,
-                 x_ref, win_ref, wout_ref, blk, ids, lqs, rows, h_ref, pre_ref, cand_ref, candt_ref, cidb_ref, logqb_ref, load_sem, out_sem, send_sem, recv_sem):
+def query_kernel(x_hbm, win_hbm, wout_hbm, tgt_ref, blk_ref, cid_ref, logq_ref, tok_ref, h_out, pre_out, cand_out, candt_out, cidb_out, logqb_out,
+                 tall_ref, square, x_ref, win_ref, wout_ref, blk, ids, lqs, rows, h_ref, pre_ref, cand_ref, candt_ref, cidb_ref, logqb_ref, load_sem, out_sem, send_sem, recv_sem):
     me = lax.axis_index("dp")
     mine = pl.ds(pl.multiple_of(me * 8, 8), 8)
     loads = [
@@ -204,7 +207,7 @@
     act = gelu_parts(pre)[0].astype(BF16)
     query = jnp.dot(act, wout_ref[...], preferred_element_type=F32)
     core = coord(me, "core")
-    streams = []
+    streams = [(tall_ref, core * TOK, 1, ORDERS[2])]
     for s in range(3):
         idx = block_index(me, ORDERS[s])
         for g in range(H_UNIT[s]):
@@ -212,7 +215,6 @@
             h_ref[core * 512 + H_OFF[s] + idx * H_UNIT[s] + g] = query[row : row + 8, :].astype(BF16)
         streams.append((h_ref, core * 512 + H_OFF[s], H_UNIT[s], ORDERS[s]))
     tall_ref[core * TOK + block_index(me, ORDERS[2])] = tgt_ref[...]
-    streams.append((tall_ref, core * TOK, 1, ORDERS[2]))
     lane = iota((1, LANE), 1)
     pl.semaphore_wait(barrier, NPEER)
 
@@ -233,7 +235,7 @@
                 cidb_ref[at, :] = column((ids[c : c + 1, :] - me * ALL).astype(F32))
                 logqb_ref[at, :] = column(lqs[c : c + 1, :])
             rows[...] = jnp.zeros_like(rows)
-        bounds = (0, 8, 17, 32, 32)
+        bounds = (0, 8, 17, SUB, SUB)
         lax.fori_loop(bounds[phase], bounds[phase + 1], pick, 0)
         if phase == 2:
             cand_ref[...] = rows[...].astype(BF16)
@@ -251,7 +253,15 @@
         where = pl.ds(c * 512, 512)
         return pltpu.make_async_copy(h_ref.at[where], h_out.at[where], out_sem.at[5 + c])
 
-    sent = gather_streams(me, streams, [(h_ref, 512), (tall_ref, TOK)], send_sem, recv_sem, fill)
+    where = tall_ref.at[pl.ds(core * TOK, TOK)]
+    swap = remote(where, where, send_sem.at[39], recv_sem.at[39], peer(me, "core", 1))
+
+    def early():
+        swap.start()
+        swap.wait_recv()
+        arrange(tall_ref, square, tok_ref)
+
+    sent = gather_streams(me, streams, [(h_ref, 512)], send_sem, recv_sem, fill, early) + [swap]
     half(1 - core).start()
     for c in outs:
         c.wait()
@@ -340,16 +350,15 @@
         for a in range(LANE // per):
             half, rest = divmod(a, TOK // per)
             for r in range(rows):
-                at = 32 * half + H_OFF[s] // 16 + rest * rows + r
+                at = SUB * half + H_OFF[s] // 16 + rest * rows + r
                 tok_ref[at : at + 1, :] = full[a : a + 1, LANE * r : LANE * r + LANE]
 
 
-def target_kernel(tall_ref, h_hbm, blk_hbm, zst_ref, pos_ref, code_ref, local_ref, hc_ref, te_out, h_ref, blk_ref, te_ref, zd, hs, es, square, tgt_ref, codes, load_sem, sem):
+def target_kernel(tgt_ref, h_hbm, blk_hbm, zst_ref, pos_ref, code_ref, local_ref, hc_ref, te_out, h_ref, blk_ref, te_ref, zd, hs, es, codes, load_sem, sem):
     block_rows = blk_ref.shape[0]
     loads = [pltpu.make_async_copy(h_hbm, h_ref, load_sem.at[0]), pltpu.make_async_copy(blk_hbm, blk_ref, load_sem.at[1])]
     for c in loads:
         c.start()
-    arrange(tall_ref, square, tgt_ref)
     rel = tgt_ref[...] - lax.axis_index("dp") * block_rows
     local_ref[...] = rel.astype(F32)
     own = (rel >= 0) & (rel < block_rows)
@@ -447,27 +456,27 @@
         return carry
 
     repeat(de_ref.shape[0] // LANE, clear)
-    for c in loads:
+    for c in loads[:2]:
         c.wait()
+    base = me * ALL
+
+    def place(i, carry):
+        for u in range(SUB):
+            de_ref[one(cidx[lax.shift_right_logical(i, 2), (i & 3) * SUB + u] - base), :] = dcand[one(i * SUB + u), :]
+        return carry
+
+    repeat(SUB, place)
+    loads[-1].wait()
     for half in range(2):
-        base = 192 * half
+        base = HALF * half
         dwout_ref[PART * half : PART * half + PART, :] = whole[base : base + TOK].reshape(PART, LANE)
         for j in range(4):
-            at = base + TOK + 32 * j
+            at = base + TOK + SUB * j
             col = PART * half + LANE * j
-            dwin_ref[:, col : col + LANE] = whole[at : at + 32].reshape(WIDE, LANE)
+            dwin_ref[:, col : col + LANE] = whole[at : at + SUB].reshape(WIDE, LANE)
     outs = [pltpu.make_async_copy(dwin_ref, dwin_out, sem.at[4]), pltpu.make_async_copy(dwout_ref, dwout_out, sem.at[5])]
     for c in outs:
         c.start()
-
-    base = me * ALL
-
-    def place(i, carry):
-        for u in range(32):
-            de_ref[one(cidx[lax.shift_right_logical(i, 2), (i & 3) * 32 + u] - base), :] = dcand[one(i * 32 + u), :]
-        return carry
-
-    repeat(32, place)
     count = jnp.sum(flag(pos_ref[...] >= 0.0)).astype(jnp.int32)
     slot0 = iota((LANE, LANE), 0).astype(F32)
 
@@ -514,7 +523,7 @@
     barrier = greet(me)
     for g in range(8):
         for half in range(2):
-            cur[g, 2, 4 * half : 4 * half + 4, :] = zst_ref[32 * half + 4 * g : 32 * half + 4 * g + 4, :]
+            cur[g, 2, 4 * half : 4 * half + 4, :] = zst_ref[SUB * half + 4 * g : SUB * half + 4 * g + 4, :]
     for c in loads[:4]:
         c.wait()
 
@@ -552,13 +561,13 @@
         stats.receive(s)
 
         def norms(g, carry):
-            m, t, z = cur[32 + g, 0], cur[32 + g, 1], cur[32 + g, 2]
+            m, t, z = cur[SUB + g, 0], cur[SUB + g, 1], cur[SUB + g, 2]
             top = jnp.maximum(m, z)
             log_norm = top + jnp.log(t * jnp.exp(m - top) + jnp.exp(z - top))
             grad = (jnp.exp(z - log_norm) - 1.0) / ALL
             total[...] += log_norm - z
             for half in range(2):
-                rows = pl.ds(32 * half + 4 * g, 4)
+                rows = pl.ds(SUB * half + 4 * g, 4)
                 norm[rows, :] = log_norm[4 * half : 4 * half + 4, :]
                 g_ref[rows, :] = grad[4 * half : 4 * half + 4, :]
             return carry
@@ -668,26 +677,33 @@
     dh = jnp.concatenate([dh_ref[...].reshape(TOK, LANE), dhp_ref[...].reshape(TOK, LANE)], axis=0)
     d_pre = (slope * nt_dot(dh, wout_ref[pl.ds(pl.multiple_of(core * PART, PART), PART), :])).astype(BF16)
     dw_out = tn_dot(act.astype(BF16), dh)
-    mine = core * 192
+    mine = core * HALF
     tiles[pl.ds(mine, TOK)] = dw_out.reshape(TOK, 8, LANE)
     dw_in = tn_dot(jnp.concatenate([x_ref[...], xp_ref[...]], axis=0), d_pre)
     for j in range(4):
-        tiles[pl.ds(mine + TOK + 32 * j, 32)] = dw_in[:, LANE * j : LANE * j + LANE].reshape(32, 8, LANE)
+        tiles[pl.ds(mine + TOK + SUB * j, SUB)] = dw_in[:, LANE * j : LANE * j + LANE].reshape(SUB, 8, LANE)
     streams = [(TOK * s, 1, ORDERS[s]) for s in range(3)]
     sent += [give_x, give_pre, give_dh]
-    scatter = Scatter(me, tiles, core * 192, trecv, 0, streams, send_sem.at[1], recv_sem.at[1])
+    scatter = Scatter(me, tiles, core * HALF, trecv, 0, streams, send_sem.at[1], recv_sem.at[1])
     for s in range(3):
         scatter.send(s)
     scatter.rest()
     sent += scatter.sent
     streams = []
     for s in range(3):
-        own = core * 192 + TOK * s + block_index(me, ORDERS[s])
+        own = core * HALF + TOK * s + block_index(me, ORDERS[s])
         whole[own] = tiles[own]
-        streams.append((whole, core * 192 + TOK * s, 1, ORDERS[s]))
-    sent += gather_streams(me, streams, [(whole, 192)], send_sem.at[2], recv_sem.at[2])
-    tiles_copy = pltpu.make_async_copy(whole, tiles_out, load_sem.at[10])
-    tiles_copy.start()
+        streams.append((whole, core * HALF + TOK * s, 1, ORDERS[s]))
+    def leave(c):
+        where = pl.ds(c * HALF, HALF)
+        return pltpu.make_async_copy(whole.at[where], tiles_out.at[where], load_sem.at[10 + c])
+
+    def push(phase):
+        if phase == 3:
+            leave(core).start()
+
+    sent += gather_streams(me, streams, [(whole, HALF)], send_sem.at[2], recv_sem.at[2], push)
+    leave(1 - core).start()
     dcand_copy.wait()
     for c in sent:
         c.wait_send()
@@ -697,7 +713,8 @@
         return carry
 
     repeat(8, swap_done)
-    tiles_copy.wait()
+    leave(core).wait()
+    leave(1 - core).wait()
 
 
 def vmem(n):
@@ -722,14 +739,15 @@
         tok_total = features.shape[0] * num_dev
         anyspec = pl.BlockSpec(memory_space=pl.ANY)
         cid_rows, logq_rows = cand_ids.reshape(KILO, LANE), log_q.reshape(KILO, LANE)
-        tall, h_all, pre, cand_rows, cand_t, cidb, logqb = pl.pallas_call(
+        tgt_all, h_all, pre, cand_rows, cand_t, cidb, logqb = pl.pallas_call(
             query_kernel,
             out_shape=[
-                jax.ShapeDtypeStruct((LANE, 1, TOK), jnp.int32), jax.ShapeDtypeStruct((KILO, 8, LANE), BF16), jax.ShapeDtypeStruct((2, TOK, PART), F32),
+                jax.ShapeDtypeStruct((TOK, LANE), jnp.int32), jax.ShapeDtypeStruct((KILO, 8, LANE), BF16), jax.ShapeDtypeStruct((2, TOK, PART), F32),
                 jax.ShapeDtypeStruct((cand_dev, LANE), BF16), jax.ShapeDtypeStruct((LANE, cand_dev), BF16),
                 jax.ShapeDtypeStruct((cand_dev, LANE), F32), jax.ShapeDtypeStruct((cand_dev, LANE), F32)],
             in_specs=[anyspec] * 3 + vmem(1) + [anyspec] * 3, out_specs=vmem(1) + [anyspec] * 6,
             scratch_shapes=[
+                pltpu.VMEM((LANE, 1, TOK), jnp.int32), pltpu.VMEM((LANE, TOK), jnp.int32),
                 pltpu.VMEM(features.shape, BF16), pltpu.VMEM(w_in.shape, BF16), pltpu.VMEM(w_out.shape, BF16),
                 pltpu.VMEM((block_rows, LANE), BF16), pltpu.VMEM((8, LANE), jnp.int32), pltpu.VMEM((8, LANE), F32), pltpu.VMEM((cand_dev, LANE), F32),
                 pltpu.VMEM((KILO, 8, LANE), BF16), pltpu.VMEM((2, TOK, PART), F32), pltpu.VMEM((cand_dev, LANE), BF16), pltpu.VMEM((LANE, cand_dev), BF16),
@@ -749,9 +767,9 @@
             in_specs=vmem(1) + [anyspec] * 2, out_specs=vmem(4) + [anyspec] * 2,
             scratch_shapes=[
                 pltpu.VMEM((tok_total, LANE), BF16), pltpu.VMEM((block_rows, LANE), BF16), pltpu.VMEM((tok_total + 8, LANE), F32), pltpu.VMEM((TOK, LANE), F32),
-                square, square, pltpu.VMEM((LANE, TOK), jnp.int32), pltpu.VMEM((TOK, LANE), jnp.int32), pltpu.SMEM((TOK, LANE), jnp.int32), dma(4), pltpu.SemaphoreType.DMA],
+                square, square, pltpu.SMEM((TOK, LANE), jnp.int32), dma(4), pltpu.SemaphoreType.DMA],
             compiler_params=big, name="target_rows",
-        )(tall, query_all, table_blk)
+        )(tgt_all, query_all, table_blk)
         grad_tgt, loss_row, tiles, dcand = pl.pallas_call(
             grad_kernel,
             out_shape=[
@@ -767,7 +785,7 @@
                 pltpu.VMEM((LANE, cand_dev), BF16), pltpu.VMEM((tok_total, LANE), F32),
                 pltpu.VMEM(features.shape, BF16), pltpu.VMEM(w_out.shape, BF16), pltpu.VMEM(pre.shape, F32),
                 pltpu.VMEM(features.shape, BF16), pltpu.VMEM((TOK, PART), F32), pltpu.VMEM((8, 8, LANE), BF16), pltpu.VMEM((8, 8, LANE), BF16),
-                dma(11), dma(8), dma(8), dma(4, 3 * NPEER), dma(4, 3 * NPEER)],
+                dma(12), dma(8), dma(8), dma(4, 3 * NPEER), dma(4, 3 * NPEER)],
             compiler_params=params(1), name="grad_reduce",
         )(local, zst, query_all, cand_rows, cidb, logqb, cand_t, te, features, w_out, pre)
         grad_blk, grad_w_in, grad_w_out, loss = pl.pallas_call(

time: 133 us -> 131 us (0.985)
  Pallas kernels: 131 us -> 129 us
    pallas_call x1, Pallas kernels: 9.51 us -> 7.9 us  [local_step(): pl.pallas_call(target_kernel, out_shape=[jax.ShapeDtypeStruct((TOK, LANE)...]
where the time goes in v9:
time: 131 us; the launch traced here: 130 us
  Pallas kernels  129 us (98%)
    pallas_call x1, Pallas kernels, local_step(): pl.pallas_call(grad_kernel, out_shape=[jax.ShapeDtypeStruct((TOK, LANE),...  85.2 us
    pallas_call x1, Pallas kernels, local_step(): pl.pallas_call(query_kernel, out_shape=[jax.ShapeDtypeStruct((TOK, LANE),...  26.9 us
    pallas_call x1, Pallas kernels, local_step(): pl.pallas_call(table_kernel, out_shape=[jax.ShapeDtypeStruct((block_rows,...  9.16 us
    pallas_call x1, Pallas kernels, local_step(): pl.pallas_call(target_kernel, out_shape=[jax.ShapeDtypeStruct((TOK, LANE)...  7.9 us

profile of v9, /device:TPU:1, one launch (start us, length us, event | category | flops | bytes accessed | tf_op | source)
XLA Modules:
  0.0 130.1 jit_solution(2672874211577605250)
XLA Ops:
  0.6 26.9 %query_gather.1 = (s32[64,128]{1,0:T(8,128)}, bf16[1024,8,128]{2,1,0:T(8,128)(2,1)}, f32[2,64,512]{2,1,0:T(8,128)}, bf16[1024,128]{1,0:T(8,128)(2,1)}, bf16[128,...) custom-call(bf16[64,256]{1,0:T(8,128)(2,1)} %x_hbm.3, bf16[256,1024]{1,0:T(8,128)(2,1)} %win_hbm.1, ...), custom_call_target="tpu_custom_call" | custom-call | tf_op jit(solution)/shard_map/query_gather/pallas_call | solution.py:742
  27.6 7.9 %target_rows.1 = (f32[64,128]{1,0:T(8,128)}, f32[64,128]{1,0:T(8,128)}, s32[64,128]{1,0:T(8,128)}, f32[64,128]{1,0:T(8,128)}, f32[8192,128]{1,0:T(8,128)}, /*index=5*/f32[8192,128]{1,0:T(8,128)}) custom-call(s32[64,128]{1,0:T(8,128)} %get-tuple-element.25.tgt_ref, bf16[8192,128]{1,0:T(8,128)(2,1)} %bitcast.5, bf16[8192,128]{1,0:T(8,128)(2,1)} %blk_hbm.1), custom_call_target="tpu_custom_call" | custom-call | tf_op jit(solution)/shard_map/target_rows/pallas_call | solution.py:762
  35.5 85.2 %grad_reduce.1 = (f32[64,128]{1,0:T(8,128)}, f32[8,128]{1,0:T(8,128)}, f32[384,8,128]{2,1,0:T(8,128)}, f32[1024,128]{1,0:T(8,128)}) custom-call(f32[64,128]{1,0:T(8,128)} %get-tuple-element.28.local, f32[64,128]{1,0:T(8,128)} %get-tuple-element.29.zst_ref, bf16[8192,128]{1,0:T(8,128)(2,1)} %bitcast.6, bf16[1024,128]{1,0:T(8,128)(2,1)} %get-tuple-element.30.cand_hbm, ...), custom_call_target="tpu_custom_call" | custom-call | tf_op jit(solution)/shard_map/grad_reduce/pallas_call | solution.py:773
  120.7 9.2 %table_grad.1 = (f32[8192,128]{1,0:T(8,128)}, f32[256,1024]{1,0:T(8,128)}, f32[1024,128]{1,0:T(8,128)}, f32[1,1]{1,0:T(1,128)}) custom-call(s32[64,128]{1,0:T(8,128)} %get-tuple-element.27.code_ref, f32[64,128]{1,0:T(8,128)} %get-tuple-element.36.g_ref, f32[64,128]{1,0:T(8,128)} %get-tuple-element.37.pos_ref, f32[8,128]{1,0:T(8,128)} %get-tuple-element.38.lossrow_ref, ...), custom_call_target="tpu_custom_call" | custom-call | tf_op jit(solution)/shard_map/table_grad/pallas_call | solution.py:791

commit v10 on v9

--- a/solution.py
+++ b/solution.py
@@ -83,7 +83,7 @@
                 for c in pending[s]:
                     c.wait_recv()
             if phase == 3:
-                if early and s == 0:
+                if early and s == 3:
                     early()
                 continue
             span = 4 ** phase
@@ -207,13 +207,14 @@
     act = gelu_parts(pre)[0].astype(BF16)
     query = jnp.dot(act, wout_ref[...], preferred_element_type=F32)
     core = coord(me, "core")
-    streams = [(tall_ref, core * TOK, 1, ORDERS[2])]
+    streams = []
     for s in range(3):
         idx = block_index(me, ORDERS[s])
         for g in range(H_UNIT[s]):
             row = 8 * (H_FIRST[s] + g)
             h_ref[core * 512 + H_OFF[s] + idx * H_UNIT[s] + g] = query[row : row + 8, :].astype(BF16)
         streams.append((h_ref, core * 512 + H_OFF[s], H_UNIT[s], ORDERS[s]))
+    streams.append((tall_ref, core * TOK, 1, ORDERS[2]))
     tall_ref[core * TOK + block_index(me, ORDERS[2])] = tgt_ref[...]
     lane = iota((1, LANE), 1)
     pl.semaphore_wait(barrier, NPEER)
@@ -244,6 +245,8 @@
                 c.start()
         if phase == 3:
             half(core).start()
+            swap.wait_recv()
+            arrange(tall_ref, square, tok_ref)
 
     outs = [
         pltpu.make_async_copy(a, b, out_sem.at[i]) for i, (a, b) in enumerate([
@@ -256,12 +259,7 @@
     where = tall_ref.at[pl.ds(core * TOK, TOK)]
     swap = remote(where, where, send_sem.at[39], recv_sem.at[39], peer(me, "core", 1))
 
-    def early():
-        swap.start()
-        swap.wait_recv()
-        arrange(tall_ref, square, tok_ref)
-
-    sent = gather_streams(me, streams, [(h_ref, 512)], send_sem, recv_sem, fill, early) + [swap]
+    sent = gather_streams(me, streams, [(h_ref, 512)], send_sem, recv_sem, fill, swap.start) + [swap]
     half(1 - core).start()
     for c in outs:
         c.wait()

time: 131 us -> 129 us (0.985)
  no operation moved by 1% of the time
where the time goes in v10:
time: 129 us
  Pallas kernels  128 us (99%)
    pallas_call x1, Pallas kernels, local_step(): pl.pallas_call(grad_kernel, out_shape=[jax.ShapeDtypeStruct((TOK, LANE),...  84.8 us
    pallas_call x1, Pallas kernels, local_step(): pl.pallas_call(query_kernel, out_shape=[jax.ShapeDtypeStruct((TOK, LANE),...  25.9 us
    pallas_call x1, Pallas kernels, local_step(): pl.pallas_call(table_kernel, out_shape=[jax.ShapeDtypeStruct((block_rows,...  9.17 us
    pallas_call x1, Pallas kernels, local_step(): pl.pallas_call(target_kernel, out_shape=[jax.ShapeDtypeStruct((TOK, LANE)...  7.9 us

profile of v10, /device:TPU:1, one launch (start us, length us, event | category | flops | bytes accessed | tf_op | source)
XLA Modules:
  0.0 128.6 jit_solution(10810417578347675527)
XLA Ops:
  0.6 25.9 %query_gather.1 = (s32[64,128]{1,0:T(8,128)}, bf16[1024,8,128]{2,1,0:T(8,128)(2,1)}, f32[2,64,512]{2,1,0:T(8,128)}, bf16[1024,128]{1,0:T(8,128)(2,1)}, bf16[128,...) custom-call(bf16[64,256]{1,0:T(8,128)(2,1)} %x_hbm.3, bf16[256,1024]{1,0:T(8,128)(2,1)} %win_hbm.1, ...), custom_call_target="tpu_custom_call" | custom-call | tf_op jit(solution)/shard_map/query_gather/pallas_call | solution.py:740
  26.6 7.9 %target_rows.1 = (f32[64,128]{1,0:T(8,128)}, f32[64,128]{1,0:T(8,128)}, s32[64,128]{1,0:T(8,128)}, f32[64,128]{1,0:T(8,128)}, f32[8192,128]{1,0:T(8,128)}, /*index=5*/f32[8192,128]{1,0:T(8,128)}) custom-call(s32[64,128]{1,0:T(8,128)} %get-tuple-element.25.tgt_ref, bf16[8192,128]{1,0:T(8,128)(2,1)} %bitcast.5, bf16[8192,128]{1,0:T(8,128)(2,1)} %blk_hbm.1), custom_call_target="tpu_custom_call" | custom-call | tf_op jit(solution)/shard_map/target_rows/pallas_call | solution.py:760
  34.5 84.8 %grad_reduce.1 = (f32[64,128]{1,0:T(8,128)}, f32[8,128]{1,0:T(8,128)}, f32[384,8,128]{2,1,0:T(8,128)}, f32[1024,128]{1,0:T(8,128)}) custom-call(f32[64,128]{1,0:T(8,128)} %get-tuple-element.28.local, f32[64,128]{1,0:T(8,128)} %get-tuple-element.29.zst_ref, bf16[8192,128]{1,0:T(8,128)(2,1)} %bitcast.6, bf16[1024,128]{1,0:T(8,128)(2,1)} %get-tuple-element.30.cand_hbm, ...), custom_call_target="tpu_custom_call" | custom-call | tf_op jit(solution)/shard_map/grad_reduce/pallas_call | solution.py:771
  119.2 9.2 %table_grad.1 = (f32[8192,128]{1,0:T(8,128)}, f32[256,1024]{1,0:T(8,128)}, f32[1024,128]{1,0:T(8,128)}, f32[1,1]{1,0:T(1,128)}) custom-call(s32[64,128]{1,0:T(8,128)} %get-tuple-element.27.code_ref, f32[64,128]{1,0:T(8,128)} %get-tuple-element.36.g_ref, f32[64,128]{1,0:T(8,128)} %get-tuple-element.37.pos_ref, f32[8,128]{1,0:T(8,128)} %get-tuple-element.38.lossrow_ref, ...), custom_call_target="tpu_custom_call" | custom-call | tf_op jit(solution)/shard_map/table_grad/pallas_call | solution.py:789

commit v11 on v10

--- a/solution.py
+++ b/solution.py
@@ -516,7 +516,7 @@
         pltpu.make_async_copy(a, b, load_sem.at[i]) for i, (a, b) in enumerate([
             (cand_hbm, cand_ref), (cidb_hbm, cidb), (logqb_hbm, logqb), (h_hbm, h_ref),
             (candt_hbm, candt_ref), (te_hbm, te_ref), (x_hbm, x_ref), (wout_hbm, wout_ref), (pre_hbm, pre_ref)])]
-    for c in loads:
+    for c in loads[:4]:
         c.start()
     barrier = greet(me)
     for g in range(8):
@@ -524,6 +524,8 @@
             cur[g, 2, 4 * half : 4 * half + 4, :] = zst_ref[SUB * half + 4 * g : SUB * half + 4 * g + 4, :]
     for c in loads[:4]:
         c.wait()
+    for c in loads[4:]:
+        c.start()
 
     def score(t, carry):
         for j in range(2):

time: 129 us -> 130 us (level)
  Pallas kernels: 128 us -> 130 us
    pallas_call x1, Pallas kernels: 7.9 us -> 9.44 us  [local_step(): pl.pallas_call(target_kernel, out_shape=[jax.ShapeDtypeStruct((TOK, LANE)...]
where the time goes in v11:
time: 130 us; the launch traced here: 131 us
  Pallas kernels  130 us (100%)
    pallas_call x1, Pallas kernels, local_step(): pl.pallas_call(grad_kernel, out_shape=[jax.ShapeDtypeStruct((TOK, LANE),...  84.4 us
    pallas_call x1, Pallas kernels, local_step(): pl.pallas_call(query_kernel, out_shape=[jax.ShapeDtypeStruct((TOK, LANE),...  25.9 us
    pallas_call x1, Pallas kernels, local_step(): pl.pallas_call(table_kernel, out_shape=[jax.ShapeDtypeStruct((block_rows,...  10.1 us
    pallas_call x1, Pallas kernels, local_step(): pl.pallas_call(target_kernel, out_shape=[jax.ShapeDtypeStruct((TOK, LANE)...  9.44 us

profile of v11, /device:TPU:1, one launch (start us, length us, event | category | flops | bytes accessed | tf_op | source)
XLA Modules:
  0.0 130.6 jit_solution(9365569536025761980)
XLA Ops:
  0.6 25.9 %query_gather.1 = (s32[64,128]{1,0:T(8,128)}, bf16[1024,8,128]{2,1,0:T(8,128)(2,1)}, f32[2,64,512]{2,1,0:T(8,128)}, bf16[1024,128]{1,0:T(8,128)(2,1)}, bf16[128,...) custom-call(bf16[64,256]{1,0:T(8,128)(2,1)} %x_hbm.3, bf16[256,1024]{1,0:T(8,128)(2,1)} %win_hbm.1, ...), custom_call_target="tpu_custom_call" | custom-call | tf_op jit(solution)/shard_map/query_gather/pallas_call | solution.py:742
  26.6 9.4 %target_rows.1 = (f32[64,128]{1,0:T(8,128)}, f32[64,128]{1,0:T(8,128)}, s32[64,128]{1,0:T(8,128)}, f32[64,128]{1,0:T(8,128)}, f32[8192,128]{1,0:T(8,128)}, /*index=5*/f32[8192,128]{1,0:T(8,128)}) custom-call(s32[64,128]{1,0:T(8,128)} %get-tuple-element.25.tgt_ref, bf16[8192,128]{1,0:T(8,128)(2,1)} %bitcast.5, bf16[8192,128]{1,0:T(8,128)(2,1)} %blk_hbm.1), custom_call_target="tpu_custom_call" | custom-call | tf_op jit(solution)/shard_map/target_rows/pallas_call | solution.py:762
  36.0 84.4 %grad_reduce.1 = (f32[64,128]{1,0:T(8,128)}, f32[8,128]{1,0:T(8,128)}, f32[384,8,128]{2,1,0:T(8,128)}, f32[1024,128]{1,0:T(8,128)}) custom-call(f32[64,128]{1,0:T(8,128)} %get-tuple-element.28.local, f32[64,128]{1,0:T(8,128)} %get-tuple-element.29.zst_ref, bf16[8192,128]{1,0:T(8,128)(2,1)} %bitcast.6, bf16[1024,128]{1,0:T(8,128)(2,1)} %get-tuple-element.30.cand_hbm, ...), custom_call_target="tpu_custom_call" | custom-call | tf_op jit(solution)/shard_map/grad_reduce/pallas_call | solution.py:773
  120.4 10.1 %table_grad.1 = (f32[8192,128]{1,0:T(8,128)}, f32[256,1024]{1,0:T(8,128)}, f32[1024,128]{1,0:T(8,128)}, f32[1,1]{1,0:T(1,128)}) custom-call(s32[64,128]{1,0:T(8,128)} %get-tuple-element.27.code_ref, f32[64,128]{1,0:T(8,128)} %get-tuple-element.36.g_ref, f32[64,128]{1,0:T(8,128)} %get-tuple-element.37.pos_ref, f32[8,128]{1,0:T(8,128)} %get-tuple-element.38.lossrow_ref, ...), custom_call_target="tpu_custom_call" | custom-call | tf_op jit(solution)/shard_map/table_grad/pallas_call | solution.py:791
